TPU v7x, 1024 devices: a whole 8x8x8 slice. The times are simulated.
1024 devices in a mesh: seq: 32 (over z, x_hi, core), head: 32 (over x_lo, y).
Axes of the slice: x: 8 (x_hi: 2, x_lo: 4; x = x_hi * 4 + x_lo), y: 8, z: 8, core: 2. Of those that a mesh axis runs over, the one named last changes fastest.
Arguments:
- queries: bfloat16 [4096, 128, 576], P('seq', 'head'), may hold values from -24 to 24
- latent_kv: bfloat16 [4096, 576], P('seq'), may hold values from -4.5 to 4.5
- grad_out: bfloat16 [4096, 128, 512], P('seq', 'head'), may hold values from -6 to 6
- doc_start: int32 [4096], P('seq'), may hold values from 0 to 4095, as said below
Outputs:
- grad_queries: bfloat16 [4096, 128, 576], P('seq', 'head')
- grad_latent: float32 [4096, 576], P('seq')
Inputs may be any that keep to these rules, and one draw needn't show every extreme that they name: doc_start[p] is the first position of the document holding position p: it never falls along the sequence, doc_start[p] <= p, doc_start[0] = 0, every document holds at most 385 positions, and one document holds exactly 385.
All inputs are finite; a program needn't handle non-finite values.
Results may differ from a plain program's by a relative error of at most 0.0048.
Values may be sent and summed in bfloat16 or wider, within the bound.
No kernel may reach another device: no remote copies, remote signals or barrier semaphores. Data moves between devices by JAX's collectives and lax.ppermute only.
A program may use at most 32 MiB of HBM per device.

v0:
```python
from functools import partial

import jax
import jax.numpy as jnp
from jax import lax
from jax.sharding import PartitionSpec as P

LAT = 512
REACH = 4


softmax_scale = 192.0 ** (-0.5)
lowest = -1e30
contract_last = (((1,), (1,)), ((), ()))
contract_first = (((0,), (0,)), ((), ()))


def passed_along(block, axis, distance):
    devices = range(lax.axis_size(axis))
    route = [(i - distance, i) for i in devices if i - distance in devices]
    return lax.ppermute(block, axis, route)


def cut_along(value, dim, length):
    before, after = (value.shape[:dim], value.shape[dim + 1 :])
    return jnp.moveaxis(value.reshape(*before, length, -1, *after), dim, 0)


def sum_at_owner(value, axis, dim):
    blocks = cut_along(value, dim, lax.axis_size(axis))
    arrived = lax.all_to_all(blocks, axis, split_axis=0, concat_axis=0, tiled=True)
    return arrived.sum(axis=0)


def copy_for_each(value, axis):
    length = lax.axis_size(axis)
    return lax.all_to_all(
        jnp.broadcast_to(value[None], (length, *value.shape)), axis, 0, 0, tiled=True
    )


def laid_out(blocks, dim):
    blocks = jnp.moveaxis(blocks, 0, dim)
    shape = blocks.shape
    return blocks.reshape(*shape[:dim], shape[dim] * shape[dim + 1], *shape[dim + 2 :])


def gather_directly(value, axis, dim):
    blocks = copy_for_each(value, axis)
    return laid_out(blocks, dim)


def product_tiles(query_rows, grad_rows, kv_block, unused):
    scores = (
        lax.dot_general(query_rows, kv_block, contract_last, preferred_element_type=jnp.float32)
        * softmax_scale
    )
    grad_probs = lax.dot_general(
        grad_rows, kv_block[:, :LAT], contract_last, preferred_element_type=jnp.float32
    )
    return (scores, grad_probs)


def empty_tiles(query_count, key_count, unused):
    blank = jnp.zeros((query_count, key_count), jnp.float32)
    return (blank, blank)


def grads_update(
    query_rows, grad_rows, kv_block, scores, grad_probs, visible, log_total, row_delta, unused
):
    weights = jnp.where(visible, jnp.exp(scores - log_total[:, None]), 0.0)
    grad_bf = (weights * (grad_probs - row_delta[:, None])).astype(jnp.bfloat16)
    prob_bf = weights.astype(jnp.bfloat16)
    query_part = jnp.dot(grad_bf, kv_block, preferred_element_type=jnp.float32)
    from_scores = (
        lax.dot_general(grad_bf, query_rows, contract_first, preferred_element_type=jnp.float32)
        * softmax_scale
    )
    from_values = lax.dot_general(
        prob_bf, grad_rows, contract_first, preferred_element_type=jnp.float32
    )
    term = jnp.concatenate([from_scores[:, :LAT] + from_values, from_scores[:, LAT:]], axis=1)
    return (query_part, term)


def no_grads(query_count, tokens, row_width, unused):
    return (
        jnp.zeros((query_count, row_width), jnp.float32),
        jnp.zeros((tokens, row_width), jnp.float32),
    )


def per_device(queries, latent_kv, grad_out, doc_start):
    tokens, head_local, row_width = queries.shape
    query_count = tokens * head_local
    first_pos = lax.axis_index("seq") * tokens
    query_rows = queries.reshape(query_count, row_width)
    grad_rows = grad_out.reshape(query_count, LAT)
    row_pos = jnp.repeat(first_pos + jnp.arange(tokens, dtype=jnp.int32), head_local)
    row_first = jnp.repeat(doc_start, head_local)
    low_first = jnp.min(doc_start)
    windows = [latent_kv]
    for distance in range(1, REACH):
        windows.append(passed_along(latent_kv, "seq", distance))
    key_starts = [first_pos - distance * tokens for distance in range(REACH)]
    wanted = [start + tokens > low_first for start in key_starts]
    blank = jnp.zeros((query_count,), jnp.float32)
    row_top = jnp.full((query_count,), lowest, jnp.float32)
    total_exp = blank
    weighted = blank
    kept = []
    for distance in range(REACH):
        scores, grad_probs = lax.cond(
            wanted[distance],
            partial(product_tiles, query_rows, grad_rows, windows[distance]),
            partial(empty_tiles, query_count, tokens),
            0,
        )
        key_pos = key_starts[distance] + jnp.arange(tokens, dtype=jnp.int32)
        visible = (key_pos[None, :] <= row_pos[:, None]) & (key_pos[None, :] >= row_first[:, None])
        new_top = jnp.maximum(row_top, jnp.max(jnp.where(visible, scores, lowest), axis=1))
        rescale = jnp.exp(row_top - new_top)
        weights = jnp.where(visible, jnp.exp(scores - new_top[:, None]), 0.0)
        total_exp = total_exp * rescale + jnp.sum(weights, axis=1)
        weighted = weighted * rescale + jnp.sum(weights * grad_probs, axis=1)
        row_top = new_top
        kept.append((scores, grad_probs, visible))
    log_total = row_top + jnp.log(total_exp)
    row_delta = weighted / total_exp
    query_grad = jnp.zeros((query_count, row_width), jnp.float32)
    terms = []
    for distance in range(REACH):
        scores, grad_probs, visible = kept[distance]
        compute = partial(
            grads_update,
            query_rows,
            grad_rows,
            windows[distance],
            scores,
            grad_probs,
            visible,
            log_total,
            row_delta,
        )
        query_part, term = lax.cond(
            wanted[distance], compute, partial(no_grads, query_count, tokens, row_width), 0
        )
        query_grad = query_grad + query_part
        terms.append(term)
    stacked = jnp.stack(terms).reshape(REACH, tokens * row_width)
    shares = sum_at_owner(stacked, "head", 1)
    own_share = shares[0]
    for distance in range(1, REACH):
        own_share = own_share + passed_along(shares[distance], "seq", -distance)
    grad_latent = gather_directly(own_share, "head", 0).reshape(tokens, row_width)
    grad_queries = (
        (softmax_scale * query_grad).astype(jnp.bfloat16).reshape(tokens, head_local, row_width)
    )
    return (grad_queries, grad_latent)


def solution(mesh):
    in_specs = (P("seq", "head", None), P("seq", None), P("seq", "head", None), P("seq"))
    out_specs = (P("seq", "head", None), P("seq", None))
    return jax.shard_map(
        per_device, mesh=mesh, in_specs=in_specs, out_specs=out_specs, check_vma=False
    )
```

profile of v0, /device:TPU:128, one launch (start us, length us, event | category | flops | bytes accessed | tf_op | source)
XLA Modules:
  0.0 138.9 jit_solution(15844171518664496401)
XLA Ops:
  0.6 1.1 copy.43
  1.8 6.8 %collective-permute-start.2 = (bf16[128,576]{1,0:T(8,128)(2,1)S(1)}, bf16[128,576]{1,0:T(8,128)(2,1)S(1)}, u32[]{:S(2)}, u32[]{:S(2)}) collective-permute-start(bf16[128,576]{1,0:T(8,128)(2,1)S(1)} %copy.43), channel_id=1, source_target_pairs={{0,96},{32,128},{64,160},{96,192},{128,224},{160,256},{192,288},{2... | collective-permute-start | bytes 442376 | tf_op jit(solution)/shard_map/ppermute | solution.py:21
  8.6 5.1 %collective-permute-start.1 = (bf16[128,576]{1,0:T(8,128)(2,1)S(1)}, bf16[128,576]{1,0:T(8,128)(2,1)}, u32[]{:S(2)}, u32[]{:S(2)}) collective-permute-start(bf16[128,576]{1,0:T(8,128)(2,1)S(1)} %copy.43), channel_id=1, source_target_pairs={{0,64},{32,96},{64,128},{96,160},{128,192},{160,224},{192,256},{22... | collective-permute-start | bytes 442376 | tf_op jit(solution)/shard_map/ppermute | solution.py:21
  13.7 2.4 %collective-permute-start = (bf16[128,576]{1,0:T(8,128)(2,1)S(1)}, bf16[128,576]{1,0:T(8,128)(2,1)}, u32[]{:S(2)}, u32[]{:S(2)}) collective-permute-start(bf16[128,576]{1,0:T(8,128)(2,1)S(1)} %copy.43), channel_id=1, source_target_pairs={{0,32},{32,64},{64,96},{96,128},{128,160},{160,192},{192,224},{224... | collective-permute-start | bytes 442376 | tf_op jit(solution)/shard_map/ppermute | solution.py:21
  16.1 1.3 reduce_min.9
  20.2 0.7 broadcast_in_dim.64
  21.1 1.2 reshape.87
  22.3 0.8 copy.41
  23.4 0.8 conditional.8
  24.6 1.0 compare_and_fusion.2
  25.5 2.5 %conditional.9 = (f32[512,128]{1,0:T(8,128)S(1)}, f32[512,128]{1,0:T(8,128)S(1)}) conditional(s32[]{:T(128)} %convert_element_type.44, () %tuple.83, (bf16[512,576]{1,0:T(8,128)(2,1)S(1)}, bf16[128,576]{1,0:T(8,128)(2,1)}, bf16[512,512]{1,0:T(8,128)(2,1)S(1)}) %tuple.84), branch_computations={%region_4.5_spmd, %region_5.6_spmd} | conditional | flops 142671872 | bytes 1916944 | solution.py:114
  25.5 1.3 convolution_multiply_fusion.1
  26.8 1.2 fusion.2
  28.1 0.7 copy-done.8
  28.9 0.6 multiply_reduce_fusion.3
  29.6 0.9 multiply_reduce_fusion.2
  30.4 0.6 add_divide_fusion
  31.0 0.6 log_add_fusion
  31.6 5.0 %conditional.13 = (f32[512,576]{0,1:T(8,128)S(1)}, f32[1,32,2304]{2,0,1:T(1,128)}) conditional(s32[]{:T(128)} %convert_element_type.44, () %tuple.90, (f32[512]{0:T(512)}, f32[512,128]{1,0:T(8,128)S(1)}, pred[512,128]{1,0:T(32,128)(4,1)S(1)}, f32[512]{0:T(512)}, f32[512,128]{1,0:T(8,128)S(1)}, /*index=5*/bf16[128,576]{1,0:T(8,128)(2,1)}, ...), branch_computations={%region_23.24_spmd, %region_24.25_spmd} | conditional | flops 218841088 | bytes 7460936 | solution.py:146
  31.6 0.9 multiply_convert_fusion.1
  32.9 1.1 convolution_add_fusion.1
  34.3 1.1 stack.25
  35.3 1.3 fusion.36
  36.6 1.0 conditional.14
  36.6 0.9 stack.18.clone
  37.7 1.0 copy-done
  38.8 1.0 conditional.15
  38.8 0.9 stack.20.clone
  39.9 1.0 copy-done.1
  40.9 5.3 %conditional.12 = (f32[512,576]{0,1:T(8,128)}, f32[1,32,2304]{2,0,1:T(1,128)}) conditional(s32[]{:T(128)} %convert_element_type.43, () %tuple.80, (f32[512]{0:T(512)}, f32[512,128]{1,0:T(8,128)S(1)}, pred[512,128]{1,0:T(32,128)(4,1)}, f32[512]{0:T(512)}, f32[512,128]{1,0:T(8,128)S(1)}, /*index=5*/bf16[128,576]{0,1:T(8,128)(2,1)S(1)}, ...), branch_computations={%region_21.22_spmd, %region_22.23_spmd} | conditional | flops 218841088 | bytes 6674476 | solution.py:146
  40.9 1.1 multiply_convert_fusion
  42.4 1.1 convolution_add_fusion
  43.7 1.1 stack.24
  44.8 1.3 fusion.35
  46.1 2.3 %maximum_bitcast_fusion = f32[32,4,2304]{2,1,0:T(4,128)S(1)} fusion(f32[1,32,2304]{2,0,1:T(1,128)} %get-tuple-element.210, f32[1,32,2304]{2,0,1:T(1,128)} %get-tuple-element.209, f32[1,32,2304]{2,0,1:T(1,128)} %get-tuple-element.208, f32[1,32,2304]{2,0,1:T(1,128)} %get-tuple-element.207), kind=kLoop, calls=%fused_computation.48 | loop fusion | flops 884736 | bytes 2359296 | tf_op jit(solution)/shard_map/transpose | solution.py:26
  48.5 41.2 %all_to_all.11 = f32[32,4,2304]{2,1,0:T(4,128)S(1)} all-to-all(f32[32,4,2304]{2,1,0:T(4,128)S(1)} %maximum_bitcast_fusion), channel_id=1, replica_groups=mesh['seq'=32,'head'=32] {'head'}, dimensions={0} | all-to-all | bytes 2359296 | tf_op jit(solution)/shard_map/all_to_all | solution.py:31
  89.9 18.0 %collective-permute-start.3 = (f32[2304]{0:T(1024)S(1)}, f32[2304]{0:T(1024)S(1)}, u32[]{:S(2)}, u32[]{:S(2)}) collective-permute-start(f32[2304]{0:T(1024)S(1)} %get-tuple-element.219), channel_id=1, source_target_pairs={{32,0},{64,32},{96,64},{128,96},{160,128},{192,160},{224,192},{256... | collective-permute-start | bytes 27656 | tf_op jit(solution)/shard_map/ppermute | solution.py:21
  107.9 1.9 %collective-permute-start.5 = (f32[2304]{0:T(1024)S(1)}, f32[2304]{0:T(1024)S(1)}, u32[]{:S(2)}, u32[]{:S(2)}) collective-permute-start(f32[2304]{0:T(1024)S(1)} %get-tuple-element.220), channel_id=1, source_target_pairs={{96,0},{128,32},{160,64},{192,96},{224,128},{256,160},{288,192},{3... | collective-permute-start | bytes 27656 | tf_op jit(solution)/shard_map/ppermute | solution.py:21
  109.9 1.9 %collective-permute-start.4 = (f32[2304]{0:T(1024)S(1)}, f32[2304]{0:T(1024)S(1)}, u32[]{:S(2)}, u32[]{:S(2)}) collective-permute-start(f32[2304]{0:T(1024)S(1)} %get-tuple-element.221), channel_id=1, source_target_pairs={{64,0},{96,32},{128,64},{160,96},{192,128},{224,160},{256,192},{28... | collective-permute-start | bytes 27656 | tf_op jit(solution)/shard_map/ppermute | solution.py:21
  111.8 5.1 %collective-permute-done.5 = f32[2304]{0:T(1024)S(1)} collective-permute-done((f32[2304]{0:T(1024)S(1)}, f32[2304]{0:T(1024)S(1)}, u32[]{:S(2)}, u32[]{:S(2)}) %collective-permute-start.5) | collective-permute-done | bytes 9248 | tf_op jit(solution)/shard_map/ppermute | solution.py:21
  116.9 2.5 %collective-permute-done.4 = f32[2304]{0:T(1024)S(1)} collective-permute-done((f32[2304]{0:T(1024)S(1)}, f32[2304]{0:T(1024)S(1)}, u32[]{:S(2)}, u32[]{:S(2)}) %collective-permute-start.4) | collective-permute-done | bytes 9248 | tf_op jit(solution)/shard_map/ppermute | solution.py:21
  119.4 0.9 broadcast_in_dim.69
  120.2 4.7 %all-to-all-start.1 = ((f32[32,1,2304]{2,1,0:T(1,128)}), f32[32,1,2304]{2,1,0:T(1,128)S(1)}, u32[]{:S(2)}, u32[]{:S(2)}) async-start(f32[32,1,2304]{2,1,0:T(1,128)} %broadcast_in_dim.69), calls=%async_computation.1 | async-start | bytes 589824 | tf_op jit(solution)/shard_map/all_to_all | solution.py:37
  124.9 2.6 %multiply_convert_fusion.4 = bf16[512,576]{0,1:T(8,128)(2,1)S(1)} fusion(f32[512,576]{0,1:T(8,128)} %copy-done.1, f32[512,576]{0,1:T(8,128)} %copy-done, f32[512,576]{0,1:T(8,128)} %get-tuple-element.162, f32[512,576]{0,1:T(8,128)S(1)} %get-tuple-element.163), kind=kLoop, calls=%fused_computation.49 | loop fusion | flops 1474560 | bytes 5308416 | tf_op jit(solution)/shard_map/convert_element_type | solution.py:158
  128.0 1.3 copy.52
  129.3 7.9 %all-to-all-done.1 = f32[32,1,2304]{2,1,0:T(1,128)S(1)} async-done(((f32[32,1,2304]{2,1,0:T(1,128)}), f32[32,1,2304]{2,1,0:T(1,128)S(1)}, u32[]{:S(2)}, u32[]{:S(2)}) %all-to-all-start.1) | async-done | bytes 294944 | tf_op jit(solution)/shard_map/all_to_all | solution.py:37
  137.1 0.7 reduce.4
  138.0 0.9 copy.53
  (63 shorter events, 4.5 us)
Async XLA Ops:
  0.6 21.6 %copy-start.17 = (bf16[128,4,576]{0,2,1:T(8,128)(2,1)S(1)}, bf16[128,4,576]{0,2,1:T(8,128)(2,1)}, u32[]{:S(2)}) copy-start(bf16[128,4,576]{0,2,1:T(8,128)(2,1)} %param.20) | copy-start | bytes 1769476
  1.8 26.3 %collective-permute-start.2 = (bf16[128,576]{1,0:T(8,128)(2,1)S(1)}, bf16[128,576]{1,0:T(8,128)(2,1)S(1)}, u32[]{:S(2)}, u32[]{:S(2)}) collective-permute-start(bf16[128,576]{1,0:T(8,128)(2,1)S(1)} %copy.43), channel_id=1, source_target_pairs={{0,96},{32,128},{64,160},{96,192},{128,224},{160,256},{192,288},{2... | collective-permute-start | bytes 442376 | tf_op jit(solution)/shard_map/ppermute | solution.py:21
  8.6 19.4 %collective-permute-start.1 = (bf16[128,576]{1,0:T(8,128)(2,1)S(1)}, bf16[128,576]{1,0:T(8,128)(2,1)}, u32[]{:S(2)}, u32[]{:S(2)}) collective-permute-start(bf16[128,576]{1,0:T(8,128)(2,1)S(1)} %copy.43), channel_id=1, source_target_pairs={{0,64},{32,96},{64,128},{96,160},{128,192},{160,224},{192,256},{22... | collective-permute-start | bytes 442376 | tf_op jit(solution)/shard_map/ppermute | solution.py:21
  13.7 11.8 %collective-permute-start = (bf16[128,576]{1,0:T(8,128)(2,1)S(1)}, bf16[128,576]{1,0:T(8,128)(2,1)}, u32[]{:S(2)}, u32[]{:S(2)}) collective-permute-start(bf16[128,576]{1,0:T(8,128)(2,1)S(1)} %copy.43), channel_id=1, source_target_pairs={{0,32},{32,64},{64,96},{96,128},{128,160},{160,192},{192,224},{224... | collective-permute-start | bytes 442376 | tf_op jit(solution)/shard_map/ppermute | solution.py:21
  22.3 1.1 copy-start.5
  24.2 4.6 %copy-start.6 = (f32[512,128]{1,0:T(8,128)}, f32[512,128]{1,0:T(8,128)S(1)}, u32[]{:S(2)}) copy-start(f32[512,128]{1,0:T(8,128)S(1)} %get-tuple-element.158) | copy-start | bytes 786436
  28.1 3.5 %copy-start.2 = (f32[512,128]{1,0:T(8,128)}, f32[512,128]{1,0:T(8,128)S(1)}, u32[]{:S(2)}) copy-start(f32[512,128]{1,0:T(8,128)S(1)} %get-tuple-element.160) | copy-start | bytes 786436
  28.1 0.7 copy-start.8
  28.9 1.6 %copy-start.3 = (f32[512,128]{1,0:T(8,128)}, f32[512,128]{1,0:T(8,128)S(1)}, u32[]{:S(2)}) copy-start(f32[512,128]{1,0:T(8,128)S(1)} %get-tuple-element.161) | copy-start | bytes 786436
  28.9 2.7 %copy-start.21 = (pred[512,128]{1,0:T(32,128)(4,1)S(1)}, pred[512,128]{1,0:T(32,128)(4,1)}, u32[]{:S(2)}) copy-start(pred[512,128]{1,0:T(32,128)(4,1)} %get-tuple-element.235) | copy-start | bytes 196612
  32.5 1.5 %copy-start.11 = (bf16[512,128]{1,0:T(8,128)(2,1)}, bf16[512,128]{1,0:T(8,128)(2,1)S(1)}, u32[]{:S(2)}) copy-start(bf16[512,128]{1,0:T(8,128)(2,1)S(1)} %multiply_convert_fusion.1) | copy-start | bytes 393220 | tf_op jit(solution)/shard_map/cond
  34.1 1.3 copy-start.12
  36.6 1.1 copy-start.4
  37.6 1.0 copy-start
  37.7 1.2 copy-start.7
  39.8 1.1 copy-start.1
  40.9 1.5 %copy-start.18 = (pred[512,128]{1,0:T(32,128)(4,1)S(1)}, pred[512,128]{1,0:T(32,128)(4,1)}, u32[]{:S(2)}) copy-start(pred[512,128]{1,0:T(32,128)(4,1)} %get-tuple-element.104) | copy-start | bytes 196612 | tf_op jit(solution)/shard_map/cond
  89.9 21.8 %collective-permute-start.3 = (f32[2304]{0:T(1024)S(1)}, f32[2304]{0:T(1024)S(1)}, u32[]{:S(2)}, u32[]{:S(2)}) collective-permute-start(f32[2304]{0:T(1024)S(1)} %get-tuple-element.219), channel_id=1, source_target_pairs={{32,0},{64,32},{96,64},{128,96},{160,128},{192,160},{224,192},{256... | collective-permute-start | bytes 27656 | tf_op jit(solution)/shard_map/ppermute | solution.py:21
  107.9 9.0 %collective-permute-start.5 = (f32[2304]{0:T(1024)S(1)}, f32[2304]{0:T(1024)S(1)}, u32[]{:S(2)}, u32[]{:S(2)}) collective-permute-start(f32[2304]{0:T(1024)S(1)} %get-tuple-element.220), channel_id=1, source_target_pairs={{96,0},{128,32},{160,64},{192,96},{224,128},{256,160},{288,192},{3... | collective-permute-start | bytes 27656 | tf_op jit(solution)/shard_map/ppermute | solution.py:21
  109.9 9.5 %collective-permute-start.4 = (f32[2304]{0:T(1024)S(1)}, f32[2304]{0:T(1024)S(1)}, u32[]{:S(2)}, u32[]{:S(2)}) collective-permute-start(f32[2304]{0:T(1024)S(1)} %get-tuple-element.221), channel_id=1, source_target_pairs={{64,0},{96,32},{128,64},{160,96},{192,128},{224,160},{256,192},{28... | collective-permute-start | bytes 27656 | tf_op jit(solution)/shard_map/ppermute | solution.py:21
  120.2 16.9 %all-to-all-start.1 = ((f32[32,1,2304]{2,1,0:T(1,128)}), f32[32,1,2304]{2,1,0:T(1,128)S(1)}, u32[]{:S(2)}, u32[]{:S(2)}) async-start(f32[32,1,2304]{2,1,0:T(1,128)} %broadcast_in_dim.69), calls=%async_computation.1 | async-start | bytes 589824 | tf_op jit(solution)/shard_map/all_to_all | solution.py:37
where the time goes:
time: 140 us; the launch traced here: 139 us
  blocking collectives  41.2 us (29%)
  starting transfers between devices  40.8 us (29%)
  local copies, waits for them, and re-layouts  15.8 us (11%)
  waiting for transfers between devices  15.4 us (11%)
  other arithmetic  13.1 us (9%)
  matrix products  8.7 us (6%)
  between operations  3.59 us (3%)
    all_to_all x1, blocking collectives, sum_at_owner(): lax.all_to_all(blocks, axis, split_axis=0, concat_axis=0, tiled=True)  41.2 us
    ppermute x6, starting transfers between devices, passed_along(): return lax.ppermute(block, axis, route)  36.1 us
    all_to_all x1, waiting for transfers between devices, copy_for_each(): lax.all_to_all(jnp.broadcast_to(value[None], (length, *value.shape)), axi...  7.86 us
    ppermute x6, waiting for transfers between devices, passed_along(): return lax.ppermute(block, axis, route)  7.57 us
    unnamed x26, local copies, waits for them, and re-layouts  7.01 us
    all_to_all x1, starting transfers between devices, copy_for_each(): lax.all_to_all(jnp.broadcast_to(value[None], (length, *value.shape)), axi...  4.7 us
    another operation x4, local copies, waits for them, and re-layouts, per_device(): stacked = jnp.stack(terms).reshape(REACH, tokens * row_width)  3.85 us
  transfers between devices with their start and end apart: 7, of which 3 were waited for; matrix products, arithmetic and copies ran while one was open for 10% of the time, Pallas kernels for 0%

commit v1 on v0

v1 whole, which is shorter than its diff:
```python
from functools import partial

import jax
import jax.numpy as jnp
from jax import lax
from jax.experimental import pallas as pl
from jax.experimental.pallas import tpu as pltpu
from jax.sharding import Mesh
from jax.sharding import PartitionSpec as P

LAT = 512
KVW = 576
TOK = 128
HEADS = 4
ROWS = TOK * HEADS
PART = 72
SEQ = ("z", "xh", "core")
RING = ("xh", "xl")

softmax_scale = 192.0 ** (-0.5)
lowest = -1e30
whole = pl.BlockSpec(memory_space=pltpu.VMEM)
scalars = pl.BlockSpec(memory_space=pltpu.SMEM)


def f32_dot(a, b):
    return jnp.dot(a, b, preferred_element_type=jnp.float32)


def attention_kernel(
    place, doc_ref, q_ref, qt_ref, g_ref, gt_ref, own_ref, px_ref, p2_ref, sw_ref,
    keep_ref, send_ref, ds_ref, kv_ref, bias_ref, p_ref,
):
    seq = place[0]
    core = lax.rem(seq, 2)
    for slot, ref in enumerate((own_ref, px_ref, p2_ref, sw_ref)):
        kv_ref[:, slot * TOK : (slot + 1) * TOK] = ref[...]
    first = jnp.broadcast_to(doc_ref[...].astype(jnp.float32), (TOK, TOK)).T
    row = lax.broadcasted_iota(jnp.int32, (TOK, TOK), 0)
    lane = lax.broadcasted_iota(jnp.int32, (TOK, TOK), 1)
    for slot, back in enumerate((0, 3 - 2 * core, 2, 1 + 2 * core)):
        key = lane + (seq - back) * TOK
        seen = (key <= row + seq * TOK) & (key.astype(jnp.float32) >= first)
        bias_ref[:, slot * TOK : (slot + 1) * TOK] = jnp.where(seen, 0.0, lowest)
    for head in range(HEADS):
        rows = slice(head * TOK, (head + 1) * TOK)
        scores = f32_dot(q_ref[rows, :], kv_ref[...]) * softmax_scale + bias_ref[...]
        grad_probs = f32_dot(g_ref[rows, :], kv_ref[:LAT, :])
        top = jnp.max(scores, axis=1, keepdims=True)
        exps = jnp.exp(scores - top)
        inverse = 1.0 / jnp.sum(exps, axis=1, keepdims=True)
        delta = jnp.sum(exps * grad_probs, axis=1, keepdims=True) * inverse
        probs = exps * inverse
        p_ref[rows, :] = probs.astype(jnp.bfloat16)
        ds_ref[rows, :] = (probs * (grad_probs - delta)).astype(jnp.bfloat16)
    for part in range(KVW // PART):
        cols = slice(part * PART, (part + 1) * PART)
        term = f32_dot(qt_ref[cols, :], ds_ref[...]) * softmax_scale
        term = term + f32_dot(gt_ref[cols, :], p_ref[...])
        keep_ref[0, part] = term[:, 0 * TOK : 1 * TOK]
        send_ref[0, part] = term[:, 1 * TOK : 2 * TOK].astype(jnp.bfloat16)
        keep_ref[1, part] = term[:, 2 * TOK : 3 * TOK]
        send_ref[1, part] = term[:, 3 * TOK : 4 * TOK].astype(jnp.bfloat16)


def attention(place, doc, q, qt, g, gt, own, px, p2, sw):
    parts = KVW // PART
    return pl.pallas_call(
        attention_kernel,
        out_shape=(
            jax.ShapeDtypeStruct((2, parts, PART, TOK), jnp.float32),
            jax.ShapeDtypeStruct((2, parts, PART, TOK), jnp.bfloat16),
            jax.ShapeDtypeStruct((ROWS, 4 * TOK), jnp.bfloat16),
        ),
        in_specs=[scalars] + [whole] * 9,
        out_specs=(whole, whole, whole),
        scratch_shapes=[
            pltpu.VMEM((KVW, 4 * TOK), jnp.bfloat16),
            pltpu.VMEM((TOK, 4 * TOK), jnp.float32),
            pltpu.VMEM((ROWS, 4 * TOK), jnp.bfloat16),
        ],
        cost_estimate=pl.CostEstimate(
            flops=4 * 2 * ROWS * 4 * TOK * KVW, bytes_accessed=6 << 20, transcendentals=ROWS * 4 * TOK
        ),
        compiler_params=pltpu.CompilerParams(vmem_limit_bytes=24 << 20),
        name="attention",
    )(place, doc, q, qt, g, gt, own, px, p2, sw)


def queries_kernel(ds_ref, own_ref, px_ref, p2_ref, sw_ref, out_ref, kv_ref):
    for slot, ref in enumerate((own_ref, px_ref, p2_ref, sw_ref)):
        kv_ref[:, slot * TOK : (slot + 1) * TOK] = ref[...]
    for head in range(HEADS):
        rows = slice(head * TOK, (head + 1) * TOK)
        total = lax.dot_general(
            kv_ref[...], ds_ref[rows, :], (((1,), (1,)), ((), ())), preferred_element_type=jnp.float32
        )
        out_ref[head] = (total * softmax_scale).astype(jnp.bfloat16)


def query_grads(ds, own, px, p2, sw):
    return pl.pallas_call(
        queries_kernel,
        out_shape=jax.ShapeDtypeStruct((HEADS, KVW, TOK), jnp.bfloat16),
        in_specs=[whole] * 5,
        out_specs=whole,
        scratch_shapes=[pltpu.VMEM((KVW, 4 * TOK), jnp.bfloat16)],
        cost_estimate=pl.CostEstimate(
            flops=2 * ROWS * 4 * TOK * KVW, bytes_accessed=2 << 20, transcendentals=0
        ),
        compiler_params=pltpu.CompilerParams(vmem_limit_bytes=12 << 20),
        name="query_grads",
    )(ds, own, px, p2, sw)


def join_kernel(core_ref, keep_ref, came_ref, out_ref):
    even = core_ref[0] == 0
    for part in range(KVW // PART):
        side = came_ref[0, part].astype(jnp.float32)
        zero = jnp.zeros_like(side)
        out_ref[part, 0] = (keep_ref[0, part] + jnp.where(even, side, zero)).astype(jnp.bfloat16)
        out_ref[part, 1] = (keep_ref[1, part] + came_ref[1, part].astype(jnp.float32)).astype(
            jnp.bfloat16
        )
        out_ref[part, 2] = jnp.where(even, zero, side).astype(jnp.bfloat16)


def join_cores(core, keep, came):
    return pl.pallas_call(
        join_kernel,
        out_shape=jax.ShapeDtypeStruct((KVW // PART, 3, PART, TOK), jnp.bfloat16),
        in_specs=[scalars, whole, whole],
        out_specs=whole,
        cost_estimate=pl.CostEstimate(flops=1 << 20, bytes_accessed=2 << 20, transcendentals=0),
        compiler_params=pltpu.CompilerParams(vmem_limit_bytes=8 << 20),
        name="join_cores",
    )(core, keep, came)


def per_device(queries, latent_kv, grad_out, doc_start):
    tokens, _, width = queries.shape
    count = lax.axis_size(SEQ)
    seq = lax.axis_index(SEQ).astype(jnp.int32)
    core = lax.axis_index("core").astype(jnp.int32)
    half = lax.axis_index("xh")

    own = latent_kv.T
    p2 = lax.ppermute(own, SEQ, [(i, i + 2) for i in range(count - 2)])
    mixed = [(i, i + 1 + 2 * (i % 2)) for i in range(count)]
    px = lax.ppermute(own, SEQ, [(a, b) for a, b in mixed if b < count])
    sw = lax.ppermute(p2, "core", [(0, 1), (1, 0)])

    q = queries.transpose(1, 0, 2).reshape(ROWS, width)
    qt = queries.transpose(2, 1, 0).reshape(width, ROWS)
    g = grad_out.transpose(1, 0, 2).reshape(ROWS, LAT)
    gt = jnp.pad(grad_out.transpose(2, 1, 0).reshape(LAT, ROWS), ((0, width - LAT), (0, 0)))

    keep, send, ds = attention(
        seq.reshape(1), doc_start.reshape(1, tokens), q, qt, g, gt, own, px, p2, sw
    )
    came = lax.ppermute(send, "core", [(0, 1), (1, 0)])
    terms = join_cores(core.reshape(1), keep, came)
    here = lax.all_to_all(terms, "y", 0, 0, tiled=True).astype(jnp.float32).sum(axis=0)

    low = half == 0
    nothing = jnp.zeros_like(here[0])
    cross = jnp.stack([jnp.where(low, here[2], nothing), jnp.where(low, here[1], here[2])])
    planes = lax.axis_size("z")
    below = lax.ppermute(cross, "z", [(i, i - 1) for i in range(1, planes)])
    plane = below + jnp.stack([jnp.where(low, here[0], here[1]), jnp.where(low, nothing, here[0])])
    plane = plane.astype(jnp.bfloat16)
    spread = jnp.broadcast_to(plane[:, None], (2, 4, PART, tokens)).reshape(8, PART, tokens)
    mine = lax.all_to_all(spread, RING, 0, 0, tiled=True).astype(jnp.float32).sum(axis=0)
    mine = mine.astype(jnp.bfloat16)
    grad = lax.all_to_all(
        jnp.broadcast_to(mine[None], (8, PART, tokens)), "y", 0, 0, tiled=True
    )
    grad_latent = grad.astype(jnp.float32).reshape(width, tokens).T

    grad_queries = query_grads(ds, own, px, p2, sw).transpose(2, 0, 1)
    return grad_queries, grad_latent


def solution(mesh):
    fine = Mesh(mesh.devices.reshape(8, 2, 2, 4, 8), ("z", "xh", "core", "xl", "y"))
    head = ("xl", "y")
    in_specs = (P(SEQ, head, None), P(SEQ, None), P(SEQ, head, None), P(SEQ))
    out_specs = (P(SEQ, head, None), P(SEQ, None))
    return jax.shard_map(
        per_device, mesh=fine, in_specs=in_specs, out_specs=out_specs, check_vma=False
    )
```

time: 140 us -> 91.2 us (0.65)
  the two profiles are of different devices: /device:TPU:128 before, /device:TPU:640 now
where the time goes in v1:
time: 91.2 us; the launch traced here: 90.6 us
  waiting for transfers between devices  32.9 us (36%)
  starting transfers between devices  27.1 us (30%)
  blocking collectives  19.3 us (21%)
  Pallas kernels  5.06 us (6%)
  local copies, waits for them, and re-layouts  4.59 us (5%)
    all_to_all x1, blocking collectives, per_device(): lax.all_to_all(spread, RING, 0, 0, tiled=True).astype(jnp.float32)  19.3 us
    all_to_all x1, waiting for transfers between devices, per_device(): lax.all_to_all(terms, 'y', 0, 0, tiled=True).astype(jnp.float32).sum(axis=0)  16.3 us
    all_to_all x1, waiting for transfers between devices, per_device(): lax.all_to_all(jnp.broadcast_to(mine[None], (8, PART, tokens)), 'y', 0, 0...  7.57 us
    all_to_all x1, starting transfers between devices, per_device(): lax.all_to_all(terms, 'y', 0, 0, tiled=True).astype(jnp.float32).sum(axis=0)  7.52 us
    ppermute x1, starting transfers between devices, per_device(): p2 = lax.ppermute(own, SEQ, [(i, i + 2) for i in range(count - 2)])  7.4 us
    ppermute x1, waiting for transfers between devices, per_device(): below = lax.ppermute(cross, 'z', [(i, i - 1) for i in range(1, planes)])  5.11 us
    all_to_all x1, starting transfers between devices, per_device(): lax.all_to_all(jnp.broadcast_to(mine[None], (8, PART, tokens)), 'y', 0, 0...  3.38 us
    ppermute x1, starting transfers between devices, per_device(): sw = lax.ppermute(p2, 'core', [(0, 1), (1, 0)])  2.71 us
  transfers between devices with their start and end apart: 7, of which 6 were waited for; matrix products, arithmetic and copies ran while one was open for 2% of the time, Pallas kernels for 2%

profile of v1, /device:TPU:640, one launch (start us, length us, event | category | flops | bytes accessed | tf_op | source)
XLA Modules:
  0.0 90.6 jit_solution(4167825588850590493)
XLA Ops:
  0.6 7.4 %collective-permute-start.1 = (bf16[576,128]{1,0:T(8,128)(2,1)}, bf16[576,128]{1,0:T(8,128)(2,1)S(1)}, u32[]{:S(2)}, u32[]{:S(2)}) collective-permute-start(bf16[576,128]{1,0:T(8,128)(2,1)} %bitcast.28), channel_id=1, source_target_pairs={{0,64},{32,96},{64,128},{96,160},{128,192},{160,224},{192,256},{22... | collective-permute-start | bytes 442376 | tf_op jit(solution)/shard_map/ppermute | solution.py:148
  8.0 1.9 %collective-permute-start = (bf16[576,128]{1,0:T(8,128)(2,1)}, bf16[576,128]{1,0:T(8,128)(2,1)S(1)}, u32[]{:S(2)}, u32[]{:S(2)}) collective-permute-start(bf16[576,128]{1,0:T(8,128)(2,1)} %bitcast.29), channel_id=1, source_target_pairs={{0,32},{32,128},{64,96},{96,192},{128,160},{160,256},{192,224},{22... | collective-permute-start | bytes 442376 | tf_op jit(solution)/shard_map/ppermute | solution.py:150
  10.0 0.0 copy-start.3
  10.0 1.2 %copy.12 = bf16[4,128,512]{2,1,0:T(8,128)(2,1)S(1)} copy(bf16[4,128,512]{2,0,1:T(4,128)(2,1)} %bitcast.34) | data formatting | bytes 1048576 | tf_op jit(solution)/shard_map/transpose | solution.py:155
  11.2 0.0 copy-done.3
  11.2 0.6 copy.13
  11.8 0.0 copy-start.2
  11.8 0.1 copy.18
  11.9 1.0 %copy-done.2 = bf16[128,4,576]{0,2,1:T(8,128)(2,1)S(1)} copy-done((bf16[128,4,576]{0,2,1:T(8,128)(2,1)S(1)}, bf16[128,4,576]{0,2,1:T(8,128)(2,1)}, u32[]{:S(2)}) %copy-start.2) | copy-done | bytes 589848
  12.8 0.3 copy.10
  13.2 0.0 copy-start
  13.2 1.9 %collective-permute-done.1.p2_ref = bf16[576,128]{1,0:T(8,128)(2,1)S(1)} collective-permute-done((bf16[576,128]{1,0:T(8,128)(2,1)}, bf16[576,128]{1,0:T(8,128)(2,1)S(1)}, u32[]{:S(2)}, u32[]{:S(2)}) %collective-permute-start.1) | collective-permute-done | bytes 147488 | tf_op jit(solution)/shard_map/ppermute | solution.py:148
  15.1 2.7 %collective-permute-start.2 = (bf16[576,128]{1,0:T(8,128)(2,1)S(1)}, bf16[576,128]{1,0:T(8,128)(2,1)S(1)}, u32[]{:S(2)}, u32[]{:S(2)}) collective-permute-start(bf16[576,128]{1,0:T(8,128)(2,1)S(1)} %collective-permute-done.1.p2_ref), channel_id=1, source_target_pairs={{0,32},{32,0},{1,33},{33,1},{2,34},{34,2},{3,35},{35,3},{4,36},{36... | collective-permute-start | bytes 442376 | tf_op jit(solution)/shard_map/ppermute | solution.py:151
  17.8 0.1 copy_bitcast_fusion.qt_ref
  17.9 0.0 collective-permute-done.px_ref
  17.9 0.9 collective-permute-done.2.sw_ref
  18.8 0.0 copy-start.1
  18.8 0.0 copy-done
  18.8 0.7 copy-done.1
  19.4 2.6 %attention.1 = (f32[2,8,72,128]{3,2,1,0:T(8,128)S(1)}, bf16[2,8,72,128]{3,2,1,0:T(8,128)(2,1)S(1)}, bf16[512,512]{1,0:T(8,128)(2,1)S(1)}) custom-call(s32[1]{0:T(128)} %bitcast.place, s32[1,128]{1,0:T(1,128)S(1)} %bitcast.32, bf16[512,576]{1,0:T(8,128)(2,1)S(1)} %bitcast.26, bf16[576,512]{1,0:T(8,128)(2,1)S(1)} %copy_bitcast_fusion.qt_ref, ...), custom_call_target="tpu_custom_call" | custom-call | flops 1207959552 | bytes 6291456 | tf_op jit(solution)/shard_map/attention/pallas_call | solution.py:68
  22.0 2.3 %collective-permute-start.3 = (bf16[2,8,72,128]{3,2,1,0:T(8,128)(2,1)S(1)}, bf16[2,8,72,128]{3,2,1,0:T(8,128)(2,1)S(1)}, u32[]{:S(2)}, u32[]{:S(2)}) collective-permute-start(bf16[2,8,72,128]{3,2,1,0:T(8,128)(2,1)S(1)} %get-tuple-element.7), channel_id=1, source_target_pairs={{0,32},{32,0},{1,33},{33,1},{2,34},{34,2},{3,35},{35,3},{4,36},{36... | collective-permute-start | bytes 884744 | tf_op jit(solution)/shard_map/ppermute | solution.py:161
  24.3 1.2 %collective-permute-done.3.came_ref = bf16[2,8,72,128]{3,2,1,0:T(8,128)(2,1)S(1)} collective-permute-done((bf16[2,8,72,128]{3,2,1,0:T(8,128)(2,1)S(1)}, bf16[2,8,72,128]{3,2,1,0:T(8,128)(2,1)S(1)}, u32[]{:S(2)}, u32[]{:S(2)}) %collective-permute-start.3) | collective-permute-done | bytes 294944 | tf_op jit(solution)/shard_map/ppermute | solution.py:161
  25.5 0.8 join_cores.1
  26.4 7.5 %all-to-all-start = ((bf16[8,3,72,128]{3,2,1,0:T(8,128)(2,1)}), bf16[8,3,72,128]{3,2,1,0:T(8,128)(2,1)S(1)}, u32[]{:S(2)}, u32[]{:S(2)}) async-start(bf16[8,3,72,128]{3,2,1,0:T(8,128)(2,1)} %join_cores.1), calls=%async_computation | async-start | bytes 884736 | tf_op jit(solution)/shard_map/all_to_all | solution.py:163
  33.9 16.3 %all-to-all-done = bf16[8,3,72,128]{3,2,1,0:T(8,128)(2,1)S(1)} async-done(((bf16[8,3,72,128]{3,2,1,0:T(8,128)(2,1)}), bf16[8,3,72,128]{3,2,1,0:T(8,128)(2,1)S(1)}, u32[]{:S(2)}, u32[]{:S(2)}) %all-to-all-start) | async-done | bytes 442400 | tf_op jit(solution)/shard_map/all_to_all | solution.py:163
  50.2 0.1 convert_reduce_fusion
  50.3 1.9 %collective-permute-start.4 = (f32[2,72,128]{2,1,0:T(8,128)S(1)}, f32[2,72,128]{2,1,0:T(8,128)S(1)}, u32[]{:S(2)}, u32[]{:S(2)}) collective-permute-start(f32[2,72,128]{2,1,0:T(8,128)S(1)} %pad_maximum_fusion), channel_id=1, source_target_pairs={{128,0},{256,128},{384,256},{512,384},{640,512},{768,640},{896,768... | collective-permute-start | bytes 221192 | tf_op jit(solution)/shard_map/ppermute | solution.py:169
  52.2 5.1 %collective-permute-done.4 = f32[2,72,128]{2,1,0:T(8,128)S(1)} collective-permute-done((f32[2,72,128]{2,1,0:T(8,128)S(1)}, f32[2,72,128]{2,1,0:T(8,128)S(1)}, u32[]{:S(2)}, u32[]{:S(2)}) %collective-permute-start.4) | collective-permute-done | bytes 73760 | tf_op jit(solution)/shard_map/ppermute | solution.py:169
  57.3 19.3 %all_to_all.15 = bf16[8,72,128]{2,1,0:T(8,128)(2,1)S(1)} all-to-all(bf16[8,72,128]{2,1,0:T(8,128)(2,1)S(1)} %bitcast.39), channel_id=1, replica_groups=mesh['z'=8,'xh'=2,'core'=2,'xl'=4,'y'=8] {'xh','xl'}, dimensions={0} | all-to-all | bytes 294912 | tf_op jit(solution)/shard_map/all_to_all | solution.py:173
  76.7 0.7 broadcast_in_dim.8
  77.3 3.4 %all-to-all-start.2 = ((bf16[8,72,128]{2,1,0:T(8,128)(2,1)}), bf16[8,72,128]{2,1,0:T(8,128)(2,1)S(1)}, u32[]{:S(2)}, u32[]{:S(2)}) async-start(bf16[8,72,128]{2,1,0:T(8,128)(2,1)} %broadcast_in_dim.8), calls=%async_computation.2 | async-start | bytes 294912 | tf_op jit(solution)/shard_map/all_to_all | solution.py:175
  80.7 1.6 %query_grads.1 = bf16[4,576,128]{2,1,0:T(8,128)(2,1)} custom-call(bf16[512,512]{1,0:T(8,128)(2,1)S(1)} %get-tuple-element.5.ds_ref, bf16[576,128]{1,0:T(8,128)(2,1)S(1)} %bitcast.31, bf16[576,128]{1,0:T(8,128)(2,1)S(1)} %collective-permute-done.px_ref, bf16[576,128]{1,0:T(8,128)(2,1)S(1)} %collective-permute-done.1.p2_ref, ...), custom_call_target="tpu_custom_call" | custom-call | flops 301989888 | bytes 2097152 | tf_op jit(solution)/shard_map/query_grads/pallas_call | solution.py:102
  82.3 7.6 %all-to-all-done.2 = bf16[8,72,128]{2,1,0:T(8,128)(2,1)S(1)} async-done(((bf16[8,72,128]{2,1,0:T(8,128)(2,1)}), bf16[8,72,128]{2,1,0:T(8,128)(2,1)S(1)}, u32[]{:S(2)}, u32[]{:S(2)}) %all-to-all-start.2) | async-done | bytes 147488 | tf_op jit(solution)/shard_map/all_to_all | solution.py:175
  89.9 0.7 convert_bitcast_fusion
  (6 shorter events, 0.1 us)
Async XLA Ops:
  0.6 14.4 %collective-permute-start.1 = (bf16[576,128]{1,0:T(8,128)(2,1)}, bf16[576,128]{1,0:T(8,128)(2,1)S(1)}, u32[]{:S(2)}, u32[]{:S(2)}) collective-permute-start(bf16[576,128]{1,0:T(8,128)(2,1)} %bitcast.28), channel_id=1, source_target_pairs={{0,64},{32,96},{64,128},{96,160},{128,192},{160,224},{192,256},{22... | collective-permute-start | bytes 442376 | tf_op jit(solution)/shard_map/ppermute | solution.py:148
  8.0 9.8 %collective-permute-start = (bf16[576,128]{1,0:T(8,128)(2,1)}, bf16[576,128]{1,0:T(8,128)(2,1)S(1)}, u32[]{:S(2)}, u32[]{:S(2)}) collective-permute-start(bf16[576,128]{1,0:T(8,128)(2,1)} %bitcast.29), channel_id=1, source_target_pairs={{0,32},{32,128},{64,96},{96,192},{128,160},{160,256},{192,224},{22... | collective-permute-start | bytes 442376 | tf_op jit(solution)/shard_map/ppermute | solution.py:150
  10.0 1.2 %copy-start.3 = (bf16[128,4,512]{2,1,0:T(4,128)(2,1)S(1)}, bf16[128,4,512]{2,1,0:T(4,128)(2,1)}, u32[]{:S(2)}) copy-start(bf16[128,4,512]{2,1,0:T(4,128)(2,1)} %param.6) | copy-start | bytes 1572868
  11.8 1.1 %copy-start.2 = (bf16[128,4,576]{0,2,1:T(8,128)(2,1)S(1)}, bf16[128,4,576]{0,2,1:T(8,128)(2,1)}, u32[]{:S(2)}) copy-start(bf16[128,4,576]{0,2,1:T(8,128)(2,1)} %param.4) | copy-start | bytes 1769476
  13.2 5.6 %copy-start = (bf16[128,576]{0,1:T(8,128)(2,1)S(1)}, bf16[128,576]{0,1:T(8,128)(2,1)}, u32[]{:S(2)}) copy-start(bf16[128,576]{0,1:T(8,128)(2,1)} %param.5) | copy-start | bytes 442372
  15.1 3.7 %collective-permute-start.2 = (bf16[576,128]{1,0:T(8,128)(2,1)S(1)}, bf16[576,128]{1,0:T(8,128)(2,1)S(1)}, u32[]{:S(2)}, u32[]{:S(2)}) collective-permute-start(bf16[576,128]{1,0:T(8,128)(2,1)S(1)} %collective-permute-done.1.p2_ref), channel_id=1, source_target_pairs={{0,32},{32,0},{1,33},{33,1},{2,34},{34,2},{3,35},{35,3},{4,36},{36... | collective-permute-start | bytes 442376 | tf_op jit(solution)/shard_map/ppermute | solution.py:151
  18.8 0.7 copy-start.1
  22.0 3.5 %collective-permute-start.3 = (bf16[2,8,72,128]{3,2,1,0:T(8,128)(2,1)S(1)}, bf16[2,8,72,128]{3,2,1,0:T(8,128)(2,1)S(1)}, u32[]{:S(2)}, u32[]{:S(2)}) collective-permute-start(bf16[2,8,72,128]{3,2,1,0:T(8,128)(2,1)S(1)} %get-tuple-element.7), channel_id=1, source_target_pairs={{0,32},{32,0},{1,33},{33,1},{2,34},{34,2},{3,35},{35,3},{4,36},{36... | collective-permute-start | bytes 884744 | tf_op jit(solution)/shard_map/ppermute | solution.py:161
  26.4 23.8 %all-to-all-start = ((bf16[8,3,72,128]{3,2,1,0:T(8,128)(2,1)}), bf16[8,3,72,128]{3,2,1,0:T(8,128)(2,1)S(1)}, u32[]{:S(2)}, u32[]{:S(2)}) async-start(bf16[8,3,72,128]{3,2,1,0:T(8,128)(2,1)} %join_cores.1), calls=%async_computation | async-start | bytes 884736 | tf_op jit(solution)/shard_map/all_to_all | solution.py:163
  50.3 7.0 %collective-permute-start.4 = (f32[2,72,128]{2,1,0:T(8,128)S(1)}, f32[2,72,128]{2,1,0:T(8,128)S(1)}, u32[]{:S(2)}, u32[]{:S(2)}) collective-permute-start(f32[2,72,128]{2,1,0:T(8,128)S(1)} %pad_maximum_fusion), channel_id=1, source_target_pairs={{128,0},{256,128},{384,256},{512,384},{640,512},{768,640},{896,768... | collective-permute-start | bytes 221192 | tf_op jit(solution)/shard_map/ppermute | solution.py:169
  77.3 12.6 %all-to-all-start.2 = ((bf16[8,72,128]{2,1,0:T(8,128)(2,1)}), bf16[8,72,128]{2,1,0:T(8,128)(2,1)S(1)}, u32[]{:S(2)}, u32[]{:S(2)}) async-start(bf16[8,72,128]{2,1,0:T(8,128)(2,1)} %broadcast_in_dim.8), calls=%async_computation.2 | async-start | bytes 294912 | tf_op jit(solution)/shard_map/all_to_all | solution.py:175

commit v2 on v1

--- a/solution.py
+++ b/solution.py
@@ -29,13 +29,13 @@
 
 def attention_kernel(
     place, doc_ref, q_ref, qt_ref, g_ref, gt_ref, own_ref, px_ref, p2_ref, sw_ref,
-    keep_ref, send_ref, ds_ref, kv_ref, bias_ref, p_ref,
+    term_ref, ds_ref, kv_ref, bias_ref, p_ref,
 ):
     seq = place[0]
     core = lax.rem(seq, 2)
     for slot, ref in enumerate((own_ref, px_ref, p2_ref, sw_ref)):
         kv_ref[:, slot * TOK : (slot + 1) * TOK] = ref[...]
-    first = jnp.broadcast_to(doc_ref[...].astype(jnp.float32), (TOK, TOK)).T
+    first = jnp.broadcast_to(doc_ref[...], (TOK, TOK)).T
     row = lax.broadcasted_iota(jnp.int32, (TOK, TOK), 0)
     lane = lax.broadcasted_iota(jnp.int32, (TOK, TOK), 1)
     for slot, back in enumerate((0, 3 - 2 * core, 2, 1 + 2 * core)):
@@ -56,24 +56,23 @@
     for part in range(KVW // PART):
         cols = slice(part * PART, (part + 1) * PART)
         term = f32_dot(qt_ref[cols, :], ds_ref[...]) * softmax_scale
-        term = term + f32_dot(gt_ref[cols, :], p_ref[...])
-        keep_ref[0, part] = term[:, 0 * TOK : 1 * TOK]
-        send_ref[0, part] = term[:, 1 * TOK : 2 * TOK].astype(jnp.bfloat16)
-        keep_ref[1, part] = term[:, 2 * TOK : 3 * TOK]
-        send_ref[1, part] = term[:, 3 * TOK : 4 * TOK].astype(jnp.bfloat16)
+        term = (term + f32_dot(gt_ref[cols, :], p_ref[...])).astype(jnp.bfloat16)
+        same, other = core, 1 - core
+        term_ref[same, part, 0] = term[:, 0 * TOK : 1 * TOK]
+        term_ref[other, part, 0] = term[:, 1 * TOK : 2 * TOK]
+        term_ref[same, part, 1] = term[:, 2 * TOK : 3 * TOK]
+        term_ref[other, part, 1] = term[:, 3 * TOK : 4 * TOK]
 
 
 def attention(place, doc, q, qt, g, gt, own, px, p2, sw):
-    parts = KVW // PART
     return pl.pallas_call(
         attention_kernel,
         out_shape=(
-            jax.ShapeDtypeStruct((2, parts, PART, TOK), jnp.float32),
-            jax.ShapeDtypeStruct((2, parts, PART, TOK), jnp.bfloat16),
+            jax.ShapeDtypeStruct((2, KVW // PART, 2, PART, TOK), jnp.bfloat16),
             jax.ShapeDtypeStruct((ROWS, 4 * TOK), jnp.bfloat16),
         ),
         in_specs=[scalars] + [whole] * 9,
-        out_specs=(whole, whole, whole),
+        out_specs=(whole, whole),
         scratch_shapes=[
             pltpu.VMEM((KVW, 4 * TOK), jnp.bfloat16),
             pltpu.VMEM((TOK, 4 * TOK), jnp.float32),
@@ -113,36 +112,47 @@
     )(ds, own, px, p2, sw)
 
 
-def join_kernel(core_ref, keep_ref, came_ref, out_ref):
-    even = core_ref[0] == 0
-    for part in range(KVW // PART):
-        side = came_ref[0, part].astype(jnp.float32)
-        zero = jnp.zeros_like(side)
-        out_ref[part, 0] = (keep_ref[0, part] + jnp.where(even, side, zero)).astype(jnp.bfloat16)
-        out_ref[part, 1] = (keep_ref[1, part] + came_ref[1, part].astype(jnp.float32)).astype(
-            jnp.bfloat16
-        )
-        out_ref[part, 2] = jnp.where(even, zero, side).astype(jnp.bfloat16)
+def combine_kernel(place, came_ref, cross_ref, plane_ref):
+    seq = place[0]
+    even = lax.rem(seq, 2) == 0
+    low = lax.rem(lax.div(seq, 2), 2) == 0
+    parts = KVW // PART
+
+    def summed(core, window):
+        total = came_ref[core * parts, window].astype(jnp.float32)
+        for part in range(1, parts):
+            total = total + came_ref[core * parts + part, window].astype(jnp.float32)
+        return total
+
+    near, far = [summed(0, 0), summed(0, 1)], [summed(1, 0), summed(1, 1)]
+    nothing = jnp.zeros((PART, TOK), jnp.float32)
+    side = jnp.where(even, far[0], near[0])
+    first = jnp.where(even, near[0], far[0]) + jnp.where(even, side, nothing)
+    second = near[1] + far[1]
+    third = jnp.where(even, nothing, side)
+    cross_ref[0] = jnp.where(low, third, nothing)
+    cross_ref[1] = jnp.where(low, second, third)
+    plane_ref[0] = jnp.where(low, first, second)
+    plane_ref[1] = jnp.where(low, nothing, first)
 
 
-def join_cores(core, keep, came):
+def combine(place, came):
+    shape = jax.ShapeDtypeStruct((2, PART, TOK), jnp.float32)
     return pl.pallas_call(
-        join_kernel,
-        out_shape=jax.ShapeDtypeStruct((KVW // PART, 3, PART, TOK), jnp.bfloat16),
-        in_specs=[scalars, whole, whole],
-        out_specs=whole,
-        cost_estimate=pl.CostEstimate(flops=1 << 20, bytes_accessed=2 << 20, transcendentals=0),
+        combine_kernel,
+        out_shape=(shape, shape),
+        in_specs=[scalars, whole],
+        out_specs=(whole, whole),
+        cost_estimate=pl.CostEstimate(flops=1 << 19, bytes_accessed=1 << 20, transcendentals=0),
         compiler_params=pltpu.CompilerParams(vmem_limit_bytes=8 << 20),
-        name="join_cores",
-    )(core, keep, came)
+        name="combine",
+    )(place, came)
 
 
 def per_device(queries, latent_kv, grad_out, doc_start):
     tokens, _, width = queries.shape
     count = lax.axis_size(SEQ)
     seq = lax.axis_index(SEQ).astype(jnp.int32)
-    core = lax.axis_index("core").astype(jnp.int32)
-    half = lax.axis_index("xh")
 
     own = latent_kv.T
     p2 = lax.ppermute(own, SEQ, [(i, i + 2) for i in range(count - 2)])
@@ -155,20 +165,20 @@
     g = grad_out.transpose(1, 0, 2).reshape(ROWS, LAT)
     gt = jnp.pad(grad_out.transpose(2, 1, 0).reshape(LAT, ROWS), ((0, width - LAT), (0, 0)))
 
-    keep, send, ds = attention(
-        seq.reshape(1), doc_start.reshape(1, tokens), q, qt, g, gt, own, px, p2, sw
+    doc = doc_start.astype(jnp.float32).reshape(1, tokens)
+    place = seq.reshape(1)
+    terms, ds = attention(place, doc, q, qt, g, gt, own, px, p2, sw)
+    parts = width // PART
+    came = lax.all_to_all(
+        terms.reshape(2 * parts, 2, PART, tokens), ("core", "y"), 0, 0, tiled=True
     )
-    came = lax.ppermute(send, "core", [(0, 1), (1, 0)])
-    terms = join_cores(core.reshape(1), keep, came)
-    here = lax.all_to_all(terms, "y", 0, 0, tiled=True).astype(jnp.float32).sum(axis=0)
-
-    low = half == 0
-    nothing = jnp.zeros_like(here[0])
-    cross = jnp.stack([jnp.where(low, here[2], nothing), jnp.where(low, here[1], here[2])])
+    cross, here = combine(place, came)
+    ds, cross = lax.optimization_barrier((ds, cross))
     planes = lax.axis_size("z")
     below = lax.ppermute(cross, "z", [(i, i - 1) for i in range(1, planes)])
-    plane = below + jnp.stack([jnp.where(low, here[0], here[1]), jnp.where(low, nothing, here[0])])
-    plane = plane.astype(jnp.bfloat16)
+    plane = (below + here).astype(jnp.bfloat16)
+    query_grad = query_grads(ds, own, px, p2, sw)
+    plane, query_grad = lax.optimization_barrier((plane, query_grad))
     spread = jnp.broadcast_to(plane[:, None], (2, 4, PART, tokens)).reshape(8, PART, tokens)
     mine = lax.all_to_all(spread, RING, 0, 0, tiled=True).astype(jnp.float32).sum(axis=0)
     mine = mine.astype(jnp.bfloat16)
@@ -176,9 +186,7 @@
         jnp.broadcast_to(mine[None], (8, PART, tokens)), "y", 0, 0, tiled=True
     )
     grad_latent = grad.astype(jnp.float32).reshape(width, tokens).T
-
-    grad_queries = query_grads(ds, own, px, p2, sw).transpose(2, 0, 1)
-    return grad_queries, grad_latent
+    return query_grad.transpose(2, 0, 1), grad_latent
 
 
 def solution(mesh):

time: 91.2 us -> 87.6 us (0.961)
  blocking collectives: 19.3 us -> 58 us
  waiting for transfers between devices: 32.9 us -> 6.12 us
  starting transfers between devices: 27.1 us -> 13.9 us
  local copies, waits for them, and re-layouts: 4.59 us -> 3.28 us
    all_to_all x0 -> x2, blocking collectives: none -> 38.4 us  [the longest x1 26.8 us: per_device(): lax.all_to_all(terms.reshape(2 * parts, 2, PART, tokens), ('core', 'y'),...]
    all_to_all x2 -> x0, waiting for transfers between devices: 23.8 us -> none  [the longest x1 16.3 us: per_device(): lax.all_to_all(terms, 'y', 0, 0, tiled=True).astype(jnp.float32).sum(axis=0)]
    all_to_all x2 -> x0, starting transfers between devices: 10.9 us -> none  [the longest x1 7.52 us: per_device(): lax.all_to_all(terms, 'y', 0, 0, tiled=True).astype(jnp.float32).sum(axis=0)]
    ppermute x1 -> x0, starting transfers between devices: 2.27 us -> none  [per_device(): came = lax.ppermute(send, 'core', [(0, 1), (1, 0)])]
    ppermute x1, waiting for transfers between devices: 5.11 us -> 3.39 us  [per_device(): below = lax.ppermute(cross, 'z', [(i, i - 1) for i in range(1, planes)])]
    ppermute x1 -> x0, waiting for transfers between devices: 1.2 us -> none  [per_device(): came = lax.ppermute(send, 'core', [(0, 1), (1, 0)])]
  transfers between devices with their start and end apart: 7 -> 4, of which waited for: 6 -> 3; matrix products, arithmetic and copies ran while one was open for 2% -> 3% of each run, Pallas kernels for 2% -> 2%
where the time goes in v2:
time: 87.6 us; the launch traced here: 87.2 us
  blocking collectives  58 us (66%)
  starting transfers between devices  13.9 us (16%)
  waiting for transfers between devices  6.12 us (7%)
  Pallas kernels  4.29 us (5%)
  local copies, waits for them, and re-layouts  3.28 us (4%)
    all_to_all x1, blocking collectives, per_device(): lax.all_to_all(terms.reshape(2 * parts, 2, PART, tokens), ('core', 'y'),...  26.8 us
    all_to_all x1, blocking collectives, per_device(): lax.all_to_all(spread, RING, 0, 0, tiled=True).astype(jnp.float32)  19.6 us
    all_to_all x1, blocking collectives, per_device(): lax.all_to_all(jnp.broadcast_to(mine[None], (8, PART, tokens)), 'y', 0, 0...  11.6 us
    ppermute x1, starting transfers between devices, per_device(): p2 = lax.ppermute(own, SEQ, [(i, i + 2) for i in range(count - 2)])  7.4 us
    ppermute x1, waiting for transfers between devices, per_device(): below = lax.ppermute(cross, 'z', [(i, i - 1) for i in range(1, planes)])  3.39 us
    ppermute x1, starting transfers between devices, per_device(): sw = lax.ppermute(p2, 'core', [(0, 1), (1, 0)])  2.67 us
    pallas_call x1, Pallas kernels, attention(): pl.pallas_call(attention_kernel, out_shape=(jax.ShapeDtypeStruct((2, KVW...  2.6 us
    ppermute x1, starting transfers between devices, per_device(): px = lax.ppermute(own, SEQ, [(a, b) for a, b in mixed if b < count])  1.92 us
  transfers between devices with their start and end apart: 4, of which 3 were waited for; matrix products, arithmetic and copies ran while one was open for 3% of the time, Pallas kernels for 2%

profile of v2, /device:TPU:640, one launch (start us, length us, event | category | flops | bytes accessed | tf_op | source)
XLA Modules:
  0.0 87.2 jit_solution(588026562296373467)
XLA Ops:
  0.6 7.4 %collective-permute-start.1 = (bf16[576,128]{1,0:T(8,128)(2,1)}, bf16[576,128]{1,0:T(8,128)(2,1)S(1)}, u32[]{:S(2)}, u32[]{:S(2)}) collective-permute-start(bf16[576,128]{1,0:T(8,128)(2,1)} %bitcast.30), channel_id=1, source_target_pairs={{0,64},{32,96},{64,128},{96,160},{128,192},{160,224},{192,256},{22... | collective-permute-start | bytes 442376 | tf_op jit(solution)/shard_map/ppermute | solution.py:158
  8.0 1.9 %collective-permute-start = (bf16[576,128]{1,0:T(8,128)(2,1)}, bf16[576,128]{1,0:T(8,128)(2,1)S(1)}, u32[]{:S(2)}, u32[]{:S(2)}) collective-permute-start(bf16[576,128]{1,0:T(8,128)(2,1)} %bitcast.31), channel_id=1, source_target_pairs={{0,32},{32,128},{64,96},{96,192},{128,160},{160,256},{192,224},{22... | collective-permute-start | bytes 442376 | tf_op jit(solution)/shard_map/ppermute | solution.py:160
  10.0 0.0 copy-start.2
  10.0 1.2 %copy.12 = bf16[4,128,512]{2,1,0:T(8,128)(2,1)S(1)} copy(bf16[4,128,512]{2,0,1:T(4,128)(2,1)} %bitcast.35) | data formatting | bytes 1048576 | tf_op jit(solution)/shard_map/transpose | solution.py:165
  11.2 0.0 copy-done.2
  11.2 0.6 copy.13
  11.8 0.0 copy-start.1
  11.8 0.1 copy.18
  11.9 1.0 %copy-done.1 = bf16[128,4,576]{0,2,1:T(8,128)(2,1)S(1)} copy-done((bf16[128,4,576]{0,2,1:T(8,128)(2,1)S(1)}, bf16[128,4,576]{0,2,1:T(8,128)(2,1)}, u32[]{:S(2)}) %copy-start.1) | copy-done | bytes 589848
  12.8 0.3 copy.10
  13.2 0.0 copy-start.3
  13.2 0.0 copy-start
  13.2 0.1 copy_bitcast_fusion.qt_ref
  13.3 1.8 %collective-permute-done.1.p2_ref = bf16[576,128]{1,0:T(8,128)(2,1)S(1)} collective-permute-done((bf16[576,128]{1,0:T(8,128)(2,1)}, bf16[576,128]{1,0:T(8,128)(2,1)S(1)}, u32[]{:S(2)}, u32[]{:S(2)}) %collective-permute-start.1) | collective-permute-done | bytes 147488 | tf_op jit(solution)/shard_map/ppermute | solution.py:158
  15.1 2.7 %collective-permute-start.2 = (bf16[576,128]{1,0:T(8,128)(2,1)S(1)}, bf16[576,128]{1,0:T(8,128)(2,1)S(1)}, u32[]{:S(2)}, u32[]{:S(2)}) collective-permute-start(bf16[576,128]{1,0:T(8,128)(2,1)S(1)} %collective-permute-done.1.p2_ref), channel_id=1, source_target_pairs={{0,32},{32,0},{1,33},{33,1},{2,34},{34,2},{3,35},{35,3},{4,36},{36... | collective-permute-start | bytes 442376 | tf_op jit(solution)/shard_map/ppermute | solution.py:161
  17.7 0.0 copy-done.3
  17.8 0.0 collective-permute-done.px_ref
  17.8 1.0 %collective-permute-done.2.sw_ref = bf16[576,128]{1,0:T(8,128)(2,1)S(1)} collective-permute-done((bf16[576,128]{1,0:T(8,128)(2,1)S(1)}, bf16[576,128]{1,0:T(8,128)(2,1)S(1)}, u32[]{:S(2)}, u32[]{:S(2)}) %collective-permute-start.2) | collective-permute-done | bytes 147488 | tf_op jit(solution)/shard_map/ppermute | solution.py:161
  18.7 0.0 copy-done
  18.7 2.6 %attention.1 = (bf16[2,8,2,72,128]{4,3,2,1,0:T(8,128)(2,1)S(1)}, bf16[512,512]{1,0:T(8,128)(2,1)S(1)}) custom-call(s32[1]{0:T(128)} %bitcast.place, f32[1,128]{1,0:T(1,128)S(1)} %convert_bitcast_fusion.1.doc_ref, bf16[512,576]{1,0:T(8,128)(2,1)S(1)} %bitcast.27, bf16[576,512]{1,0:T(8,128)(2,1)S(1)} %copy_bitcast_fusion.qt_ref, ...), custom_call_target="tpu_custom_call" | custom-call | flops 1207959552 | bytes 6291456 | tf_op jit(solution)/shard_map/attention/pallas_call | solution.py:68
  21.3 26.8 %all_to_all.15.came_ref = bf16[16,2,72,128]{3,2,1,0:T(8,128)(2,1)S(1)} all-to-all(bf16[16,2,72,128]{3,2,1,0:T(8,128)(2,1)S(1)} %bitcast.28), channel_id=1, replica_groups=mesh['z'=8,'xh'=2,'core'=2,'xl'=4,'y'=8] {'core','y'}, dimensions={0} | all-to-all | bytes 1179648 | tf_op jit(solution)/shard_map/all_to_all | solution.py:172
  48.1 0.1 combine.1
  48.2 1.9 %collective-permute-start.3 = (f32[2,72,128]{2,1,0:T(8,128)S(1)}, f32[2,72,128]{2,1,0:T(8,128)S(1)}, u32[]{:S(2)}, u32[]{:S(2)}) collective-permute-start(f32[2,72,128]{2,1,0:T(8,128)S(1)} %get-tuple-element.13), channel_id=1, source_target_pairs={{128,0},{256,128},{384,256},{512,384},{640,512},{768,640},{896,768... | collective-permute-start | bytes 221192 | tf_op jit(solution)/shard_map/ppermute | solution.py:178
  50.2 1.6 %query_grads.1 = bf16[4,576,128]{2,1,0:T(8,128)(2,1)} custom-call(bf16[512,512]{1,0:T(8,128)(2,1)S(1)} %get-tuple-element.15.ds_ref, bf16[576,128]{1,0:T(8,128)(2,1)S(1)} %bitcast.33, bf16[576,128]{1,0:T(8,128)(2,1)S(1)} %collective-permute-done.px_ref, bf16[576,128]{1,0:T(8,128)(2,1)S(1)} %collective-permute-done.1.p2_ref, ...), custom_call_target="tpu_custom_call" | custom-call | flops 301989888 | bytes 2097152 | tf_op jit(solution)/shard_map/query_grads/pallas_call | solution.py:101
  51.8 3.4 %collective-permute-done.3 = f32[2,72,128]{2,1,0:T(8,128)S(1)} collective-permute-done((f32[2,72,128]{2,1,0:T(8,128)S(1)}, f32[2,72,128]{2,1,0:T(8,128)S(1)}, u32[]{:S(2)}, u32[]{:S(2)}) %collective-permute-start.3) | collective-permute-done | bytes 73760 | tf_op jit(solution)/shard_map/ppermute | solution.py:178
  55.2 19.6 %all_to_all.16 = bf16[8,72,128]{2,1,0:T(8,128)(2,1)S(1)} all-to-all(bf16[8,72,128]{2,1,0:T(8,128)(2,1)S(1)} %bitcast.40), channel_id=1, replica_groups=mesh['z'=8,'xh'=2,'core'=2,'xl'=4,'y'=8] {'xh','xl'}, dimensions={0} | all-to-all | bytes 294912 | tf_op jit(solution)/shard_map/all_to_all | solution.py:183
  74.8 11.6 %all_to_all.17 = bf16[8,72,128]{2,1,0:T(8,128)(2,1)S(1)} all-to-all(bf16[8,72,128]{2,1,0:T(8,128)(2,1)S(1)} %broadcast_in_dim.5), channel_id=1, replica_groups=mesh['z'=8,'xh'=2,'core'=2,'xl'=4,'y'=8] {'y'}, dimensions={0} | all-to-all | bytes 294912 | tf_op jit(solution)/shard_map/all_to_all | solution.py:185
  86.4 0.7 convert_bitcast_fusion
  (6 shorter events, 0.1 us)
Async XLA Ops:
  0.6 14.4 %collective-permute-start.1 = (bf16[576,128]{1,0:T(8,128)(2,1)}, bf16[576,128]{1,0:T(8,128)(2,1)S(1)}, u32[]{:S(2)}, u32[]{:S(2)}) collective-permute-start(bf16[576,128]{1,0:T(8,128)(2,1)} %bitcast.30), channel_id=1, source_target_pairs={{0,64},{32,96},{64,128},{96,160},{128,192},{160,224},{192,256},{22... | collective-permute-start | bytes 442376 | tf_op jit(solution)/shard_map/ppermute | solution.py:158
  8.0 9.7 %collective-permute-start = (bf16[576,128]{1,0:T(8,128)(2,1)}, bf16[576,128]{1,0:T(8,128)(2,1)S(1)}, u32[]{:S(2)}, u32[]{:S(2)}) collective-permute-start(bf16[576,128]{1,0:T(8,128)(2,1)} %bitcast.31), channel_id=1, source_target_pairs={{0,32},{32,128},{64,96},{96,192},{128,160},{160,256},{192,224},{22... | collective-permute-start | bytes 442376 | tf_op jit(solution)/shard_map/ppermute | solution.py:160
  10.0 1.2 %copy-start.2 = (bf16[128,4,512]{2,1,0:T(4,128)(2,1)S(1)}, bf16[128,4,512]{2,1,0:T(4,128)(2,1)}, u32[]{:S(2)}) copy-start(bf16[128,4,512]{2,1,0:T(4,128)(2,1)} %param.6) | copy-start | bytes 1572868
  11.8 1.1 %copy-start.1 = (bf16[128,4,576]{0,2,1:T(8,128)(2,1)S(1)}, bf16[128,4,576]{0,2,1:T(8,128)(2,1)}, u32[]{:S(2)}) copy-start(bf16[128,4,576]{0,2,1:T(8,128)(2,1)} %param.4) | copy-start | bytes 1769476
  13.2 4.5 %copy-start.3 = (s32[128]{0:T(128)S(1)}, s32[128]{0:T(128)}, u32[]{:S(2)}) copy-start(s32[128]{0:T(128)} %param.7) | copy-start | bytes 1540
  13.2 5.5 %copy-start = (bf16[128,576]{0,1:T(8,128)(2,1)S(1)}, bf16[128,576]{0,1:T(8,128)(2,1)}, u32[]{:S(2)}) copy-start(bf16[128,576]{0,1:T(8,128)(2,1)} %param.5) | copy-start | bytes 442372
  15.1 3.7 %collective-permute-start.2 = (bf16[576,128]{1,0:T(8,128)(2,1)S(1)}, bf16[576,128]{1,0:T(8,128)(2,1)S(1)}, u32[]{:S(2)}, u32[]{:S(2)}) collective-permute-start(bf16[576,128]{1,0:T(8,128)(2,1)S(1)} %collective-permute-done.1.p2_ref), channel_id=1, source_target_pairs={{0,32},{32,0},{1,33},{33,1},{2,34},{34,2},{3,35},{35,3},{4,36},{36... | collective-permute-start | bytes 442376 | tf_op jit(solution)/shard_map/ppermute | solution.py:161
  48.2 6.9 %collective-permute-start.3 = (f32[2,72,128]{2,1,0:T(8,128)S(1)}, f32[2,72,128]{2,1,0:T(8,128)S(1)}, u32[]{:S(2)}, u32[]{:S(2)}) collective-permute-start(f32[2,72,128]{2,1,0:T(8,128)S(1)} %get-tuple-element.13), channel_id=1, source_target_pairs={{128,0},{256,128},{384,256},{512,384},{640,512},{768,640},{896,768... | collective-permute-start | bytes 221192 | tf_op jit(solution)/shard_map/ppermute | solution.py:178

commit v3 on v2

v3 whole, which is shorter than its diff:
```python
import jax
import jax.numpy as jnp
from jax import lax
from jax.experimental import pallas as pl
from jax.experimental.pallas import tpu as pltpu
from jax.sharding import Mesh
from jax.sharding import PartitionSpec as P

LAT = 512
KVW = 576
TOK = 128
HEADS = 4
ROWS = TOK * HEADS
PART = 72
SHARES = 32
SHARE = KVW // SHARES
SEQ = ("z", "xh", "core")
HEAD = ("xl", "y")

softmax_scale = 192.0 ** (-0.5)
lowest = -1e30
whole = pl.BlockSpec(memory_space=pltpu.VMEM)
scalars = pl.BlockSpec(memory_space=pltpu.SMEM)


def f32_dot(a, b):
    return jnp.dot(a, b, preferred_element_type=jnp.float32)


def attention_kernel(
    place, doc_ref, q_ref, qt_ref, g_ref, gt_ref, own_ref, px_ref, p2_ref, sw_ref,
    term_ref, ds_ref, kv_ref, bias_ref, p_ref, mixed_ref,
):
    seq = place[0]
    core = lax.rem(seq, 2)
    for slot, ref in enumerate((own_ref, px_ref, p2_ref, sw_ref)):
        kv_ref[:, slot * TOK : (slot + 1) * TOK] = ref[...]
    first = jnp.broadcast_to(doc_ref[...], (TOK, TOK)).T
    row = lax.broadcasted_iota(jnp.int32, (TOK, TOK), 0)
    lane = lax.broadcasted_iota(jnp.int32, (TOK, TOK), 1)
    for slot, back in enumerate((0, 3 - 2 * core, 2, 1 + 2 * core)):
        key = lane + (seq - back) * TOK
        seen = (key <= row + seq * TOK) & (key.astype(jnp.float32) >= first)
        bias_ref[:, slot * TOK : (slot + 1) * TOK] = jnp.where(seen, 0.0, lowest)
    for head in range(HEADS):
        rows = slice(head * TOK, (head + 1) * TOK)
        scores = f32_dot(q_ref[rows, :], kv_ref[...]) * softmax_scale + bias_ref[...]
        grad_probs = f32_dot(g_ref[rows, :], kv_ref[:LAT, :])
        top = jnp.max(scores, axis=1, keepdims=True)
        exps = jnp.exp(scores - top)
        inverse = 1.0 / jnp.sum(exps, axis=1, keepdims=True)
        delta = jnp.sum(exps * grad_probs, axis=1, keepdims=True) * inverse
        probs = exps * inverse
        p_ref[rows, :] = probs.astype(jnp.bfloat16)
        ds_ref[rows, :] = (probs * (grad_probs - delta)).astype(jnp.bfloat16)
    for part in range(KVW // PART):
        cols = slice(part * PART, (part + 1) * PART)
        term = f32_dot(qt_ref[cols, :], ds_ref[...]) * softmax_scale
        term = term + f32_dot(gt_ref[cols, :], p_ref[...])
        for slot in range(4):
            rows = pl.ds(4 * PART * part + slot, PART, stride=4)
            mixed_ref[rows, :] = term[:, slot * TOK : (slot + 1) * TOK]
    turn = lax.rem(lax.div(seq, 2), 2) * (SHARES // 2)
    for share in range(SHARES):
        rows = slice(4 * SHARE * share, 4 * SHARE * (share + 1))
        term_ref[lax.rem(share + turn, SHARES)] = mixed_ref[rows, :].astype(jnp.bfloat16)


def attention(place, doc, q, qt, g, gt, own, px, p2, sw):
    return pl.pallas_call(
        attention_kernel,
        out_shape=(
            jax.ShapeDtypeStruct((SHARES, 4 * SHARE, TOK), jnp.bfloat16),
            jax.ShapeDtypeStruct((ROWS, 4 * TOK), jnp.bfloat16),
        ),
        in_specs=[scalars] + [whole] * 9,
        out_specs=(whole, whole),
        scratch_shapes=[
            pltpu.VMEM((KVW, 4 * TOK), jnp.bfloat16),
            pltpu.VMEM((TOK, 4 * TOK), jnp.float32),
            pltpu.VMEM((ROWS, 4 * TOK), jnp.bfloat16),
            pltpu.VMEM((4 * KVW, TOK), jnp.float32),
        ],
        cost_estimate=pl.CostEstimate(
            flops=4 * 2 * ROWS * 4 * TOK * KVW, bytes_accessed=6 << 20, transcendentals=ROWS * 4 * TOK
        ),
        compiler_params=pltpu.CompilerParams(vmem_limit_bytes=24 << 20),
        name="attention",
    )(place, doc, q, qt, g, gt, own, px, p2, sw)


def queries_kernel(ds_ref, own_ref, px_ref, p2_ref, sw_ref, out_ref, kv_ref):
    for slot, ref in enumerate((own_ref, px_ref, p2_ref, sw_ref)):
        kv_ref[:, slot * TOK : (slot + 1) * TOK] = ref[...]
    for head in range(HEADS):
        rows = slice(head * TOK, (head + 1) * TOK)
        total = lax.dot_general(
            kv_ref[...], ds_ref[rows, :], (((1,), (1,)), ((), ())), preferred_element_type=jnp.float32
        )
        out_ref[head] = (total * softmax_scale).astype(jnp.bfloat16)


def query_grads(ds, own, px, p2, sw):
    return pl.pallas_call(
        queries_kernel,
        out_shape=jax.ShapeDtypeStruct((HEADS, KVW, TOK), jnp.bfloat16),
        in_specs=[whole] * 5,
        out_specs=whole,
        scratch_shapes=[pltpu.VMEM((KVW, 4 * TOK), jnp.bfloat16)],
        cost_estimate=pl.CostEstimate(
            flops=2 * ROWS * 4 * TOK * KVW, bytes_accessed=2 << 20, transcendentals=0
        ),
        compiler_params=pltpu.CompilerParams(vmem_limit_bytes=12 << 20),
        name="query_grads",
    )(ds, own, px, p2, sw)


def combine_kernel(came_ref, own_ref, px_ref, p2_ref, sw_ref, sum_ref):
    total = came_ref[0].astype(jnp.float32)
    for source in range(1, SHARES):
        total = total + came_ref[source].astype(jnp.float32)
    sum_ref[...] = total
    for slot, ref in enumerate((own_ref, px_ref, p2_ref, sw_ref)):
        ref[...] = sum_ref[pl.ds(slot, SHARE, stride=4), :]


def combine(came):
    shape = jax.ShapeDtypeStruct((SHARE, TOK), jnp.float32)
    return pl.pallas_call(
        combine_kernel,
        out_shape=(shape,) * 4,
        in_specs=[whole],
        out_specs=(whole,) * 4,
        scratch_shapes=[pltpu.VMEM((4 * SHARE, TOK), jnp.float32)],
        cost_estimate=pl.CostEstimate(flops=1 << 19, bytes_accessed=1 << 20, transcendentals=0),
        compiler_params=pltpu.CompilerParams(vmem_limit_bytes=8 << 20),
        name="combine",
    )(came)


def finish_kernel(place, came_ref, out_ref):
    turn = lax.rem(lax.div(place[0], 2), 2) * (SHARES // 2)
    for share in range(SHARES):
        rows = slice(SHARE * share, SHARE * (share + 1))
        out_ref[rows, :] = came_ref[lax.rem(share + turn, SHARES)].astype(jnp.float32)


def finish(place, came):
    return pl.pallas_call(
        finish_kernel,
        out_shape=jax.ShapeDtypeStruct((KVW, TOK), jnp.float32),
        in_specs=[scalars, whole],
        out_specs=whole,
        cost_estimate=pl.CostEstimate(flops=1 << 17, bytes_accessed=1 << 19, transcendentals=0),
        compiler_params=pltpu.CompilerParams(vmem_limit_bytes=8 << 20),
        name="finish",
    )(place, came)


def routes(count):
    across = SHARES // 2
    halo = [(i, i + 2, across) for i in range(count)]
    mixed = [(i, i + 1 + 2 * (i % 2), 0) for i in range(count)]
    turned = [(i, i + 3 - 2 * (i % 2), across) for i in range(count)]

    def pairs(moves, back):
        route = []
        for start, end, other in moves:
            if end < count:
                for head in range(SHARES):
                    pair = (start * SHARES + head, end * SHARES + (head ^ other))
                    route.append(pair[::-1] if back else pair)
        return route

    return pairs(halo, False), pairs(mixed, False), [pairs(m, True) for m in (mixed, halo, turned)]


def per_device(queries, latent_kv, grad_out, doc_start):
    tokens, _, width = queries.shape
    everyone = SEQ + HEAD
    halo, mixed, back = routes(lax.axis_size(SEQ))
    place = lax.axis_index(SEQ).astype(jnp.int32).reshape(1)

    own = latent_kv.T
    p2 = lax.ppermute(own, everyone, halo)
    px = lax.ppermute(own, everyone, mixed)
    sw = lax.ppermute(p2, "core", [(0, 1), (1, 0)])

    q = queries.transpose(1, 0, 2).reshape(ROWS, width)
    qt = queries.transpose(2, 1, 0).reshape(width, ROWS)
    g = grad_out.transpose(1, 0, 2).reshape(ROWS, LAT)
    gt = jnp.pad(grad_out.transpose(2, 1, 0).reshape(LAT, ROWS), ((0, width - LAT), (0, 0)))
    doc = doc_start.astype(jnp.float32).reshape(1, tokens)

    terms, ds = attention(place, doc, q, qt, g, gt, own, px, p2, sw)
    came = lax.all_to_all(terms, HEAD, 0, 0, tiled=True)
    mine, *others = combine(came)
    ds, mine, *others = lax.optimization_barrier((ds, mine, *others))
    for part, route in zip(others, back):
        mine = mine + lax.ppermute(part, everyone, route)
    query_grad = query_grads(ds, own, px, p2, sw)
    mine, query_grad = lax.optimization_barrier((mine.astype(jnp.bfloat16), query_grad))
    spread = jnp.broadcast_to(mine[None], (SHARES, SHARE, tokens))
    grad = lax.all_to_all(spread, HEAD, 0, 0, tiled=True)
    return query_grad.transpose(2, 0, 1), finish(place, grad).T


def solution(mesh):
    fine = Mesh(mesh.devices.reshape(8, 2, 2, 4, 8), ("z", "xh", "core", "xl", "y"))
    in_specs = (P(SEQ, HEAD, None), P(SEQ, None), P(SEQ, HEAD, None), P(SEQ))
    out_specs = (P(SEQ, HEAD, None), P(SEQ, None))
    return jax.shard_map(
        per_device, mesh=fine, in_specs=in_specs, out_specs=out_specs, check_vma=False
    )
```

time: 87.6 us -> 83.7 us (0.955)
  the two profiles are of different devices: /device:TPU:640 before, /device:TPU:398 now
where the time goes in v3:
time: 83.7 us; the launch traced here: 83.3 us
  blocking collectives  45.7 us (55%)
  starting transfers between devices  21 us (25%)
  waiting for transfers between devices  7.49 us (9%)
  Pallas kernels  5.13 us (6%)
  local copies, waits for them, and re-layouts  3.27 us (4%)
    all_to_all x1, blocking collectives, per_device(): came = lax.all_to_all(terms, HEAD, 0, 0, tiled=True)  28.9 us
    all_to_all x1, blocking collectives, per_device(): grad = lax.all_to_all(spread, HEAD, 0, 0, tiled=True)  16.8 us
    ppermute x3, starting transfers between devices, per_device(): mine = mine + lax.ppermute(part, everyone, route)  8.78 us
    ppermute x1, starting transfers between devices, per_device(): p2 = lax.ppermute(own, everyone, halo)  7.13 us
    ppermute x3, waiting for transfers between devices, per_device(): mine = mine + lax.ppermute(part, everyone, route)  5.26 us
    ppermute x1, starting transfers between devices, per_device(): sw = lax.ppermute(p2, 'core', [(0, 1), (1, 0)])  3.14 us
    pallas_call x1, Pallas kernels, attention(): pl.pallas_call(attention_kernel, out_shape=(jax.ShapeDtypeStruct((SHARES,...  2.67 us
    ppermute x1, starting transfers between devices, per_device(): px = lax.ppermute(own, everyone, mixed)  1.92 us
  transfers between devices with their start and end apart: 6, of which 4 were waited for; matrix products, arithmetic and copies ran while one was open for 3% of the time, Pallas kernels for 2%

profile of v3, /device:TPU:398, one launch (start us, length us, event | category | flops | bytes accessed | tf_op | source)
XLA Modules:
  0.0 83.3 jit_solution(12091345309320037024)
XLA Ops:
  0.6 7.1 %collective-permute-start.1 = (bf16[576,128]{1,0:T(8,128)(2,1)}, bf16[576,128]{1,0:T(8,128)(2,1)S(1)}, u32[]{:S(2)}, u32[]{:S(2)}) collective-permute-start(bf16[576,128]{1,0:T(8,128)(2,1)} %bitcast.23), channel_id=1, source_target_pairs={{0,80},{1,81},{2,82},{3,83},{4,84},{5,85},{6,86},{7,87},{8,88},{9,... | collective-permute-start | bytes 442376 | tf_op jit(solution)/shard_map/ppermute | solution.py:185
  7.8 1.9 %collective-permute-start = (bf16[576,128]{1,0:T(8,128)(2,1)}, bf16[576,128]{1,0:T(8,128)(2,1)S(1)}, u32[]{:S(2)}, u32[]{:S(2)}) collective-permute-start(bf16[576,128]{1,0:T(8,128)(2,1)} %bitcast.24), channel_id=1, source_target_pairs={{0,32},{1,33},{2,34},{3,35},{4,36},{5,37},{6,38},{7,39},{8,40},{9,... | collective-permute-start | bytes 442376 | tf_op jit(solution)/shard_map/ppermute | solution.py:186
  9.7 0.0 copy-start.2
  9.7 1.2 %copy.8 = bf16[4,128,512]{2,1,0:T(8,128)(2,1)S(1)} copy(bf16[4,128,512]{2,0,1:T(4,128)(2,1)} %bitcast.28) | data formatting | bytes 1048576 | tf_op jit(solution)/shard_map/transpose | solution.py:191
  10.9 0.0 copy-done.2
  10.9 0.6 copy.9
  11.5 0.0 copy-start.1
  11.5 0.1 copy.14
  11.6 1.0 %copy-done.1 = bf16[128,4,576]{0,2,1:T(8,128)(2,1)S(1)} copy-done((bf16[128,4,576]{0,2,1:T(8,128)(2,1)S(1)}, bf16[128,4,576]{0,2,1:T(8,128)(2,1)}, u32[]{:S(2)}) %copy-start.1) | copy-done | bytes 589848
  12.6 0.3 copy.6
  12.9 0.0 copy-start.3
  12.9 0.0 copy-start
  13.0 0.1 copy_bitcast_fusion.qt_ref
  13.0 1.3 %collective-permute-done.1.p2_ref = bf16[576,128]{1,0:T(8,128)(2,1)S(1)} collective-permute-done((bf16[576,128]{1,0:T(8,128)(2,1)}, bf16[576,128]{1,0:T(8,128)(2,1)S(1)}, u32[]{:S(2)}, u32[]{:S(2)}) %collective-permute-start.1) | collective-permute-done | bytes 147488 | tf_op jit(solution)/shard_map/ppermute | solution.py:185
  14.3 3.1 %collective-permute-start.2 = (bf16[576,128]{1,0:T(8,128)(2,1)S(1)}, bf16[576,128]{1,0:T(8,128)(2,1)S(1)}, u32[]{:S(2)}, u32[]{:S(2)}) collective-permute-start(bf16[576,128]{1,0:T(8,128)(2,1)S(1)} %collective-permute-done.1.p2_ref), channel_id=1, source_target_pairs={{0,32},{32,0},{1,33},{33,1},{2,34},{34,2},{3,35},{35,3},{4,36},{36... | collective-permute-start | bytes 442376 | tf_op jit(solution)/shard_map/ppermute | solution.py:187
  17.4 0.0 copy-done.3
  17.5 0.0 collective-permute-done.px_ref
  17.5 1.0 %collective-permute-done.2.sw_ref = bf16[576,128]{1,0:T(8,128)(2,1)S(1)} collective-permute-done((bf16[576,128]{1,0:T(8,128)(2,1)S(1)}, bf16[576,128]{1,0:T(8,128)(2,1)S(1)}, u32[]{:S(2)}, u32[]{:S(2)}) %collective-permute-start.2) | collective-permute-done | bytes 147488 | tf_op jit(solution)/shard_map/ppermute | solution.py:187
  18.4 0.0 copy-done
  18.4 2.7 %attention.1 = (bf16[32,72,128]{2,1,0:T(8,128)(2,1)S(1)}, bf16[512,512]{1,0:T(8,128)(2,1)S(1)}) custom-call(s32[1]{0:T(128)} %bitcast.place, f32[1,128]{1,0:T(1,128)S(1)} %convert_bitcast_fusion.doc_ref, bf16[512,576]{1,0:T(8,128)(2,1)S(1)} %bitcast.21, bf16[576,512]{1,0:T(8,128)(2,1)S(1)} %copy_bitcast_fusion.qt_ref, bf16[512,512]{1,0:T(8,128)(2,1)S(1)} %bitcast.22, ...), custom_call_target="tpu_custom_call" | custom-call | flops 1207959552 | bytes 6291456 | tf_op jit(solution)/shard_map/attention/pallas_call | solution.py:70
  21.1 28.9 %all_to_all.10.came_ref = bf16[32,72,128]{2,1,0:T(8,128)(2,1)S(1)} all-to-all(bf16[32,72,128]{2,1,0:T(8,128)(2,1)S(1)} %get-tuple-element.16), channel_id=1, replica_groups=mesh['z'=8,'xh'=2,'core'=2,'xl'=4,'y'=8] {'xl','y'}, dimensions={0} | all-to-all | bytes 1179648 | tf_op jit(solution)/shard_map/all_to_all | solution.py:196
  50.0 0.1 combine.1
  50.1 1.9 %collective-permute-start.3 = (f32[18,128]{1,0:T(8,128)S(1)}, f32[18,128]{1,0:T(8,128)S(1)}, u32[]{:S(2)}, u32[]{:S(2)}) collective-permute-start(f32[18,128]{1,0:T(8,128)S(1)} %get-tuple-element.22), channel_id=1, source_target_pairs={{32,0},{33,1},{34,2},{35,3},{36,4},{37,5},{38,6},{39,7},{40,8},{41... | collective-permute-start | bytes 27656 | tf_op jit(solution)/shard_map/ppermute | solution.py:200
  52.0 4.5 %collective-permute-start.4 = (f32[18,128]{1,0:T(8,128)S(1)}, f32[18,128]{1,0:T(8,128)S(1)}, u32[]{:S(2)}, u32[]{:S(2)}) collective-permute-start(f32[18,128]{1,0:T(8,128)S(1)} %get-tuple-element.23), channel_id=1, source_target_pairs={{80,0},{81,1},{82,2},{83,3},{84,4},{85,5},{86,6},{87,7},{88,8},{89... | collective-permute-start | bytes 27656 | tf_op jit(solution)/shard_map/ppermute | solution.py:200
  56.5 2.4 %collective-permute-start.5 = (f32[18,128]{1,0:T(8,128)S(1)}, f32[18,128]{1,0:T(8,128)S(1)}, u32[]{:S(2)}, u32[]{:S(2)}) collective-permute-start(f32[18,128]{1,0:T(8,128)S(1)} %get-tuple-element.24), channel_id=1, source_target_pairs={{112,0},{113,1},{114,2},{115,3},{116,4},{117,5},{118,6},{119,7},{1... | collective-permute-start | bytes 27656 | tf_op jit(solution)/shard_map/ppermute | solution.py:200
  58.9 1.6 %query_grads.1 = bf16[4,576,128]{2,1,0:T(8,128)(2,1)} custom-call(bf16[512,512]{1,0:T(8,128)(2,1)S(1)} %get-tuple-element.25.ds_ref, bf16[576,128]{1,0:T(8,128)(2,1)S(1)} %bitcast.26, bf16[576,128]{1,0:T(8,128)(2,1)S(1)} %collective-permute-done.px_ref, bf16[576,128]{1,0:T(8,128)(2,1)S(1)} %collective-permute-done.1.p2_ref, ...), custom_call_target="tpu_custom_call" | custom-call | flops 301989888 | bytes 2097152 | tf_op jit(solution)/shard_map/query_grads/pallas_call | solution.py:104
  60.5 0.0 collective-permute-done.3
  60.5 1.3 %collective-permute-done.4 = f32[18,128]{1,0:T(8,128)S(1)} collective-permute-done((f32[18,128]{1,0:T(8,128)S(1)}, f32[18,128]{1,0:T(8,128)S(1)}, u32[]{:S(2)}, u32[]{:S(2)}) %collective-permute-start.4) | collective-permute-done | bytes 9248 | tf_op jit(solution)/shard_map/ppermute | solution.py:200
  61.8 3.9 %collective-permute-done.5 = f32[18,128]{1,0:T(8,128)S(1)} collective-permute-done((f32[18,128]{1,0:T(8,128)S(1)}, f32[18,128]{1,0:T(8,128)S(1)}, u32[]{:S(2)}, u32[]{:S(2)}) %collective-permute-start.5) | collective-permute-done | bytes 9248 | tf_op jit(solution)/shard_map/ppermute | solution.py:200
  65.8 16.8 %all_to_all.11.came_ref = bf16[32,18,128]{2,1,0:T(8,128)(2,1)S(1)} all-to-all(bf16[32,18,128]{2,1,0:T(8,128)(2,1)S(1)} %broadcast_in_dim.2), channel_id=1, replica_groups=mesh['z'=8,'xh'=2,'core'=2,'xl'=4,'y'=8] {'xl','y'}, dimensions={0} | all-to-all | bytes 294912 | tf_op jit(solution)/shard_map/all_to_all | solution.py:204
  82.6 0.8 finish.1
  (4 shorter events, 0.1 us)
Async XLA Ops:
  0.6 13.7 %collective-permute-start.1 = (bf16[576,128]{1,0:T(8,128)(2,1)}, bf16[576,128]{1,0:T(8,128)(2,1)S(1)}, u32[]{:S(2)}, u32[]{:S(2)}) collective-permute-start(bf16[576,128]{1,0:T(8,128)(2,1)} %bitcast.23), channel_id=1, source_target_pairs={{0,80},{1,81},{2,82},{3,83},{4,84},{5,85},{6,86},{7,87},{8,88},{9,... | collective-permute-start | bytes 442376 | tf_op jit(solution)/shard_map/ppermute | solution.py:185
  7.8 9.7 %collective-permute-start = (bf16[576,128]{1,0:T(8,128)(2,1)}, bf16[576,128]{1,0:T(8,128)(2,1)S(1)}, u32[]{:S(2)}, u32[]{:S(2)}) collective-permute-start(bf16[576,128]{1,0:T(8,128)(2,1)} %bitcast.24), channel_id=1, source_target_pairs={{0,32},{1,33},{2,34},{3,35},{4,36},{5,37},{6,38},{7,39},{8,40},{9,... | collective-permute-start | bytes 442376 | tf_op jit(solution)/shard_map/ppermute | solution.py:186
  9.7 1.2 %copy-start.2 = (bf16[128,4,512]{2,1,0:T(4,128)(2,1)S(1)}, bf16[128,4,512]{2,1,0:T(4,128)(2,1)}, u32[]{:S(2)}) copy-start(bf16[128,4,512]{2,1,0:T(4,128)(2,1)} %param.6) | copy-start | bytes 1572868
  11.5 1.1 %copy-start.1 = (bf16[128,4,576]{0,2,1:T(8,128)(2,1)S(1)}, bf16[128,4,576]{0,2,1:T(8,128)(2,1)}, u32[]{:S(2)}) copy-start(bf16[128,4,576]{0,2,1:T(8,128)(2,1)} %param.4) | copy-start | bytes 1769476
  12.9 4.5 %copy-start.3 = (s32[128]{0:T(128)S(1)}, s32[128]{0:T(128)}, u32[]{:S(2)}) copy-start(s32[128]{0:T(128)} %param.7) | copy-start | bytes 1540
  12.9 5.5 %copy-start = (bf16[128,576]{0,1:T(8,128)(2,1)S(1)}, bf16[128,576]{0,1:T(8,128)(2,1)}, u32[]{:S(2)}) copy-start(bf16[128,576]{0,1:T(8,128)(2,1)} %param.5) | copy-start | bytes 442372
  14.3 4.1 %collective-permute-start.2 = (bf16[576,128]{1,0:T(8,128)(2,1)S(1)}, bf16[576,128]{1,0:T(8,128)(2,1)S(1)}, u32[]{:S(2)}, u32[]{:S(2)}) collective-permute-start(bf16[576,128]{1,0:T(8,128)(2,1)S(1)} %collective-permute-done.1.p2_ref), channel_id=1, source_target_pairs={{0,32},{32,0},{1,33},{33,1},{2,34},{34,2},{3,35},{35,3},{4,36},{36... | collective-permute-start | bytes 442376 | tf_op jit(solution)/shard_map/ppermute | solution.py:187
  50.1 10.4 %collective-permute-start.3 = (f32[18,128]{1,0:T(8,128)S(1)}, f32[18,128]{1,0:T(8,128)S(1)}, u32[]{:S(2)}, u32[]{:S(2)}) collective-permute-start(f32[18,128]{1,0:T(8,128)S(1)} %get-tuple-element.22), channel_id=1, source_target_pairs={{32,0},{33,1},{34,2},{35,3},{36,4},{37,5},{38,6},{39,7},{40,8},{41... | collective-permute-start | bytes 27656 | tf_op jit(solution)/shard_map/ppermute | solution.py:200
  52.0 9.8 %collective-permute-start.4 = (f32[18,128]{1,0:T(8,128)S(1)}, f32[18,128]{1,0:T(8,128)S(1)}, u32[]{:S(2)}, u32[]{:S(2)}) collective-permute-start(f32[18,128]{1,0:T(8,128)S(1)} %get-tuple-element.23), channel_id=1, source_target_pairs={{80,0},{81,1},{82,2},{83,3},{84,4},{85,5},{86,6},{87,7},{88,8},{89... | collective-permute-start | bytes 27656 | tf_op jit(solution)/shard_map/ppermute | solution.py:200
  56.5 9.2 %collective-permute-start.5 = (f32[18,128]{1,0:T(8,128)S(1)}, f32[18,128]{1,0:T(8,128)S(1)}, u32[]{:S(2)}, u32[]{:S(2)}) collective-permute-start(f32[18,128]{1,0:T(8,128)S(1)} %get-tuple-element.24), channel_id=1, source_target_pairs={{112,0},{113,1},{114,2},{115,3},{116,4},{117,5},{118,6},{119,7},{1... | collective-permute-start | bytes 27656 | tf_op jit(solution)/shard_map/ppermute | solution.py:200

commit v4 on v3

v4 whole, which is shorter than its diff:
```python
import jax
import jax.numpy as jnp
from jax import lax
from jax.experimental import pallas as pl
from jax.experimental.pallas import tpu as pltpu
from jax.sharding import Mesh
from jax.sharding import PartitionSpec as P

LAT = 512
KVW = 576
TOK = 128
HEADS = 4
ROWS = TOK * HEADS
PART = 72
SHARES = 32
SHARE = KVW // SHARES
SEQ = ("z", "xh", "core")
HEAD = ("xl", "y")

softmax_scale = 192.0 ** (-0.5)
lowest = -1e30
whole = pl.BlockSpec(memory_space=pltpu.VMEM)
scalars = pl.BlockSpec(memory_space=pltpu.SMEM)


def f32_dot(a, b):
    return jnp.dot(a, b, preferred_element_type=jnp.float32)


def attention_kernel(
    place, doc_ref, q_ref, qt_ref, g_ref, gt_ref, own_ref, px_ref, p2_ref, sw_ref,
    keep_ref, send_ref, ds_ref, kv_ref, bias_ref, p_ref,
):
    seq = place[0]
    core = lax.rem(seq, 2)
    for slot, ref in enumerate((own_ref, px_ref, p2_ref, sw_ref)):
        kv_ref[:, slot * TOK : (slot + 1) * TOK] = ref[...]
    first = jnp.broadcast_to(doc_ref[...], (TOK, TOK)).T
    row = lax.broadcasted_iota(jnp.int32, (TOK, TOK), 0)
    lane = lax.broadcasted_iota(jnp.int32, (TOK, TOK), 1)
    for slot, back in enumerate((0, 3 - 2 * core, 2, 1 + 2 * core)):
        key = lane + (seq - back) * TOK
        seen = (key <= row + seq * TOK) & (key.astype(jnp.float32) >= first)
        bias_ref[:, slot * TOK : (slot + 1) * TOK] = jnp.where(seen, 0.0, lowest)
    for head in range(HEADS):
        rows = slice(head * TOK, (head + 1) * TOK)
        scores = f32_dot(q_ref[rows, :], kv_ref[...]) * softmax_scale + bias_ref[...]
        grad_probs = f32_dot(g_ref[rows, :], kv_ref[:LAT, :])
        top = jnp.max(scores, axis=1, keepdims=True)
        exps = jnp.exp(scores - top)
        inverse = 1.0 / jnp.sum(exps, axis=1, keepdims=True)
        delta = jnp.sum(exps * grad_probs, axis=1, keepdims=True) * inverse
        probs = exps * inverse
        p_ref[rows, :] = probs.astype(jnp.bfloat16)
        ds_ref[rows, :] = (probs * (grad_probs - delta)).astype(jnp.bfloat16)
    for part in range(KVW // PART):
        cols = slice(part * PART, (part + 1) * PART)
        term = f32_dot(qt_ref[cols, :], ds_ref[...]) * softmax_scale
        term = term + f32_dot(gt_ref[cols, :], p_ref[...])
        keep_ref[0, cols, :] = term[:, 0 * TOK : 1 * TOK]
        send_ref[0, cols, :] = term[:, 1 * TOK : 2 * TOK].astype(jnp.bfloat16)
        keep_ref[1, cols, :] = term[:, 2 * TOK : 3 * TOK]
        send_ref[1, cols, :] = term[:, 3 * TOK : 4 * TOK].astype(jnp.bfloat16)


def attention(place, doc, q, qt, g, gt, own, px, p2, sw):
    return pl.pallas_call(
        attention_kernel,
        out_shape=(
            jax.ShapeDtypeStruct((2, KVW, TOK), jnp.float32),
            jax.ShapeDtypeStruct((2, KVW, TOK), jnp.bfloat16),
            jax.ShapeDtypeStruct((ROWS, 4 * TOK), jnp.bfloat16),
        ),
        in_specs=[scalars] + [whole] * 9,
        out_specs=(whole, whole, whole),
        scratch_shapes=[
            pltpu.VMEM((KVW, 4 * TOK), jnp.bfloat16),
            pltpu.VMEM((TOK, 4 * TOK), jnp.float32),
            pltpu.VMEM((ROWS, 4 * TOK), jnp.bfloat16),
        ],
        cost_estimate=pl.CostEstimate(
            flops=4 * 2 * ROWS * 4 * TOK * KVW, bytes_accessed=6 << 20, transcendentals=ROWS * 4 * TOK
        ),
        compiler_params=pltpu.CompilerParams(vmem_limit_bytes=24 << 20),
        name="attention",
    )(place, doc, q, qt, g, gt, own, px, p2, sw)


def queries_kernel(ds_ref, own_ref, px_ref, p2_ref, sw_ref, out_ref, kv_ref):
    for slot, ref in enumerate((own_ref, px_ref, p2_ref, sw_ref)):
        kv_ref[:, slot * TOK : (slot + 1) * TOK] = ref[...]
    for head in range(HEADS):
        rows = slice(head * TOK, (head + 1) * TOK)
        total = lax.dot_general(
            kv_ref[...], ds_ref[rows, :], (((1,), (1,)), ((), ())), preferred_element_type=jnp.float32
        )
        out_ref[head] = (total * softmax_scale).astype(jnp.bfloat16)


def query_grads(ds, own, px, p2, sw):
    return pl.pallas_call(
        queries_kernel,
        out_shape=jax.ShapeDtypeStruct((HEADS, KVW, TOK), jnp.bfloat16),
        in_specs=[whole] * 5,
        out_specs=whole,
        scratch_shapes=[pltpu.VMEM((KVW, 4 * TOK), jnp.bfloat16)],
        cost_estimate=pl.CostEstimate(
            flops=2 * ROWS * 4 * TOK * KVW, bytes_accessed=2 << 20, transcendentals=0
        ),
        compiler_params=pltpu.CompilerParams(vmem_limit_bytes=12 << 20),
        name="query_grads",
    )(ds, own, px, p2, sw)


def small_call(kernel, name, out_shape, count, scratch=()):
    outs = out_shape if isinstance(out_shape, tuple) else (out_shape,)
    specs = (whole,) * len(outs)
    return pl.pallas_call(
        kernel,
        out_shape=out_shape,
        in_specs=[scalars] + [whole] * count,
        out_specs=specs if isinstance(out_shape, tuple) else whole,
        scratch_shapes=list(scratch),
        cost_estimate=pl.CostEstimate(flops=1 << 19, bytes_accessed=1 << 20, transcendentals=0),
        compiler_params=pltpu.CompilerParams(vmem_limit_bytes=8 << 20),
        name=name,
    )


def join_kernel(place, keep_ref, came_ref, next_ref, over_ref):
    odd = lax.rem(place[0], 2) == 1
    for part in range(KVW // PART):
        cols = slice(part * PART, (part + 1) * PART)
        side = came_ref[1, cols, :].astype(jnp.float32)
        next_ref[cols, :] = (keep_ref[1, cols, :] + side).astype(jnp.bfloat16)
        far = came_ref[0, cols, :].astype(jnp.float32)
        over_ref[cols, :] = jnp.where(odd, far, jnp.zeros_like(far)).astype(jnp.bfloat16)


def total_kernel(place, keep_ref, came_ref, next_ref, over_ref, out_ref, sum_ref):
    even = lax.rem(place[0], 2) == 0
    for part in range(KVW // PART):
        cols = slice(part * PART, (part + 1) * PART)
        near = came_ref[0, cols, :].astype(jnp.float32)
        total = keep_ref[0, cols, :] + jnp.where(even, near, jnp.zeros_like(near))
        total = total + next_ref[cols, :].astype(jnp.float32)
        sum_ref[cols, :] = total + over_ref[cols, :].astype(jnp.float32)
    for share in range(SHARES):
        rows = slice(SHARE * share, SHARE * (share + 1))
        out_ref[share] = sum_ref[rows, :].astype(jnp.bfloat16)


def reduce_kernel(place, came_ref, out_ref):
    total = came_ref[0].astype(jnp.float32)
    for source in range(1, SHARES):
        total = total + came_ref[source].astype(jnp.float32)
    total = total.astype(jnp.bfloat16)
    for share in range(SHARES):
        out_ref[share] = total


def finish_kernel(place, came_ref, out_ref):
    for share in range(SHARES):
        rows = slice(SHARE * share, SHARE * (share + 1))
        out_ref[rows, :] = came_ref[share].astype(jnp.float32)


def routes(count):
    across = SHARES // 2

    def pairs(moves):
        return [
            (a * SHARES + head, b * SHARES + (head ^ other))
            for a, b, other in moves
            if 0 <= b < count
            for head in range(SHARES)
        ]

    halo = pairs([(i, i + 2, across) for i in range(count)])
    mixed = pairs([(i, i + 1 + 2 * (i % 2), 0) for i in range(count)])
    back = pairs([(i, i - 2, across) for i in range(count)])
    over = pairs([(i, i - 4, 0) for i in range(1, count, 2)])
    return halo, mixed, back, over


def per_device(queries, latent_kv, grad_out, doc_start):
    tokens, _, width = queries.shape
    everyone = SEQ + HEAD
    swap = [(0, 1), (1, 0)]
    halo, mixed, back, over = routes(lax.axis_size(SEQ))
    place = lax.axis_index(SEQ).astype(jnp.int32).reshape(1)

    own = latent_kv.T
    p2 = lax.ppermute(own, everyone, halo)
    px = lax.ppermute(own, everyone, mixed)
    sw = lax.ppermute(p2, "core", swap)

    q = queries.transpose(1, 0, 2).reshape(ROWS, width)
    qt = queries.transpose(2, 1, 0).reshape(width, ROWS)
    g = grad_out.transpose(1, 0, 2).reshape(ROWS, LAT)
    gt = jnp.pad(grad_out.transpose(2, 1, 0).reshape(LAT, ROWS), ((0, width - LAT), (0, 0)))
    doc = doc_start.astype(jnp.float32).reshape(1, tokens)

    keep, send, ds = attention(place, doc, q, qt, g, gt, own, px, p2, sw)
    came = lax.ppermute(send, "core", swap)
    block = jax.ShapeDtypeStruct((width, tokens), jnp.bfloat16)
    pieces = jax.ShapeDtypeStruct((SHARES, SHARE, tokens), jnp.bfloat16)
    to_next, to_over = small_call(join_kernel, "join", (block, block), 2)(place, keep, came)
    ds, to_next, to_over = lax.optimization_barrier((ds, to_next, to_over))
    to_next = lax.ppermute(to_next, everyone, back)
    to_over = lax.ppermute(to_over, everyone, over)
    query_grad = query_grads(ds, own, px, p2, sw)
    to_next, to_over, query_grad = lax.optimization_barrier((to_next, to_over, query_grad))

    terms = small_call(
        total_kernel, "total", pieces, 4, [pltpu.VMEM((width, tokens), jnp.float32)]
    )(place, keep, came, to_next, to_over)
    terms = lax.all_to_all(terms, HEAD, 0, 0, tiled=True)
    terms = small_call(reduce_kernel, "reduce", pieces, 1)(place, terms)
    grad = lax.all_to_all(terms, HEAD, 0, 0, tiled=True)
    out = jax.ShapeDtypeStruct((width, tokens), jnp.float32)
    grad = small_call(finish_kernel, "finish", out, 1)(place, grad)
    return query_grad.transpose(2, 0, 1), grad.T


def solution(mesh):
    fine = Mesh(mesh.devices.reshape(8, 2, 2, 4, 8), ("z", "xh", "core", "xl", "y"))
    in_specs = (P(SEQ, HEAD, None), P(SEQ, None), P(SEQ, HEAD, None), P(SEQ))
    out_specs = (P(SEQ, HEAD, None), P(SEQ, None))
    return jax.shard_map(
        per_device, mesh=fine, in_specs=in_specs, out_specs=out_specs, check_vma=False
    )
```

time: 83.7 us -> 76.6 us (0.915)
  blocking collectives: 45.7 us -> 38.4 us
  waiting for transfers between devices: 7.49 us -> 10.6 us
  starting transfers between devices: 21 us -> 18.1 us
    all_to_all x2, blocking collectives: 45.7 us -> 38.4 us  [the longest x1 23.4 us: per_device(): terms = lax.all_to_all(terms, HEAD, 0, 0, tiled=True)]
    ppermute x4, waiting for transfers between devices: 6.22 us -> 9.37 us  [the longest x1 7.22 us: per_device(): to_next = lax.ppermute(to_next, everyone, back)]
    ppermute x4, starting transfers between devices: 11.9 us -> 9.01 us  [the longest x1 3.14 us: per_device(): sw = lax.ppermute(p2, 'core', swap)]
    pallas_call x3 -> x5, Pallas kernels: 3.53 us -> 3.55 us  [the longest x1 2.6 us: attention(): pl.pallas_call(attention_kernel, out_shape=(jax.ShapeDtypeStruct((2, KVW,...]
where the time goes in v4:
time: 76.6 us; the launch traced here: 76.3 us
  blocking collectives  38.4 us (50%)
  starting transfers between devices  18.1 us (24%)
  waiting for transfers between devices  10.6 us (14%)
  Pallas kernels  5.15 us (7%)
  local copies, waits for them, and re-layouts  3.24 us (4%)
  between operations  0.81 us (1%)
    all_to_all x1, blocking collectives, per_device(): terms = lax.all_to_all(terms, HEAD, 0, 0, tiled=True)  23.4 us
    all_to_all x1, blocking collectives, per_device(): grad = lax.all_to_all(terms, HEAD, 0, 0, tiled=True)  14.9 us
    ppermute x1, waiting for transfers between devices, per_device(): to_next = lax.ppermute(to_next, everyone, back)  7.22 us
    ppermute x1, starting transfers between devices, per_device(): p2 = lax.ppermute(own, everyone, halo)  7.13 us
    ppermute x1, starting transfers between devices, per_device(): sw = lax.ppermute(p2, 'core', swap)  3.14 us
    ppermute x1, starting transfers between devices, per_device(): to_next = lax.ppermute(to_next, everyone, back)  2.93 us
    pallas_call x1, Pallas kernels, attention(): pl.pallas_call(attention_kernel, out_shape=(jax.ShapeDtypeStruct((2, KVW,...  2.6 us
    ppermute x1, starting transfers between devices, per_device(): came = lax.ppermute(send, 'core', swap)  2.27 us
  transfers between devices with their start and end apart: 6, of which 4 were waited for; matrix products, arithmetic and copies ran while one was open for 3% of the time, Pallas kernels for 2%

profile of v4, /device:TPU:398, one launch (start us, length us, event | category | flops | bytes accessed | tf_op | source)
XLA Modules:
  0.0 76.3 jit_solution(16122746160263724847)
XLA Ops:
  0.6 7.1 %collective-permute-start.1 = (bf16[576,128]{1,0:T(8,128)(2,1)}, bf16[576,128]{1,0:T(8,128)(2,1)S(1)}, u32[]{:S(2)}, u32[]{:S(2)}) collective-permute-start(bf16[576,128]{1,0:T(8,128)(2,1)} %bitcast.23), channel_id=1, source_target_pairs={{0,80},{1,81},{2,82},{3,83},{4,84},{5,85},{6,86},{7,87},{8,88},{9,... | collective-permute-start | bytes 442376 | tf_op jit(solution)/shard_map/ppermute | solution.py:194
  7.8 1.9 %collective-permute-start = (bf16[576,128]{1,0:T(8,128)(2,1)}, bf16[576,128]{1,0:T(8,128)(2,1)S(1)}, u32[]{:S(2)}, u32[]{:S(2)}) collective-permute-start(bf16[576,128]{1,0:T(8,128)(2,1)} %bitcast.24), channel_id=1, source_target_pairs={{0,32},{1,33},{2,34},{3,35},{4,36},{5,37},{6,38},{7,39},{8,40},{9,... | collective-permute-start | bytes 442376 | tf_op jit(solution)/shard_map/ppermute | solution.py:195
  9.7 0.0 copy-start.2
  9.7 1.2 %copy.8 = bf16[4,128,512]{2,1,0:T(8,128)(2,1)S(1)} copy(bf16[4,128,512]{2,0,1:T(4,128)(2,1)} %bitcast.28) | data formatting | bytes 1048576 | tf_op jit(solution)/shard_map/transpose | solution.py:200
  10.9 0.0 copy-done.2
  10.9 0.6 copy.9
  11.5 0.0 copy-start.1
  11.5 0.1 copy.14
  11.6 1.0 %copy-done.1 = bf16[128,4,576]{0,2,1:T(8,128)(2,1)S(1)} copy-done((bf16[128,4,576]{0,2,1:T(8,128)(2,1)S(1)}, bf16[128,4,576]{0,2,1:T(8,128)(2,1)}, u32[]{:S(2)}) %copy-start.1) | copy-done | bytes 589848
  12.6 0.3 copy.6
  12.9 0.0 copy-start.3
  12.9 0.0 copy-start
  13.0 0.1 copy_bitcast_fusion.qt_ref
  13.0 1.3 %collective-permute-done.1.p2_ref = bf16[576,128]{1,0:T(8,128)(2,1)S(1)} collective-permute-done((bf16[576,128]{1,0:T(8,128)(2,1)}, bf16[576,128]{1,0:T(8,128)(2,1)S(1)}, u32[]{:S(2)}, u32[]{:S(2)}) %collective-permute-start.1) | collective-permute-done | bytes 147488 | tf_op jit(solution)/shard_map/ppermute | solution.py:194
  14.3 3.1 %collective-permute-start.2 = (bf16[576,128]{1,0:T(8,128)(2,1)S(1)}, bf16[576,128]{1,0:T(8,128)(2,1)S(1)}, u32[]{:S(2)}, u32[]{:S(2)}) collective-permute-start(bf16[576,128]{1,0:T(8,128)(2,1)S(1)} %collective-permute-done.1.p2_ref), channel_id=1, source_target_pairs={{0,32},{32,0},{1,33},{33,1},{2,34},{34,2},{3,35},{35,3},{4,36},{36... | collective-permute-start | bytes 442376 | tf_op jit(solution)/shard_map/ppermute | solution.py:196
  17.4 0.0 copy-done.3
  17.5 0.0 collective-permute-done.px_ref
  17.5 1.0 %collective-permute-done.2.sw_ref = bf16[576,128]{1,0:T(8,128)(2,1)S(1)} collective-permute-done((bf16[576,128]{1,0:T(8,128)(2,1)S(1)}, bf16[576,128]{1,0:T(8,128)(2,1)S(1)}, u32[]{:S(2)}, u32[]{:S(2)}) %collective-permute-start.2) | collective-permute-done | bytes 147488 | tf_op jit(solution)/shard_map/ppermute | solution.py:196
  18.4 0.0 copy-done
  18.4 2.6 %attention.1 = (f32[2,576,128]{2,1,0:T(8,128)S(1)}, bf16[2,576,128]{2,1,0:T(8,128)(2,1)S(1)}, bf16[512,512]{1,0:T(8,128)(2,1)S(1)}) custom-call(s32[1]{0:T(128)} %bitcast.place, f32[1,128]{1,0:T(1,128)S(1)} %convert_bitcast_fusion.doc_ref, bf16[512,576]{1,0:T(8,128)(2,1)S(1)} %bitcast.21, bf16[576,512]{1,0:T(8,128)(2,1)S(1)} %copy_bitcast_fusion.qt_ref, ...), custom_call_target="tpu_custom_call" | custom-call | flops 1207959552 | bytes 6291456 | tf_op jit(solution)/shard_map/attention/pallas_call | solution.py:67
  21.0 2.3 %collective-permute-start.3 = (bf16[2,576,128]{2,1,0:T(8,128)(2,1)S(1)}, bf16[2,576,128]{2,1,0:T(8,128)(2,1)S(1)}, u32[]{:S(2)}, u32[]{:S(2)}) collective-permute-start(bf16[2,576,128]{2,1,0:T(8,128)(2,1)S(1)} %get-tuple-element.15), channel_id=1, source_target_pairs={{0,32},{32,0},{1,33},{33,1},{2,34},{34,2},{3,35},{35,3},{4,36},{36... | collective-permute-start | bytes 884744 | tf_op jit(solution)/shard_map/ppermute | solution.py:205
  23.3 1.2 %collective-permute-done.3.came_ref = bf16[2,576,128]{2,1,0:T(8,128)(2,1)S(1)} collective-permute-done((bf16[2,576,128]{2,1,0:T(8,128)(2,1)S(1)}, bf16[2,576,128]{2,1,0:T(8,128)(2,1)S(1)}, u32[]{:S(2)}, u32[]{:S(2)}) %collective-permute-start.3) | collective-permute-done | bytes 294944 | tf_op jit(solution)/shard_map/ppermute | solution.py:205
  24.5 0.1 join.1
  24.6 2.9 %collective-permute-start.4 = (bf16[576,128]{1,0:T(8,128)(2,1)S(1)}, bf16[576,128]{1,0:T(8,128)(2,1)S(1)}, u32[]{:S(2)}, u32[]{:S(2)}) collective-permute-start(bf16[576,128]{1,0:T(8,128)(2,1)S(1)} %get-tuple-element.18), channel_id=1, source_target_pairs={{64,16},{65,17},{66,18},{67,19},{68,20},{69,21},{70,22},{71,23},{7... | collective-permute-start | bytes 442376 | tf_op jit(solution)/shard_map/ppermute | solution.py:210
  27.5 0.7 collective-permute-start.5
  28.2 1.6 %query_grads.1 = bf16[4,576,128]{2,1,0:T(8,128)(2,1)} custom-call(bf16[512,512]{1,0:T(8,128)(2,1)S(1)} %get-tuple-element.20.ds_ref, bf16[576,128]{1,0:T(8,128)(2,1)S(1)} %bitcast.26, bf16[576,128]{1,0:T(8,128)(2,1)S(1)} %collective-permute-done.px_ref, bf16[576,128]{1,0:T(8,128)(2,1)S(1)} %collective-permute-done.1.p2_ref, ...), custom_call_target="tpu_custom_call" | custom-call | flops 301989888 | bytes 2097152 | tf_op jit(solution)/shard_map/query_grads/pallas_call | solution.py:101
  29.8 7.2 %collective-permute-done.4.next_ref = bf16[576,128]{1,0:T(8,128)(2,1)S(1)} collective-permute-done((bf16[576,128]{1,0:T(8,128)(2,1)S(1)}, bf16[576,128]{1,0:T(8,128)(2,1)S(1)}, u32[]{:S(2)}, u32[]{:S(2)}) %collective-permute-start.4) | collective-permute-done | bytes 147488 | tf_op jit(solution)/shard_map/ppermute | solution.py:210
  37.0 0.0 collective-permute-done.5.over_ref
  37.0 0.1 total.1
  37.1 23.4 %all_to_all.10.came_ref = bf16[32,18,128]{2,1,0:T(8,128)(2,1)S(1)} all-to-all(bf16[32,18,128]{2,1,0:T(8,128)(2,1)S(1)} %total.1), channel_id=1, replica_groups=mesh['z'=8,'xh'=2,'core'=2,'xl'=4,'y'=8] {'xl','y'}, dimensions={0} | all-to-all | bytes 294912 | tf_op jit(solution)/shard_map/all_to_all | solution.py:218
  60.5 0.1 reduce.1
  60.6 14.9 %all_to_all.11.came_ref = bf16[32,18,128]{2,1,0:T(8,128)(2,1)S(1)} all-to-all(bf16[32,18,128]{2,1,0:T(8,128)(2,1)S(1)} %reduce.1), channel_id=1, replica_groups=mesh['z'=8,'xh'=2,'core'=2,'xl'=4,'y'=8] {'xl','y'}, dimensions={0} | all-to-all | bytes 294912 | tf_op jit(solution)/shard_map/all_to_all | solution.py:220
  75.5 0.7 finish.1
  (2 shorter events, 0.0 us)
Async XLA Ops:
  0.6 13.7 %collective-permute-start.1 = (bf16[576,128]{1,0:T(8,128)(2,1)}, bf16[576,128]{1,0:T(8,128)(2,1)S(1)}, u32[]{:S(2)}, u32[]{:S(2)}) collective-permute-start(bf16[576,128]{1,0:T(8,128)(2,1)} %bitcast.23), channel_id=1, source_target_pairs={{0,80},{1,81},{2,82},{3,83},{4,84},{5,85},{6,86},{7,87},{8,88},{9,... | collective-permute-start | bytes 442376 | tf_op jit(solution)/shard_map/ppermute | solution.py:194
  7.8 9.7 %collective-permute-start = (bf16[576,128]{1,0:T(8,128)(2,1)}, bf16[576,128]{1,0:T(8,128)(2,1)S(1)}, u32[]{:S(2)}, u32[]{:S(2)}) collective-permute-start(bf16[576,128]{1,0:T(8,128)(2,1)} %bitcast.24), channel_id=1, source_target_pairs={{0,32},{1,33},{2,34},{3,35},{4,36},{5,37},{6,38},{7,39},{8,40},{9,... | collective-permute-start | bytes 442376 | tf_op jit(solution)/shard_map/ppermute | solution.py:195
  9.7 1.2 %copy-start.2 = (bf16[128,4,512]{2,1,0:T(4,128)(2,1)S(1)}, bf16[128,4,512]{2,1,0:T(4,128)(2,1)}, u32[]{:S(2)}) copy-start(bf16[128,4,512]{2,1,0:T(4,128)(2,1)} %param.6) | copy-start | bytes 1572868
  11.5 1.1 %copy-start.1 = (bf16[128,4,576]{0,2,1:T(8,128)(2,1)S(1)}, bf16[128,4,576]{0,2,1:T(8,128)(2,1)}, u32[]{:S(2)}) copy-start(bf16[128,4,576]{0,2,1:T(8,128)(2,1)} %param.4) | copy-start | bytes 1769476
  12.9 4.5 %copy-start.3 = (s32[128]{0:T(128)S(1)}, s32[128]{0:T(128)}, u32[]{:S(2)}) copy-start(s32[128]{0:T(128)} %param.7) | copy-start | bytes 1540
  12.9 5.5 %copy-start = (bf16[128,576]{0,1:T(8,128)(2,1)S(1)}, bf16[128,576]{0,1:T(8,128)(2,1)}, u32[]{:S(2)}) copy-start(bf16[128,576]{0,1:T(8,128)(2,1)} %param.5) | copy-start | bytes 442372
  14.3 4.1 %collective-permute-start.2 = (bf16[576,128]{1,0:T(8,128)(2,1)S(1)}, bf16[576,128]{1,0:T(8,128)(2,1)S(1)}, u32[]{:S(2)}, u32[]{:S(2)}) collective-permute-start(bf16[576,128]{1,0:T(8,128)(2,1)S(1)} %collective-permute-done.1.p2_ref), channel_id=1, source_target_pairs={{0,32},{32,0},{1,33},{33,1},{2,34},{34,2},{3,35},{35,3},{4,36},{36... | collective-permute-start | bytes 442376 | tf_op jit(solution)/shard_map/ppermute | solution.py:196
  21.0 3.5 %collective-permute-start.3 = (bf16[2,576,128]{2,1,0:T(8,128)(2,1)S(1)}, bf16[2,576,128]{2,1,0:T(8,128)(2,1)S(1)}, u32[]{:S(2)}, u32[]{:S(2)}) collective-permute-start(bf16[2,576,128]{2,1,0:T(8,128)(2,1)S(1)} %get-tuple-element.15), channel_id=1, source_target_pairs={{0,32},{32,0},{1,33},{33,1},{2,34},{34,2},{3,35},{35,3},{4,36},{36... | collective-permute-start | bytes 884744 | tf_op jit(solution)/shard_map/ppermute | solution.py:205
  24.6 12.4 %collective-permute-start.4 = (bf16[576,128]{1,0:T(8,128)(2,1)S(1)}, bf16[576,128]{1,0:T(8,128)(2,1)S(1)}, u32[]{:S(2)}, u32[]{:S(2)}) collective-permute-start(bf16[576,128]{1,0:T(8,128)(2,1)S(1)} %get-tuple-element.18), channel_id=1, source_target_pairs={{64,16},{65,17},{66,18},{67,19},{68,20},{69,21},{70,22},{71,23},{7... | collective-permute-start | bytes 442376 | tf_op jit(solution)/shard_map/ppermute | solution.py:210
  27.5 9.5 %collective-permute-start.5 = (bf16[576,128]{1,0:T(8,128)(2,1)S(1)}, bf16[576,128]{1,0:T(8,128)(2,1)S(1)}, u32[]{:S(2)}, u32[]{:S(2)}) collective-permute-start(bf16[576,128]{1,0:T(8,128)(2,1)S(1)} %get-tuple-element.19), channel_id=1, source_target_pairs={{160,32},{161,33},{162,34},{163,35},{164,36},{165,37},{166,38},{16... | collective-permute-start | bytes 442376 | tf_op jit(solution)/shard_map/ppermute | solution.py:211

commit v5 on v4

--- a/solution.py
+++ b/solution.py
@@ -13,7 +13,6 @@
 ROWS = TOK * HEADS
 PART = 72
 SHARES = 32
-SHARE = KVW // SHARES
 SEQ = ("z", "xh", "core")
 HEAD = ("xl", "y")
 
@@ -112,7 +111,7 @@
     )(ds, own, px, p2, sw)
 
 
-def small_call(kernel, name, out_shape, count, scratch=()):
+def small_call(kernel, name, out_shape, count):
     outs = out_shape if isinstance(out_shape, tuple) else (out_shape,)
     specs = (whole,) * len(outs)
     return pl.pallas_call(
@@ -120,7 +119,6 @@
         out_shape=out_shape,
         in_specs=[scalars] + [whole] * count,
         out_specs=specs if isinstance(out_shape, tuple) else whole,
-        scratch_shapes=list(scratch),
         cost_estimate=pl.CostEstimate(flops=1 << 19, bytes_accessed=1 << 20, transcendentals=0),
         compiler_params=pltpu.CompilerParams(vmem_limit_bytes=8 << 20),
         name=name,
@@ -137,32 +135,28 @@
         over_ref[cols, :] = jnp.where(odd, far, jnp.zeros_like(far)).astype(jnp.bfloat16)
 
 
-def total_kernel(place, keep_ref, came_ref, next_ref, over_ref, out_ref, sum_ref):
+def total_kernel(place, keep_ref, came_ref, next_ref, over_ref, out_ref):
     even = lax.rem(place[0], 2) == 0
     for part in range(KVW // PART):
         cols = slice(part * PART, (part + 1) * PART)
         near = came_ref[0, cols, :].astype(jnp.float32)
         total = keep_ref[0, cols, :] + jnp.where(even, near, jnp.zeros_like(near))
         total = total + next_ref[cols, :].astype(jnp.float32)
-        sum_ref[cols, :] = total + over_ref[cols, :].astype(jnp.float32)
-    for share in range(SHARES):
-        rows = slice(SHARE * share, SHARE * (share + 1))
-        out_ref[share] = sum_ref[rows, :].astype(jnp.bfloat16)
+        out_ref[part] = (total + over_ref[cols, :].astype(jnp.float32)).astype(jnp.bfloat16)
 
 
 def reduce_kernel(place, came_ref, out_ref):
     total = came_ref[0].astype(jnp.float32)
-    for source in range(1, SHARES):
+    for source in range(1, came_ref.shape[0]):
         total = total + came_ref[source].astype(jnp.float32)
     total = total.astype(jnp.bfloat16)
-    for share in range(SHARES):
-        out_ref[share] = total
+    for copy in range(out_ref.shape[0]):
+        out_ref[copy] = total
 
 
 def finish_kernel(place, came_ref, out_ref):
-    for share in range(SHARES):
-        rows = slice(SHARE * share, SHARE * (share + 1))
-        out_ref[rows, :] = came_ref[share].astype(jnp.float32)
+    for part in range(KVW // PART):
+        out_ref[slice(part * PART, (part + 1) * PART), :] = came_ref[part].astype(jnp.float32)
 
 
 def routes(count):
@@ -192,19 +186,18 @@
 
     own = latent_kv.T
     p2 = lax.ppermute(own, everyone, halo)
-    px = lax.ppermute(own, everyone, mixed)
-    sw = lax.ppermute(p2, "core", swap)
-
     q = queries.transpose(1, 0, 2).reshape(ROWS, width)
     qt = queries.transpose(2, 1, 0).reshape(width, ROWS)
     g = grad_out.transpose(1, 0, 2).reshape(ROWS, LAT)
     gt = jnp.pad(grad_out.transpose(2, 1, 0).reshape(LAT, ROWS), ((0, width - LAT), (0, 0)))
     doc = doc_start.astype(jnp.float32).reshape(1, tokens)
+    after, q, qt, g, gt, doc = lax.optimization_barrier((own, q, qt, g, gt, doc))
+    px = lax.ppermute(after, everyone, mixed)
+    sw = lax.ppermute(p2, "core", swap)
 
     keep, send, ds = attention(place, doc, q, qt, g, gt, own, px, p2, sw)
     came = lax.ppermute(send, "core", swap)
     block = jax.ShapeDtypeStruct((width, tokens), jnp.bfloat16)
-    pieces = jax.ShapeDtypeStruct((SHARES, SHARE, tokens), jnp.bfloat16)
     to_next, to_over = small_call(join_kernel, "join", (block, block), 2)(place, keep, came)
     ds, to_next, to_over = lax.optimization_barrier((ds, to_next, to_over))
     to_next = lax.ppermute(to_next, everyone, back)
@@ -212,12 +205,16 @@
     query_grad = query_grads(ds, own, px, p2, sw)
     to_next, to_over, query_grad = lax.optimization_barrier((to_next, to_over, query_grad))
 
-    terms = small_call(
-        total_kernel, "total", pieces, 4, [pltpu.VMEM((width, tokens), jnp.float32)]
-    )(place, keep, came, to_next, to_over)
-    terms = lax.all_to_all(terms, HEAD, 0, 0, tiled=True)
-    terms = small_call(reduce_kernel, "reduce", pieces, 1)(place, terms)
-    grad = lax.all_to_all(terms, HEAD, 0, 0, tiled=True)
+    def pieces(count):
+        return jax.ShapeDtypeStruct((count, PART, tokens), jnp.bfloat16)
+
+    rows, lines = lax.axis_size("y"), lax.axis_size("xl")
+    terms = small_call(total_kernel, "total", pieces(rows), 4)(place, keep, came, to_next, to_over)
+    terms = lax.all_to_all(terms, "y", 0, 0, tiled=True)
+    terms = small_call(reduce_kernel, "reduce_rows", pieces(lines), 1)(place, terms)
+    terms = lax.all_to_all(terms, "xl", 0, 0, tiled=True)
+    terms = small_call(reduce_kernel, "reduce_lines", pieces(rows), 1)(place, terms)
+    grad = lax.all_to_all(terms, "y", 0, 0, tiled=True)
     out = jax.ShapeDtypeStruct((width, tokens), jnp.float32)
     grad = small_call(finish_kernel, "finish", out, 1)(place, grad)
     return query_grad.transpose(2, 0, 1), grad.T

time: 76.6 us -> 78.6 us (1.026)
  the two profiles are of different devices: /device:TPU:398 before, /device:TPU:394 now
where the time goes in v5:
time: 78.6 us; the launch traced here: 78.2 us
  blocking collectives  36.4 us (46%)
  starting transfers between devices  19.3 us (25%)
  waiting for transfers between devices  12.4 us (16%)
  Pallas kernels  5.12 us (7%)
  local copies, waits for them, and re-layouts  4.09 us (5%)
    all_to_all x1, blocking collectives, per_device(): terms = lax.all_to_all(terms, 'y', 0, 0, tiled=True)  17 us
    all_to_all x1, blocking collectives, per_device(): grad = lax.all_to_all(terms, 'y', 0, 0, tiled=True)  11.6 us
    ppermute x1, waiting for transfers between devices, per_device(): to_next = lax.ppermute(to_next, everyone, back)  10.3 us
    all_to_all x1, blocking collectives, per_device(): terms = lax.all_to_all(terms, 'xl', 0, 0, tiled=True)  7.79 us
    ppermute x1, starting transfers between devices, per_device(): p2 = lax.ppermute(own, everyone, halo)  7.24 us
    ppermute x1, starting transfers between devices, per_device(): sw = lax.ppermute(p2, 'core', swap)  4.4 us
    ppermute x1, starting transfers between devices, per_device(): to_next = lax.ppermute(to_next, everyone, back)  2.82 us
    pallas_call x1, Pallas kernels, attention(): pl.pallas_call(attention_kernel, out_shape=(jax.ShapeDtypeStruct((2, KVW,...  2.61 us
  transfers between devices with their start and end apart: 6, of which 4 were waited for; matrix products, arithmetic and copies ran while one was open for 3% of the time, Pallas kernels for 2%

profile of v5, /device:TPU:394, one launch (start us, length us, event | category | flops | bytes accessed | tf_op | source)
XLA Modules:
  0.0 78.2 jit_solution(6008009976727066275)
XLA Ops:
  0.6 7.2 %collective-permute-start.1 = (bf16[576,128]{1,0:T(8,128)(2,1)}, bf16[576,128]{1,0:T(8,128)(2,1)S(1)}, u32[]{:S(2)}, u32[]{:S(2)}) collective-permute-start(bf16[576,128]{1,0:T(8,128)(2,1)} %bitcast.23), channel_id=1, source_target_pairs={{0,80},{1,81},{2,82},{3,83},{4,84},{5,85},{6,86},{7,87},{8,88},{9,... | collective-permute-start | bytes 442376 | tf_op jit(solution)/shard_map/ppermute | solution.py:188
  7.9 0.0 copy-start.2
  7.9 1.2 %copy.8 = bf16[4,128,512]{2,1,0:T(8,128)(2,1)S(1)} copy(bf16[4,128,512]{2,0,1:T(4,128)(2,1)} %bitcast.28) | data formatting | bytes 1048576 | tf_op jit(solution)/shard_map/transpose | solution.py:191
  9.1 0.0 copy-done.2
  9.1 0.6 copy.9
  9.7 0.0 copy-start.1
  9.7 0.1 copy.14
  9.8 1.0 %copy-done.1 = bf16[128,4,576]{0,2,1:T(8,128)(2,1)S(1)} copy-done((bf16[128,4,576]{0,2,1:T(8,128)(2,1)S(1)}, bf16[128,4,576]{0,2,1:T(8,128)(2,1)}, u32[]{:S(2)}) %copy-start.1) | copy-done | bytes 589848
  10.7 0.1 copy_bitcast_fusion.qt_ref
  10.8 0.3 copy.6
  11.1 0.0 copy-start.3
  11.1 0.0 copy-start
  11.2 0.6 copy-done.3
  11.8 0.3 copy-done
  12.0 1.9 %collective-permute-start = (bf16[576,128]{1,0:T(8,128)(2,1)S(1)}, bf16[576,128]{1,0:T(8,128)(2,1)S(1)}, u32[]{:S(2)}, u32[]{:S(2)}) collective-permute-start(bf16[576,128]{1,0:T(8,128)(2,1)S(1)} %bitcast.24), channel_id=1, source_target_pairs={{0,32},{1,33},{2,34},{3,35},{4,36},{5,37},{6,38},{7,39},{8,40},{9,... | collective-permute-start | bytes 442376 | tf_op jit(solution)/shard_map/ppermute | solution.py:195
  14.0 0.0 collective-permute-done.1.p2_ref
  14.0 4.4 %collective-permute-start.2 = (bf16[576,128]{1,0:T(8,128)(2,1)S(1)}, bf16[576,128]{1,0:T(8,128)(2,1)S(1)}, u32[]{:S(2)}, u32[]{:S(2)}) collective-permute-start(bf16[576,128]{1,0:T(8,128)(2,1)S(1)} %collective-permute-done.1.p2_ref), channel_id=1, source_target_pairs={{0,32},{32,0},{1,33},{33,1},{2,34},{34,2},{3,35},{35,3},{4,36},{36... | collective-permute-start | bytes 442376 | tf_op jit(solution)/shard_map/ppermute | solution.py:196
  18.4 0.1 collective-permute-done.px_ref
  18.5 0.9 %collective-permute-done.2.sw_ref = bf16[576,128]{1,0:T(8,128)(2,1)S(1)} collective-permute-done((bf16[576,128]{1,0:T(8,128)(2,1)S(1)}, bf16[576,128]{1,0:T(8,128)(2,1)S(1)}, u32[]{:S(2)}, u32[]{:S(2)}) %collective-permute-start.2) | collective-permute-done | bytes 147488 | tf_op jit(solution)/shard_map/ppermute | solution.py:196
  19.4 2.6 %attention.1 = (f32[2,576,128]{2,1,0:T(8,128)S(1)}, bf16[2,576,128]{2,1,0:T(8,128)(2,1)S(1)}, bf16[512,512]{1,0:T(8,128)(2,1)S(1)}) custom-call(s32[1]{0:T(128)} %bitcast.place, f32[1,128]{1,0:T(1,128)S(1)} %convert_bitcast_fusion.doc_ref, bf16[512,576]{1,0:T(8,128)(2,1)S(1)} %bitcast.21, bf16[576,512]{1,0:T(8,128)(2,1)S(1)} %copy_bitcast_fusion.qt_ref, ...), custom_call_target="tpu_custom_call" | custom-call | flops 1207959552 | bytes 6291456 | tf_op jit(solution)/shard_map/attention/pallas_call | solution.py:66
  22.0 2.3 %collective-permute-start.3 = (bf16[2,576,128]{2,1,0:T(8,128)(2,1)S(1)}, bf16[2,576,128]{2,1,0:T(8,128)(2,1)S(1)}, u32[]{:S(2)}, u32[]{:S(2)}) collective-permute-start(bf16[2,576,128]{2,1,0:T(8,128)(2,1)S(1)} %get-tuple-element.27), channel_id=1, source_target_pairs={{0,32},{32,0},{1,33},{33,1},{2,34},{34,2},{3,35},{35,3},{4,36},{36... | collective-permute-start | bytes 884744 | tf_op jit(solution)/shard_map/ppermute | solution.py:199
  24.3 1.2 %collective-permute-done.3.came_ref = bf16[2,576,128]{2,1,0:T(8,128)(2,1)S(1)} collective-permute-done((bf16[2,576,128]{2,1,0:T(8,128)(2,1)S(1)}, bf16[2,576,128]{2,1,0:T(8,128)(2,1)S(1)}, u32[]{:S(2)}, u32[]{:S(2)}) %collective-permute-start.3) | collective-permute-done | bytes 294944 | tf_op jit(solution)/shard_map/ppermute | solution.py:199
  25.4 0.1 join.1
  25.5 2.8 %collective-permute-start.4 = (bf16[576,128]{1,0:T(8,128)(2,1)S(1)}, bf16[576,128]{1,0:T(8,128)(2,1)S(1)}, u32[]{:S(2)}, u32[]{:S(2)}) collective-permute-start(bf16[576,128]{1,0:T(8,128)(2,1)S(1)} %get-tuple-element.30), channel_id=1, source_target_pairs={{64,16},{65,17},{66,18},{67,19},{68,20},{69,21},{70,22},{71,23},{7... | collective-permute-start | bytes 442376 | tf_op jit(solution)/shard_map/ppermute | solution.py:203
  28.3 0.7 collective-permute-start.5
  29.0 1.6 %query_grads.1 = bf16[4,576,128]{2,1,0:T(8,128)(2,1)} custom-call(bf16[512,512]{1,0:T(8,128)(2,1)S(1)} %get-tuple-element.32.ds_ref, bf16[576,128]{1,0:T(8,128)(2,1)S(1)} %bitcast.26, bf16[576,128]{1,0:T(8,128)(2,1)S(1)} %collective-permute-done.px_ref, bf16[576,128]{1,0:T(8,128)(2,1)S(1)} %collective-permute-done.1.p2_ref, ...), custom_call_target="tpu_custom_call" | custom-call | flops 301989888 | bytes 2097152 | tf_op jit(solution)/shard_map/query_grads/pallas_call | solution.py:100
  30.6 10.3 %collective-permute-done.4.next_ref = bf16[576,128]{1,0:T(8,128)(2,1)S(1)} collective-permute-done((bf16[576,128]{1,0:T(8,128)(2,1)S(1)}, bf16[576,128]{1,0:T(8,128)(2,1)S(1)}, u32[]{:S(2)}, u32[]{:S(2)}) %collective-permute-start.4) | collective-permute-done | bytes 147488 | tf_op jit(solution)/shard_map/ppermute | solution.py:203
  40.9 0.0 collective-permute-done.5.over_ref
  40.9 0.1 total.1
  41.0 17.0 %all_to_all.15.came_ref = bf16[8,72,128]{2,1,0:T(8,128)(2,1)S(1)} all-to-all(bf16[8,72,128]{2,1,0:T(8,128)(2,1)S(1)} %total.1), channel_id=1, replica_groups=mesh['z'=8,'xh'=2,'core'=2,'xl'=4,'y'=8] {'y'}, dimensions={0} | all-to-all | bytes 294912 | tf_op jit(solution)/shard_map/all_to_all | solution.py:213
  58.0 7.8 %all_to_all.16.came_ref = bf16[4,72,128]{2,1,0:T(8,128)(2,1)S(1)} all-to-all(bf16[4,72,128]{2,1,0:T(8,128)(2,1)S(1)} %reduce_rows.1), channel_id=1, replica_groups=mesh['z'=8,'xh'=2,'core'=2,'xl'=4,'y'=8] {'xl'}, dimensions={0} | all-to-all | bytes 147456 | tf_op jit(solution)/shard_map/all_to_all | solution.py:215
  65.8 11.6 %all_to_all.17.came_ref = bf16[8,72,128]{2,1,0:T(8,128)(2,1)S(1)} all-to-all(bf16[8,72,128]{2,1,0:T(8,128)(2,1)S(1)} %reduce_lines.1), channel_id=1, replica_groups=mesh['z'=8,'xh'=2,'core'=2,'xl'=4,'y'=8] {'y'}, dimensions={0} | all-to-all | bytes 294912 | tf_op jit(solution)/shard_map/all_to_all | solution.py:217
  77.4 0.7 finish.1
  (4 shorter events, 0.1 us)
Async XLA Ops:
  0.6 13.3 %collective-permute-start.1 = (bf16[576,128]{1,0:T(8,128)(2,1)}, bf16[576,128]{1,0:T(8,128)(2,1)S(1)}, u32[]{:S(2)}, u32[]{:S(2)}) collective-permute-start(bf16[576,128]{1,0:T(8,128)(2,1)} %bitcast.23), channel_id=1, source_target_pairs={{0,80},{1,81},{2,82},{3,83},{4,84},{5,85},{6,86},{7,87},{8,88},{9,... | collective-permute-start | bytes 442376 | tf_op jit(solution)/shard_map/ppermute | solution.py:188
  7.9 1.2 %copy-start.2 = (bf16[128,4,512]{2,1,0:T(4,128)(2,1)S(1)}, bf16[128,4,512]{2,1,0:T(4,128)(2,1)}, u32[]{:S(2)}) copy-start(bf16[128,4,512]{2,1,0:T(4,128)(2,1)} %param.6) | copy-start | bytes 1572868
  9.7 1.1 %copy-start.1 = (bf16[128,4,576]{0,2,1:T(8,128)(2,1)S(1)}, bf16[128,4,576]{0,2,1:T(8,128)(2,1)}, u32[]{:S(2)}) copy-start(bf16[128,4,576]{0,2,1:T(8,128)(2,1)} %param.4) | copy-start | bytes 1769476
  11.1 0.7 copy-start.3
  11.1 0.9 %copy-start = (bf16[128,576]{0,1:T(8,128)(2,1)S(1)}, bf16[128,576]{0,1:T(8,128)(2,1)}, u32[]{:S(2)}) copy-start(bf16[128,576]{0,1:T(8,128)(2,1)} %param.5) | copy-start | bytes 442372
  12.0 6.5 %collective-permute-start = (bf16[576,128]{1,0:T(8,128)(2,1)S(1)}, bf16[576,128]{1,0:T(8,128)(2,1)S(1)}, u32[]{:S(2)}, u32[]{:S(2)}) collective-permute-start(bf16[576,128]{1,0:T(8,128)(2,1)S(1)} %bitcast.24), channel_id=1, source_target_pairs={{0,32},{1,33},{2,34},{3,35},{4,36},{5,37},{6,38},{7,39},{8,40},{9,... | collective-permute-start | bytes 442376 | tf_op jit(solution)/shard_map/ppermute | solution.py:195
  14.0 5.4 %collective-permute-start.2 = (bf16[576,128]{1,0:T(8,128)(2,1)S(1)}, bf16[576,128]{1,0:T(8,128)(2,1)S(1)}, u32[]{:S(2)}, u32[]{:S(2)}) collective-permute-start(bf16[576,128]{1,0:T(8,128)(2,1)S(1)} %collective-permute-done.1.p2_ref), channel_id=1, source_target_pairs={{0,32},{32,0},{1,33},{33,1},{2,34},{34,2},{3,35},{35,3},{4,36},{36... | collective-permute-start | bytes 442376 | tf_op jit(solution)/shard_map/ppermute | solution.py:196
  22.0 3.5 %collective-permute-start.3 = (bf16[2,576,128]{2,1,0:T(8,128)(2,1)S(1)}, bf16[2,576,128]{2,1,0:T(8,128)(2,1)S(1)}, u32[]{:S(2)}, u32[]{:S(2)}) collective-permute-start(bf16[2,576,128]{2,1,0:T(8,128)(2,1)S(1)} %get-tuple-element.27), channel_id=1, source_target_pairs={{0,32},{32,0},{1,33},{33,1},{2,34},{34,2},{3,35},{35,3},{4,36},{36... | collective-permute-start | bytes 884744 | tf_op jit(solution)/shard_map/ppermute | solution.py:199
  25.5 15.4 %collective-permute-start.4 = (bf16[576,128]{1,0:T(8,128)(2,1)S(1)}, bf16[576,128]{1,0:T(8,128)(2,1)S(1)}, u32[]{:S(2)}, u32[]{:S(2)}) collective-permute-start(bf16[576,128]{1,0:T(8,128)(2,1)S(1)} %get-tuple-element.30), channel_id=1, source_target_pairs={{64,16},{65,17},{66,18},{67,19},{68,20},{69,21},{70,22},{71,23},{7... | collective-permute-start | bytes 442376 | tf_op jit(solution)/shard_map/ppermute | solution.py:203
  28.3 12.5 %collective-permute-start.5 = (bf16[576,128]{1,0:T(8,128)(2,1)S(1)}, bf16[576,128]{1,0:T(8,128)(2,1)S(1)}, u32[]{:S(2)}, u32[]{:S(2)}) collective-permute-start(bf16[576,128]{1,0:T(8,128)(2,1)S(1)} %get-tuple-element.31), channel_id=1, source_target_pairs={{160,32},{161,33},{162,34},{163,35},{164,36},{165,37},{166,38},{16... | collective-permute-start | bytes 442376 | tf_op jit(solution)/shard_map/ppermute | solution.py:204

commit v6 on v4

--- a/solution.py
+++ b/solution.py
@@ -13,7 +13,7 @@
 ROWS = TOK * HEADS
 PART = 72
 SHARES = 32
-SHARE = KVW // SHARES
+WIDE = KVW // (2 * SHARES)
 SEQ = ("z", "xh", "core")
 HEAD = ("xl", "y")
 
@@ -145,9 +145,10 @@
         total = keep_ref[0, cols, :] + jnp.where(even, near, jnp.zeros_like(near))
         total = total + next_ref[cols, :].astype(jnp.float32)
         sum_ref[cols, :] = total + over_ref[cols, :].astype(jnp.float32)
-    for share in range(SHARES):
-        rows = slice(SHARE * share, SHARE * (share + 1))
-        out_ref[share] = sum_ref[rows, :].astype(jnp.bfloat16)
+    for lanes in range(WIDE):
+        cols = slice(lanes * TOK, (lanes + 1) * TOK)
+        picked = sum_ref[pl.ds(lanes, 2 * SHARES, stride=WIDE), :]
+        out_ref[:, cols] = picked.astype(jnp.bfloat16)
 
 
 def reduce_kernel(place, came_ref, out_ref):
@@ -160,9 +161,9 @@
 
 
 def finish_kernel(place, came_ref, out_ref):
-    for share in range(SHARES):
-        rows = slice(SHARE * share, SHARE * (share + 1))
-        out_ref[rows, :] = came_ref[share].astype(jnp.float32)
+    for lanes in range(WIDE):
+        cols = slice(lanes * TOK, (lanes + 1) * TOK)
+        out_ref[pl.ds(lanes, 2 * SHARES, stride=WIDE), :] = came_ref[:, cols].astype(jnp.float32)
 
 
 def routes(count):
@@ -204,7 +205,8 @@
     keep, send, ds = attention(place, doc, q, qt, g, gt, own, px, p2, sw)
     came = lax.ppermute(send, "core", swap)
     block = jax.ShapeDtypeStruct((width, tokens), jnp.bfloat16)
-    pieces = jax.ShapeDtypeStruct((SHARES, SHARE, tokens), jnp.bfloat16)
+    flat = jax.ShapeDtypeStruct((2 * SHARES, WIDE * tokens), jnp.bfloat16)
+    pieces = jax.ShapeDtypeStruct((SHARES, 2, WIDE * tokens), jnp.bfloat16)
     to_next, to_over = small_call(join_kernel, "join", (block, block), 2)(place, keep, came)
     ds, to_next, to_over = lax.optimization_barrier((ds, to_next, to_over))
     to_next = lax.ppermute(to_next, everyone, back)
@@ -213,13 +215,13 @@
     to_next, to_over, query_grad = lax.optimization_barrier((to_next, to_over, query_grad))
 
     terms = small_call(
-        total_kernel, "total", pieces, 4, [pltpu.VMEM((width, tokens), jnp.float32)]
+        total_kernel, "total", flat, 4, [pltpu.VMEM((width, tokens), jnp.float32)]
     )(place, keep, came, to_next, to_over)
-    terms = lax.all_to_all(terms, HEAD, 0, 0, tiled=True)
+    terms = lax.all_to_all(terms.reshape(pieces.shape), HEAD, 0, 0, tiled=True)
     terms = small_call(reduce_kernel, "reduce", pieces, 1)(place, terms)
     grad = lax.all_to_all(terms, HEAD, 0, 0, tiled=True)
     out = jax.ShapeDtypeStruct((width, tokens), jnp.float32)
-    grad = small_call(finish_kernel, "finish", out, 1)(place, grad)
+    grad = small_call(finish_kernel, "finish", out, 1)(place, grad.reshape(flat.shape))
     return query_grad.transpose(2, 0, 1), grad.T
 
 

time: 76.6 us -> 74.7 us (0.975)
  blocking collectives: 38.4 us -> 36.3 us
    all_to_all x1, blocking collectives: 14.9 us -> 13.9 us  [per_device(): grad = lax.all_to_all(terms, HEAD, 0, 0, tiled=True)]
    all_to_all x1, blocking collectives: 23.4 us -> 22.4 us  [per_device(): terms = lax.all_to_all(terms.reshape(pieces.shape), HEAD, 0, 0, tiled=True)]
where the time goes in v6:
time: 74.7 us; the launch traced here: 74.3 us
  blocking collectives  36.3 us (49%)
  starting transfers between devices  18.1 us (24%)
  waiting for transfers between devices  10.6 us (14%)
  Pallas kernels  5.16 us (7%)
  local copies, waits for them, and re-layouts  3.36 us (4%)
  between operations  0.82 us (1%)
    all_to_all x1, blocking collectives, per_device(): terms = lax.all_to_all(terms.reshape(pieces.shape), HEAD, 0, 0, tiled=True)  22.4 us
    all_to_all x1, blocking collectives, per_device(): grad = lax.all_to_all(terms, HEAD, 0, 0, tiled=True)  13.9 us
    ppermute x1, waiting for transfers between devices, per_device(): to_next = lax.ppermute(to_next, everyone, back)  7.22 us
    ppermute x1, starting transfers between devices, per_device(): p2 = lax.ppermute(own, everyone, halo)  7.13 us
    ppermute x1, starting transfers between devices, per_device(): sw = lax.ppermute(p2, 'core', swap)  3.14 us
    ppermute x1, starting transfers between devices, per_device(): to_next = lax.ppermute(to_next, everyone, back)  2.93 us
    pallas_call x1, Pallas kernels, attention(): pl.pallas_call(attention_kernel, out_shape=(jax.ShapeDtypeStruct((2, KVW,...  2.6 us
    ppermute x1, starting transfers between devices, per_device(): came = lax.ppermute(send, 'core', swap)  2.27 us
  transfers between devices with their start and end apart: 6, of which 4 were waited for; matrix products, arithmetic and copies ran while one was open for 3% of the time, Pallas kernels for 2%

profile of v6, /device:TPU:398, one launch (start us, length us, event | category | flops | bytes accessed | tf_op | source)
XLA Modules:
  0.0 74.3 jit_solution(8047204473524735454)
XLA Ops:
  0.6 7.1 %collective-permute-start.1 = (bf16[576,128]{1,0:T(8,128)(2,1)}, bf16[576,128]{1,0:T(8,128)(2,1)S(1)}, u32[]{:S(2)}, u32[]{:S(2)}) collective-permute-start(bf16[576,128]{1,0:T(8,128)(2,1)} %bitcast.23), channel_id=1, source_target_pairs={{0,80},{1,81},{2,82},{3,83},{4,84},{5,85},{6,86},{7,87},{8,88},{9,... | collective-permute-start | bytes 442376 | tf_op jit(solution)/shard_map/ppermute | solution.py:195
  7.8 1.9 %collective-permute-start = (bf16[576,128]{1,0:T(8,128)(2,1)}, bf16[576,128]{1,0:T(8,128)(2,1)S(1)}, u32[]{:S(2)}, u32[]{:S(2)}) collective-permute-start(bf16[576,128]{1,0:T(8,128)(2,1)} %bitcast.24), channel_id=1, source_target_pairs={{0,32},{1,33},{2,34},{3,35},{4,36},{5,37},{6,38},{7,39},{8,40},{9,... | collective-permute-start | bytes 442376 | tf_op jit(solution)/shard_map/ppermute | solution.py:196
  9.7 0.0 copy-start.2
  9.7 1.2 %copy.8 = bf16[4,128,512]{2,1,0:T(8,128)(2,1)S(1)} copy(bf16[4,128,512]{2,0,1:T(4,128)(2,1)} %bitcast.28) | data formatting | bytes 1048576 | tf_op jit(solution)/shard_map/transpose | solution.py:201
  10.9 0.0 copy-done.2
  10.9 0.6 copy.9
  11.5 0.0 copy-start.1
  11.5 0.1 copy.14
  11.6 1.0 %copy-done.1 = bf16[128,4,576]{0,2,1:T(8,128)(2,1)S(1)} copy-done((bf16[128,4,576]{0,2,1:T(8,128)(2,1)S(1)}, bf16[128,4,576]{0,2,1:T(8,128)(2,1)}, u32[]{:S(2)}) %copy-start.1) | copy-done | bytes 589848
  12.6 0.3 copy.6
  12.9 0.0 copy-start.3
  12.9 0.0 copy-start
  13.0 0.1 copy_bitcast_fusion.qt_ref
  13.0 1.3 %collective-permute-done.1.p2_ref = bf16[576,128]{1,0:T(8,128)(2,1)S(1)} collective-permute-done((bf16[576,128]{1,0:T(8,128)(2,1)}, bf16[576,128]{1,0:T(8,128)(2,1)S(1)}, u32[]{:S(2)}, u32[]{:S(2)}) %collective-permute-start.1) | collective-permute-done | bytes 147488 | tf_op jit(solution)/shard_map/ppermute | solution.py:195
  14.3 3.1 %collective-permute-start.2 = (bf16[576,128]{1,0:T(8,128)(2,1)S(1)}, bf16[576,128]{1,0:T(8,128)(2,1)S(1)}, u32[]{:S(2)}, u32[]{:S(2)}) collective-permute-start(bf16[576,128]{1,0:T(8,128)(2,1)S(1)} %collective-permute-done.1.p2_ref), channel_id=1, source_target_pairs={{0,32},{32,0},{1,33},{33,1},{2,34},{34,2},{3,35},{35,3},{4,36},{36... | collective-permute-start | bytes 442376 | tf_op jit(solution)/shard_map/ppermute | solution.py:197
  17.4 0.0 copy-done.3
  17.5 0.0 collective-permute-done.px_ref
  17.5 1.0 %collective-permute-done.2.sw_ref = bf16[576,128]{1,0:T(8,128)(2,1)S(1)} collective-permute-done((bf16[576,128]{1,0:T(8,128)(2,1)S(1)}, bf16[576,128]{1,0:T(8,128)(2,1)S(1)}, u32[]{:S(2)}, u32[]{:S(2)}) %collective-permute-start.2) | collective-permute-done | bytes 147488 | tf_op jit(solution)/shard_map/ppermute | solution.py:197
  18.4 0.0 copy-done
  18.4 2.6 %attention.1 = (f32[2,576,128]{2,1,0:T(8,128)S(1)}, bf16[2,576,128]{2,1,0:T(8,128)(2,1)S(1)}, bf16[512,512]{1,0:T(8,128)(2,1)S(1)}) custom-call(s32[1]{0:T(128)} %bitcast.place, f32[1,128]{1,0:T(1,128)S(1)} %convert_bitcast_fusion.doc_ref, bf16[512,576]{1,0:T(8,128)(2,1)S(1)} %bitcast.21, bf16[576,512]{1,0:T(8,128)(2,1)S(1)} %copy_bitcast_fusion.qt_ref, ...), custom_call_target="tpu_custom_call" | custom-call | flops 1207959552 | bytes 6291456 | tf_op jit(solution)/shard_map/attention/pallas_call | solution.py:67
  21.0 2.3 %collective-permute-start.3 = (bf16[2,576,128]{2,1,0:T(8,128)(2,1)S(1)}, bf16[2,576,128]{2,1,0:T(8,128)(2,1)S(1)}, u32[]{:S(2)}, u32[]{:S(2)}) collective-permute-start(bf16[2,576,128]{2,1,0:T(8,128)(2,1)S(1)} %get-tuple-element.15), channel_id=1, source_target_pairs={{0,32},{32,0},{1,33},{33,1},{2,34},{34,2},{3,35},{35,3},{4,36},{36... | collective-permute-start | bytes 884744 | tf_op jit(solution)/shard_map/ppermute | solution.py:206
  23.3 1.2 %collective-permute-done.3.came_ref = bf16[2,576,128]{2,1,0:T(8,128)(2,1)S(1)} collective-permute-done((bf16[2,576,128]{2,1,0:T(8,128)(2,1)S(1)}, bf16[2,576,128]{2,1,0:T(8,128)(2,1)S(1)}, u32[]{:S(2)}, u32[]{:S(2)}) %collective-permute-start.3) | collective-permute-done | bytes 294944 | tf_op jit(solution)/shard_map/ppermute | solution.py:206
  24.5 0.1 join.1
  24.6 2.9 %collective-permute-start.4 = (bf16[576,128]{1,0:T(8,128)(2,1)S(1)}, bf16[576,128]{1,0:T(8,128)(2,1)S(1)}, u32[]{:S(2)}, u32[]{:S(2)}) collective-permute-start(bf16[576,128]{1,0:T(8,128)(2,1)S(1)} %get-tuple-element.18), channel_id=1, source_target_pairs={{64,16},{65,17},{66,18},{67,19},{68,20},{69,21},{70,22},{71,23},{7... | collective-permute-start | bytes 442376 | tf_op jit(solution)/shard_map/ppermute | solution.py:212
  27.5 0.7 collective-permute-start.5
  28.2 1.6 %query_grads.1 = bf16[4,576,128]{2,1,0:T(8,128)(2,1)} custom-call(bf16[512,512]{1,0:T(8,128)(2,1)S(1)} %get-tuple-element.20.ds_ref, bf16[576,128]{1,0:T(8,128)(2,1)S(1)} %bitcast.26, bf16[576,128]{1,0:T(8,128)(2,1)S(1)} %collective-permute-done.px_ref, bf16[576,128]{1,0:T(8,128)(2,1)S(1)} %collective-permute-done.1.p2_ref, ...), custom_call_target="tpu_custom_call" | custom-call | flops 301989888 | bytes 2097152 | tf_op jit(solution)/shard_map/query_grads/pallas_call | solution.py:101
  29.8 7.2 %collective-permute-done.4.next_ref = bf16[576,128]{1,0:T(8,128)(2,1)S(1)} collective-permute-done((bf16[576,128]{1,0:T(8,128)(2,1)S(1)}, bf16[576,128]{1,0:T(8,128)(2,1)S(1)}, u32[]{:S(2)}, u32[]{:S(2)}) %collective-permute-start.4) | collective-permute-done | bytes 147488 | tf_op jit(solution)/shard_map/ppermute | solution.py:212
  37.0 0.0 collective-permute-done.5.over_ref
  37.0 0.1 total.1
  37.1 0.1 reshape.34
  37.2 22.4 %all_to_all.10.came_ref = bf16[32,2,1152]{2,1,0:T(2,128)(2,1)S(1)} all-to-all(bf16[32,2,1152]{2,1,0:T(2,128)(2,1)S(1)} %reshape.34), channel_id=1, replica_groups=mesh['z'=8,'xh'=2,'core'=2,'xl'=4,'y'=8] {'xl','y'}, dimensions={0} | all-to-all | bytes 294912 | tf_op jit(solution)/shard_map/all_to_all | solution.py:220
  59.6 0.1 reduce.1
  59.7 13.9 %all_to_all.11 = bf16[32,2,1152]{2,1,0:T(2,128)(2,1)S(1)} all-to-all(bf16[32,2,1152]{2,1,0:T(2,128)(2,1)S(1)} %reduce.1), channel_id=1, replica_groups=mesh['z'=8,'xh'=2,'core'=2,'xl'=4,'y'=8] {'xl','y'}, dimensions={0} | all-to-all | bytes 294912 | tf_op jit(solution)/shard_map/all_to_all | solution.py:222
  73.5 0.1 reshape.35.came_ref
  73.6 0.7 finish.1
  (2 shorter events, 0.0 us)
Async XLA Ops:
  0.6 13.7 %collective-permute-start.1 = (bf16[576,128]{1,0:T(8,128)(2,1)}, bf16[576,128]{1,0:T(8,128)(2,1)S(1)}, u32[]{:S(2)}, u32[]{:S(2)}) collective-permute-start(bf16[576,128]{1,0:T(8,128)(2,1)} %bitcast.23), channel_id=1, source_target_pairs={{0,80},{1,81},{2,82},{3,83},{4,84},{5,85},{6,86},{7,87},{8,88},{9,... | collective-permute-start | bytes 442376 | tf_op jit(solution)/shard_map/ppermute | solution.py:195
  7.8 9.7 %collective-permute-start = (bf16[576,128]{1,0:T(8,128)(2,1)}, bf16[576,128]{1,0:T(8,128)(2,1)S(1)}, u32[]{:S(2)}, u32[]{:S(2)}) collective-permute-start(bf16[576,128]{1,0:T(8,128)(2,1)} %bitcast.24), channel_id=1, source_target_pairs={{0,32},{1,33},{2,34},{3,35},{4,36},{5,37},{6,38},{7,39},{8,40},{9,... | collective-permute-start | bytes 442376 | tf_op jit(solution)/shard_map/ppermute | solution.py:196
  9.7 1.2 %copy-start.2 = (bf16[128,4,512]{2,1,0:T(4,128)(2,1)S(1)}, bf16[128,4,512]{2,1,0:T(4,128)(2,1)}, u32[]{:S(2)}) copy-start(bf16[128,4,512]{2,1,0:T(4,128)(2,1)} %param.6) | copy-start | bytes 1572868
  11.5 1.1 %copy-start.1 = (bf16[128,4,576]{0,2,1:T(8,128)(2,1)S(1)}, bf16[128,4,576]{0,2,1:T(8,128)(2,1)}, u32[]{:S(2)}) copy-start(bf16[128,4,576]{0,2,1:T(8,128)(2,1)} %param.4) | copy-start | bytes 1769476
  12.9 4.5 %copy-start.3 = (s32[128]{0:T(128)S(1)}, s32[128]{0:T(128)}, u32[]{:S(2)}) copy-start(s32[128]{0:T(128)} %param.7) | copy-start | bytes 1540
  12.9 5.5 %copy-start = (bf16[128,576]{0,1:T(8,128)(2,1)S(1)}, bf16[128,576]{0,1:T(8,128)(2,1)}, u32[]{:S(2)}) copy-start(bf16[128,576]{0,1:T(8,128)(2,1)} %param.5) | copy-start | bytes 442372
  14.3 4.1 %collective-permute-start.2 = (bf16[576,128]{1,0:T(8,128)(2,1)S(1)}, bf16[576,128]{1,0:T(8,128)(2,1)S(1)}, u32[]{:S(2)}, u32[]{:S(2)}) collective-permute-start(bf16[576,128]{1,0:T(8,128)(2,1)S(1)} %collective-permute-done.1.p2_ref), channel_id=1, source_target_pairs={{0,32},{32,0},{1,33},{33,1},{2,34},{34,2},{3,35},{35,3},{4,36},{36... | collective-permute-start | bytes 442376 | tf_op jit(solution)/shard_map/ppermute | solution.py:197
  21.0 3.5 %collective-permute-start.3 = (bf16[2,576,128]{2,1,0:T(8,128)(2,1)S(1)}, bf16[2,576,128]{2,1,0:T(8,128)(2,1)S(1)}, u32[]{:S(2)}, u32[]{:S(2)}) collective-permute-start(bf16[2,576,128]{2,1,0:T(8,128)(2,1)S(1)} %get-tuple-element.15), channel_id=1, source_target_pairs={{0,32},{32,0},{1,33},{33,1},{2,34},{34,2},{3,35},{35,3},{4,36},{36... | collective-permute-start | bytes 884744 | tf_op jit(solution)/shard_map/ppermute | solution.py:206
  24.6 12.4 %collective-permute-start.4 = (bf16[576,128]{1,0:T(8,128)(2,1)S(1)}, bf16[576,128]{1,0:T(8,128)(2,1)S(1)}, u32[]{:S(2)}, u32[]{:S(2)}) collective-permute-start(bf16[576,128]{1,0:T(8,128)(2,1)S(1)} %get-tuple-element.18), channel_id=1, source_target_pairs={{64,16},{65,17},{66,18},{67,19},{68,20},{69,21},{70,22},{71,23},{7... | collective-permute-start | bytes 442376 | tf_op jit(solution)/shard_map/ppermute | solution.py:212
  27.5 9.5 %collective-permute-start.5 = (bf16[576,128]{1,0:T(8,128)(2,1)S(1)}, bf16[576,128]{1,0:T(8,128)(2,1)S(1)}, u32[]{:S(2)}, u32[]{:S(2)}) collective-permute-start(bf16[576,128]{1,0:T(8,128)(2,1)S(1)} %get-tuple-element.19), channel_id=1, source_target_pairs={{160,32},{161,33},{162,34},{163,35},{164,36},{165,37},{166,38},{16... | collective-permute-start | bytes 442376 | tf_op jit(solution)/shard_map/ppermute | solution.py:213

commit v7 on v6

--- a/solution.py
+++ b/solution.py
@@ -27,67 +27,76 @@
     return jnp.dot(a, b, preferred_element_type=jnp.float32)
 
 
-def attention_kernel(
-    place, doc_ref, q_ref, qt_ref, g_ref, gt_ref, own_ref, px_ref, p2_ref, sw_ref,
-    keep_ref, send_ref, ds_ref, kv_ref, bias_ref, p_ref,
-):
+def load_pair(place, doc_ref, backs, blocks, kv_ref, bias_ref):
     seq = place[0]
-    core = lax.rem(seq, 2)
-    for slot, ref in enumerate((own_ref, px_ref, p2_ref, sw_ref)):
-        kv_ref[:, slot * TOK : (slot + 1) * TOK] = ref[...]
     first = jnp.broadcast_to(doc_ref[...], (TOK, TOK)).T
     row = lax.broadcasted_iota(jnp.int32, (TOK, TOK), 0)
     lane = lax.broadcasted_iota(jnp.int32, (TOK, TOK), 1)
-    for slot, back in enumerate((0, 3 - 2 * core, 2, 1 + 2 * core)):
+    for slot, (back, ref) in enumerate(zip(backs, blocks)):
+        cols = slice(slot * TOK, (slot + 1) * TOK)
+        kv_ref[:, cols] = ref[...]
         key = lane + (seq - back) * TOK
         seen = (key <= row + seq * TOK) & (key.astype(jnp.float32) >= first)
-        bias_ref[:, slot * TOK : (slot + 1) * TOK] = jnp.where(seen, 0.0, lowest)
+        bias_ref[:, cols] = jnp.where(seen, 0.0, lowest)
+
+
+def near_kernel(
+    place, doc_ref, q_ref, g_ref, own_ref, px_ref, score_ref, grad_ref, kv_ref, bias_ref
+):
+    core = lax.rem(place[0], 2)
+    load_pair(place, doc_ref, (0, 3 - 2 * core), (own_ref, px_ref), kv_ref, bias_ref)
     for head in range(HEADS):
         rows = slice(head * TOK, (head + 1) * TOK)
-        scores = f32_dot(q_ref[rows, :], kv_ref[...]) * softmax_scale + bias_ref[...]
-        grad_probs = f32_dot(g_ref[rows, :], kv_ref[:LAT, :])
-        top = jnp.max(scores, axis=1, keepdims=True)
-        exps = jnp.exp(scores - top)
-        inverse = 1.0 / jnp.sum(exps, axis=1, keepdims=True)
-        delta = jnp.sum(exps * grad_probs, axis=1, keepdims=True) * inverse
-        probs = exps * inverse
-        p_ref[rows, :] = probs.astype(jnp.bfloat16)
-        ds_ref[rows, :] = (probs * (grad_probs - delta)).astype(jnp.bfloat16)
-    for part in range(KVW // PART):
-        cols = slice(part * PART, (part + 1) * PART)
-        term = f32_dot(qt_ref[cols, :], ds_ref[...]) * softmax_scale
-        term = term + f32_dot(gt_ref[cols, :], p_ref[...])
-        keep_ref[0, cols, :] = term[:, 0 * TOK : 1 * TOK]
-        send_ref[0, cols, :] = term[:, 1 * TOK : 2 * TOK].astype(jnp.bfloat16)
-        keep_ref[1, cols, :] = term[:, 2 * TOK : 3 * TOK]
-        send_ref[1, cols, :] = term[:, 3 * TOK : 4 * TOK].astype(jnp.bfloat16)
-
-
-def attention(place, doc, q, qt, g, gt, own, px, p2, sw):
-    return pl.pallas_call(
-        attention_kernel,
-        out_shape=(
-            jax.ShapeDtypeStruct((2, KVW, TOK), jnp.float32),
-            jax.ShapeDtypeStruct((2, KVW, TOK), jnp.bfloat16),
-            jax.ShapeDtypeStruct((ROWS, 4 * TOK), jnp.bfloat16),
-        ),
-        in_specs=[scalars] + [whole] * 9,
-        out_specs=(whole, whole, whole),
-        scratch_shapes=[
-            pltpu.VMEM((KVW, 4 * TOK), jnp.bfloat16),
-            pltpu.VMEM((TOK, 4 * TOK), jnp.float32),
-            pltpu.VMEM((ROWS, 4 * TOK), jnp.bfloat16),
-        ],
-        cost_estimate=pl.CostEstimate(
-            flops=4 * 2 * ROWS * 4 * TOK * KVW, bytes_accessed=6 << 20, transcendentals=ROWS * 4 * TOK
-        ),
-        compiler_params=pltpu.CompilerParams(vmem_limit_bytes=24 << 20),
-        name="attention",
-    )(place, doc, q, qt, g, gt, own, px, p2, sw)
+        score_ref[rows, :] = f32_dot(q_ref[rows, :], kv_ref[...]) * softmax_scale + bias_ref[...]
+        grad_ref[rows, :] = f32_dot(g_ref[rows, :], kv_ref[:LAT, :])
+
+
+def add_terms(qt_ref, gt_ref, ds_ref, p_ref, part, lanes):
+    cols = slice(part * PART, (part + 1) * PART)
+    term = f32_dot(qt_ref[cols, :], ds_ref[:, lanes]) * softmax_scale
+    return cols, term + f32_dot(gt_ref[cols, :], p_ref[:, lanes])
+
+
+def attention_kernel(
+    place, doc_ref, q_ref, qt_ref, g_ref, gt_ref, score_ref, grad_ref, p2_ref, sw_ref,
+    send_ref, p_ref, ds_ref, kv_ref, bias_ref,
+):
+    core = lax.rem(place[0], 2)
+    load_pair(place, doc_ref, (2, 1 + 2 * core), (p2_ref, sw_ref), kv_ref, bias_ref)
+    for head in range(HEADS):
+        rows = slice(head * TOK, (head + 1) * TOK)
+        far = f32_dot(q_ref[rows, :], kv_ref[...]) * softmax_scale + bias_ref[...]
+        far_grads = f32_dot(g_ref[rows, :], kv_ref[:LAT, :])
+        near, near_grads = score_ref[rows, :], grad_ref[rows, :]
+        top = jnp.max(jnp.maximum(near, far), axis=1, keepdims=True)
+        near, far = jnp.exp(near - top), jnp.exp(far - top)
+        inverse = 1.0 / jnp.sum(near + far, axis=1, keepdims=True)
+        delta = jnp.sum(near * near_grads + far * far_grads, axis=1, keepdims=True) * inverse
+        for half, (exps, grads) in enumerate(((near, near_grads), (far, far_grads))):
+            probs = exps * inverse
+            for slot in range(2):
+                mine = slice(slot * TOK, (slot + 1) * TOK)
+                place_at = half + (0 if slot == 1 else 2)
+                lanes = slice(place_at * TOK, (place_at + 1) * TOK)
+                p_ref[rows, lanes] = probs[:, mine].astype(jnp.bfloat16)
+                ds_ref[rows, lanes] = (probs[:, mine] * (grads[:, mine] - delta)).astype(
+                    jnp.bfloat16
+                )
+    for part in range(KVW // PART):
+        cols, term = add_terms(qt_ref, gt_ref, ds_ref, p_ref, part, slice(0, 2 * TOK))
+        send_ref[0, cols, :] = term[:, :TOK].astype(jnp.bfloat16)
+        send_ref[1, cols, :] = term[:, TOK:].astype(jnp.bfloat16)
+
+
+def keep_kernel(place, qt_ref, gt_ref, p_ref, ds_ref, keep_ref):
+    for part in range(KVW // PART):
+        cols, term = add_terms(qt_ref, gt_ref, ds_ref, p_ref, part, slice(2 * TOK, 4 * TOK))
+        keep_ref[0, cols, :] = term[:, :TOK]
+        keep_ref[1, cols, :] = term[:, TOK:]
 
 
 def queries_kernel(ds_ref, own_ref, px_ref, p2_ref, sw_ref, out_ref, kv_ref):
-    for slot, ref in enumerate((own_ref, px_ref, p2_ref, sw_ref)):
+    for slot, ref in enumerate((px_ref, sw_ref, own_ref, p2_ref)):
         kv_ref[:, slot * TOK : (slot + 1) * TOK] = ref[...]
     for head in range(HEADS):
         rows = slice(head * TOK, (head + 1) * TOK)
@@ -112,7 +121,7 @@
     )(ds, own, px, p2, sw)
 
 
-def small_call(kernel, name, out_shape, count, scratch=()):
+def call(kernel, name, out_shape, count, scratch=(), macs=1 << 18, limit=8):
     outs = out_shape if isinstance(out_shape, tuple) else (out_shape,)
     specs = (whole,) * len(outs)
     return pl.pallas_call(
@@ -121,8 +130,8 @@
         in_specs=[scalars] + [whole] * count,
         out_specs=specs if isinstance(out_shape, tuple) else whole,
         scratch_shapes=list(scratch),
-        cost_estimate=pl.CostEstimate(flops=1 << 19, bytes_accessed=1 << 20, transcendentals=0),
-        compiler_params=pltpu.CompilerParams(vmem_limit_bytes=8 << 20),
+        cost_estimate=pl.CostEstimate(flops=2 * macs, bytes_accessed=1 << 20, transcendentals=0),
+        compiler_params=pltpu.CompilerParams(vmem_limit_bytes=limit << 20),
         name=name,
     )
 
@@ -202,26 +211,39 @@
     gt = jnp.pad(grad_out.transpose(2, 1, 0).reshape(LAT, ROWS), ((0, width - LAT), (0, 0)))
     doc = doc_start.astype(jnp.float32).reshape(1, tokens)
 
-    keep, send, ds = attention(place, doc, q, qt, g, gt, own, px, p2, sw)
+    pair = [pltpu.VMEM((width, 2 * TOK), jnp.bfloat16), pltpu.VMEM((TOK, 2 * TOK), jnp.float32)]
+    half = jax.ShapeDtypeStruct((ROWS, 2 * TOK), jnp.float32)
+    table = jax.ShapeDtypeStruct((ROWS, 4 * TOK), jnp.bfloat16)
+    sent = jax.ShapeDtypeStruct((2, width, tokens), jnp.bfloat16)
+    kept = jax.ShapeDtypeStruct((2, width, tokens), jnp.float32)
+    work = 2 * ROWS * TOK * (width + LAT)
+    px_now, p2_now = lax.optimization_barrier((px, p2))
+    scores, grads = call(near_kernel, "near", (half, half), 5, pair, work, 12)(
+        place, doc, q, g, own, px_now
+    )
+    send, probs, ds = call(attention_kernel, "attention", (sent, table, table), 9, pair, 2 * work, 20)(
+        place, doc, q, qt, g, gt, scores, grads, p2_now, sw
+    )
     came = lax.ppermute(send, "core", swap)
+    keep = call(keep_kernel, "keep", kept, 4, (), work, 12)(place, qt, gt, probs, ds)
     block = jax.ShapeDtypeStruct((width, tokens), jnp.bfloat16)
     flat = jax.ShapeDtypeStruct((2 * SHARES, WIDE * tokens), jnp.bfloat16)
     pieces = jax.ShapeDtypeStruct((SHARES, 2, WIDE * tokens), jnp.bfloat16)
-    to_next, to_over = small_call(join_kernel, "join", (block, block), 2)(place, keep, came)
+    to_next, to_over = call(join_kernel, "join", (block, block), 2)(place, keep, came)
     ds, to_next, to_over = lax.optimization_barrier((ds, to_next, to_over))
     to_next = lax.ppermute(to_next, everyone, back)
     to_over = lax.ppermute(to_over, everyone, over)
     query_grad = query_grads(ds, own, px, p2, sw)
     to_next, to_over, query_grad = lax.optimization_barrier((to_next, to_over, query_grad))
 
-    terms = small_call(
+    terms = call(
         total_kernel, "total", flat, 4, [pltpu.VMEM((width, tokens), jnp.float32)]
     )(place, keep, came, to_next, to_over)
     terms = lax.all_to_all(terms.reshape(pieces.shape), HEAD, 0, 0, tiled=True)
-    terms = small_call(reduce_kernel, "reduce", pieces, 1)(place, terms)
+    terms = call(reduce_kernel, "reduce", pieces, 1)(place, terms)
     grad = lax.all_to_all(terms, HEAD, 0, 0, tiled=True)
     out = jax.ShapeDtypeStruct((width, tokens), jnp.float32)
-    grad = small_call(finish_kernel, "finish", out, 1)(place, grad.reshape(flat.shape))
+    grad = call(finish_kernel, "finish", out, 1)(place, grad.reshape(flat.shape))
     return query_grad.transpose(2, 0, 1), grad.T
 
 

time: 74.7 us -> 73.8 us (0.988)
  waiting for transfers between devices: 10.6 us -> 9.24 us
    ppermute x1, waiting for transfers between devices: 1.2 us -> 0.34 us  [per_device(): came = lax.ppermute(send, 'core', swap)]
    pallas_call x5 -> x7, Pallas kernels: 3.56 us -> 4.02 us  [the longest x1 1.69 us: per_device(): call(attention_kernel, 'attention', (sent, table, table), 9, pair, 2 * wo...]
  transfers between devices with their start and end apart: 6 -> 6, of which waited for: 4 -> 4; matrix products, arithmetic and copies ran while one was open for 3% -> 3% of each run, Pallas kernels for 2% -> 4%
where the time goes in v7:
time: 73.8 us; the launch traced here: 73.4 us
  blocking collectives  36.3 us (49%)
  starting transfers between devices  18.1 us (25%)
  waiting for transfers between devices  9.24 us (13%)
  Pallas kernels  5.62 us (8%)
  local copies, waits for them, and re-layouts  3.36 us (5%)
  between operations  0.84 us (1%)
    all_to_all x1, blocking collectives, per_device(): terms = lax.all_to_all(terms.reshape(pieces.shape), HEAD, 0, 0, tiled=True)  22.4 us
    all_to_all x1, blocking collectives, per_device(): grad = lax.all_to_all(terms, HEAD, 0, 0, tiled=True)  13.9 us
    ppermute x1, waiting for transfers between devices, per_device(): to_next = lax.ppermute(to_next, everyone, back)  7.22 us
    ppermute x1, starting transfers between devices, per_device(): p2 = lax.ppermute(own, everyone, halo)  7.13 us
    ppermute x1, starting transfers between devices, per_device(): sw = lax.ppermute(p2, 'core', swap)  3.14 us
    ppermute x1, starting transfers between devices, per_device(): to_next = lax.ppermute(to_next, everyone, back)  2.93 us
    ppermute x1, starting transfers between devices, per_device(): came = lax.ppermute(send, 'core', swap)  2.27 us
    ppermute x1, starting transfers between devices, per_device(): px = lax.ppermute(own, everyone, mixed)  1.92 us
  transfers between devices with their start and end apart: 6, of which 4 were waited for; matrix products, arithmetic and copies ran while one was open for 3% of the time, Pallas kernels for 4%

profile of v7, /device:TPU:398, one launch (start us, length us, event | category | flops | bytes accessed | tf_op | source)
XLA Modules:
  0.0 73.4 jit_solution(3722934275447311915)
XLA Ops:
  0.6 7.1 %collective-permute-start.1 = (bf16[576,128]{1,0:T(8,128)(2,1)}, bf16[576,128]{1,0:T(8,128)(2,1)S(1)}, u32[]{:S(2)}, u32[]{:S(2)}) collective-permute-start(bf16[576,128]{1,0:T(8,128)(2,1)} %bitcast.25), channel_id=1, source_target_pairs={{0,80},{1,81},{2,82},{3,83},{4,84},{5,85},{6,86},{7,87},{8,88},{9,... | collective-permute-start | bytes 442376 | tf_op jit(solution)/shard_map/ppermute | solution.py:204
  7.8 1.9 %collective-permute-start = (bf16[576,128]{1,0:T(8,128)(2,1)}, bf16[576,128]{1,0:T(8,128)(2,1)S(1)}, u32[]{:S(2)}, u32[]{:S(2)}) collective-permute-start(bf16[576,128]{1,0:T(8,128)(2,1)} %bitcast.26), channel_id=1, source_target_pairs={{0,32},{1,33},{2,34},{3,35},{4,36},{5,37},{6,38},{7,39},{8,40},{9,... | collective-permute-start | bytes 442376 | tf_op jit(solution)/shard_map/ppermute | solution.py:205
  9.7 0.0 copy-start.2
  9.7 1.2 %copy.8 = bf16[4,128,512]{2,1,0:T(8,128)(2,1)S(1)} copy(bf16[4,128,512]{2,0,1:T(4,128)(2,1)} %bitcast.30) | data formatting | bytes 1048576 | tf_op jit(solution)/shard_map/transpose | solution.py:210
  10.9 0.0 copy-done.2
  10.9 0.6 copy.9
  11.5 0.0 copy-start.1
  11.5 0.1 copy.14
  11.6 1.0 %copy-done.1 = bf16[128,4,576]{0,2,1:T(8,128)(2,1)S(1)} copy-done((bf16[128,4,576]{0,2,1:T(8,128)(2,1)S(1)}, bf16[128,4,576]{0,2,1:T(8,128)(2,1)}, u32[]{:S(2)}) %copy-start.1) | copy-done | bytes 589848
  12.6 0.3 copy.6
  12.9 0.0 copy-start.3
  12.9 0.0 copy-start
  13.0 0.1 copy_bitcast_fusion.qt_ref
  13.0 1.3 %collective-permute-done.1.p2_ref = bf16[576,128]{1,0:T(8,128)(2,1)S(1)} collective-permute-done((bf16[576,128]{1,0:T(8,128)(2,1)}, bf16[576,128]{1,0:T(8,128)(2,1)S(1)}, u32[]{:S(2)}, u32[]{:S(2)}) %collective-permute-start.1) | collective-permute-done | bytes 147488 | tf_op jit(solution)/shard_map/ppermute | solution.py:204
  14.3 3.1 %collective-permute-start.2 = (bf16[576,128]{1,0:T(8,128)(2,1)S(1)}, bf16[576,128]{1,0:T(8,128)(2,1)S(1)}, u32[]{:S(2)}, u32[]{:S(2)}) collective-permute-start(bf16[576,128]{1,0:T(8,128)(2,1)S(1)} %collective-permute-done.1.p2_ref), channel_id=1, source_target_pairs={{0,32},{32,0},{1,33},{33,1},{2,34},{34,2},{3,35},{35,3},{4,36},{36... | collective-permute-start | bytes 442376 | tf_op jit(solution)/shard_map/ppermute | solution.py:206
  17.4 0.0 copy-done.3
  17.5 0.0 collective-permute-done.px_ref
  17.5 0.0 copy-done
  17.5 0.5 near.1
  18.0 0.4 collective-permute-done.2.sw_ref
  18.4 1.7 %attention.1 = (bf16[2,576,128]{2,1,0:T(8,128)(2,1)S(1)}, bf16[512,512]{1,0:T(8,128)(2,1)S(1)}, bf16[512,512]{1,0:T(8,128)(2,1)S(1)}) custom-call(s32[1]{0:T(128)} %bitcast.place, f32[1,128]{1,0:T(1,128)S(1)} %convert_bitcast_fusion.doc_ref, bf16[512,576]{1,0:T(8,128)(2,1)S(1)} %bitcast.22, bf16[576,512]{1,0:T(8,128)(2,1)S(1)} %copy_bitcast_fusion.qt_ref, ...), custom_call_target="tpu_custom_call" | custom-call | flops 570425344 | bytes 1048576 | tf_op jit(solution)/shard_map/attention/pallas_call | solution.py:224
  20.1 2.3 %collective-permute-start.3 = (bf16[2,576,128]{2,1,0:T(8,128)(2,1)S(1)}, bf16[2,576,128]{2,1,0:T(8,128)(2,1)S(1)}, u32[]{:S(2)}, u32[]{:S(2)}) collective-permute-start(bf16[2,576,128]{2,1,0:T(8,128)(2,1)S(1)} %get-tuple-element.23), channel_id=1, source_target_pairs={{0,32},{32,0},{1,33},{33,1},{2,34},{34,2},{3,35},{35,3},{4,36},{36... | collective-permute-start | bytes 884744 | tf_op jit(solution)/shard_map/ppermute | solution.py:227
  22.4 0.9 %keep.1.keep_ref = f32[2,576,128]{2,1,0:T(8,128)S(1)} custom-call(s32[1]{0:T(128)} %bitcast.place, bf16[576,512]{1,0:T(8,128)(2,1)S(1)} %copy_bitcast_fusion.qt_ref, bf16[576,512]{1,0:T(8,128)(2,1)S(1)} %pad.4.gt_ref, bf16[512,512]{1,0:T(8,128)(2,1)S(1)} %get-tuple-element.22.p_ref, bf16[512,512]{1,0:T(8,128)(2,1)S(1)} %get-tuple-element.28.ds_ref), custom_call_target="tpu_custom_call" | custom-call | flops 285212672 | bytes 1048576 | tf_op jit(solution)/shard_map/keep/pallas_call | solution.py:228
  23.3 0.3 collective-permute-done.3.came_ref
  23.6 0.1 join.1
  23.7 2.9 %collective-permute-start.4 = (bf16[576,128]{1,0:T(8,128)(2,1)S(1)}, bf16[576,128]{1,0:T(8,128)(2,1)S(1)}, u32[]{:S(2)}, u32[]{:S(2)}) collective-permute-start(bf16[576,128]{1,0:T(8,128)(2,1)S(1)} %get-tuple-element.26), channel_id=1, source_target_pairs={{64,16},{65,17},{66,18},{67,19},{68,20},{69,21},{70,22},{71,23},{7... | collective-permute-start | bytes 442376 | tf_op jit(solution)/shard_map/ppermute | solution.py:234
  26.6 0.7 collective-permute-start.5
  27.3 1.6 %query_grads.1 = bf16[4,576,128]{2,1,0:T(8,128)(2,1)} custom-call(bf16[512,512]{1,0:T(8,128)(2,1)S(1)} %get-tuple-element.28.ds_ref, bf16[576,128]{1,0:T(8,128)(2,1)S(1)} %bitcast.28, bf16[576,128]{1,0:T(8,128)(2,1)S(1)} %collective-permute-done.px_ref, bf16[576,128]{1,0:T(8,128)(2,1)S(1)} %collective-permute-done.1.p2_ref, ...), custom_call_target="tpu_custom_call" | custom-call | flops 301989888 | bytes 2097152 | tf_op jit(solution)/shard_map/query_grads/pallas_call | solution.py:110
  28.9 7.2 %collective-permute-done.4.next_ref = bf16[576,128]{1,0:T(8,128)(2,1)S(1)} collective-permute-done((bf16[576,128]{1,0:T(8,128)(2,1)S(1)}, bf16[576,128]{1,0:T(8,128)(2,1)S(1)}, u32[]{:S(2)}, u32[]{:S(2)}) %collective-permute-start.4) | collective-permute-done | bytes 147488 | tf_op jit(solution)/shard_map/ppermute | solution.py:234
  36.1 0.0 collective-permute-done.5.over_ref
  36.1 0.1 total.1
  36.2 0.1 reshape.34
  36.3 22.4 %all_to_all.10.came_ref = bf16[32,2,1152]{2,1,0:T(2,128)(2,1)S(1)} all-to-all(bf16[32,2,1152]{2,1,0:T(2,128)(2,1)S(1)} %reshape.34), channel_id=1, replica_groups=mesh['z'=8,'xh'=2,'core'=2,'xl'=4,'y'=8] {'xl','y'}, dimensions={0} | all-to-all | bytes 294912 | tf_op jit(solution)/shard_map/all_to_all | solution.py:242
  58.7 0.1 reduce.1
  58.8 13.9 %all_to_all.11 = bf16[32,2,1152]{2,1,0:T(2,128)(2,1)S(1)} all-to-all(bf16[32,2,1152]{2,1,0:T(2,128)(2,1)S(1)} %reduce.1), channel_id=1, replica_groups=mesh['z'=8,'xh'=2,'core'=2,'xl'=4,'y'=8] {'xl','y'}, dimensions={0} | all-to-all | bytes 294912 | tf_op jit(solution)/shard_map/all_to_all | solution.py:244
  72.6 0.1 reshape.35.came_ref
  72.7 0.7 %finish.1 = f32[576,128]{1,0:T(8,128)} custom-call(s32[1]{0:T(128)} %bitcast.place, bf16[64,1152]{1,0:T(8,128)(2,1)S(1)} %reshape.35.came_ref), custom_call_target="tpu_custom_call" | custom-call | flops 524288 | bytes 1048576 | tf_op jit(solution)/shard_map/finish/pallas_call | solution.py:246
  (2 shorter events, 0.0 us)
Async XLA Ops:
  0.6 13.7 %collective-permute-start.1 = (bf16[576,128]{1,0:T(8,128)(2,1)}, bf16[576,128]{1,0:T(8,128)(2,1)S(1)}, u32[]{:S(2)}, u32[]{:S(2)}) collective-permute-start(bf16[576,128]{1,0:T(8,128)(2,1)} %bitcast.25), channel_id=1, source_target_pairs={{0,80},{1,81},{2,82},{3,83},{4,84},{5,85},{6,86},{7,87},{8,88},{9,... | collective-permute-start | bytes 442376 | tf_op jit(solution)/shard_map/ppermute | solution.py:204
  7.8 9.7 %collective-permute-start = (bf16[576,128]{1,0:T(8,128)(2,1)}, bf16[576,128]{1,0:T(8,128)(2,1)S(1)}, u32[]{:S(2)}, u32[]{:S(2)}) collective-permute-start(bf16[576,128]{1,0:T(8,128)(2,1)} %bitcast.26), channel_id=1, source_target_pairs={{0,32},{1,33},{2,34},{3,35},{4,36},{5,37},{6,38},{7,39},{8,40},{9,... | collective-permute-start | bytes 442376 | tf_op jit(solution)/shard_map/ppermute | solution.py:205
  9.7 1.2 %copy-start.2 = (bf16[128,4,512]{2,1,0:T(4,128)(2,1)S(1)}, bf16[128,4,512]{2,1,0:T(4,128)(2,1)}, u32[]{:S(2)}) copy-start(bf16[128,4,512]{2,1,0:T(4,128)(2,1)} %param.6) | copy-start | bytes 1572868
  11.5 1.1 %copy-start.1 = (bf16[128,4,576]{0,2,1:T(8,128)(2,1)S(1)}, bf16[128,4,576]{0,2,1:T(8,128)(2,1)}, u32[]{:S(2)}) copy-start(bf16[128,4,576]{0,2,1:T(8,128)(2,1)} %param.4) | copy-start | bytes 1769476
  12.9 4.5 %copy-start.3 = (s32[128]{0:T(128)S(1)}, s32[128]{0:T(128)}, u32[]{:S(2)}) copy-start(s32[128]{0:T(128)} %param.7) | copy-start | bytes 1540
  12.9 4.5 %copy-start = (bf16[128,576]{0,1:T(8,128)(2,1)S(1)}, bf16[128,576]{0,1:T(8,128)(2,1)}, u32[]{:S(2)}) copy-start(bf16[128,576]{0,1:T(8,128)(2,1)} %param.5) | copy-start | bytes 442372
  14.3 4.1 %collective-permute-start.2 = (bf16[576,128]{1,0:T(8,128)(2,1)S(1)}, bf16[576,128]{1,0:T(8,128)(2,1)S(1)}, u32[]{:S(2)}, u32[]{:S(2)}) collective-permute-start(bf16[576,128]{1,0:T(8,128)(2,1)S(1)} %collective-permute-done.1.p2_ref), channel_id=1, source_target_pairs={{0,32},{32,0},{1,33},{33,1},{2,34},{34,2},{3,35},{35,3},{4,36},{36... | collective-permute-start | bytes 442376 | tf_op jit(solution)/shard_map/ppermute | solution.py:206
  20.1 3.5 %collective-permute-start.3 = (bf16[2,576,128]{2,1,0:T(8,128)(2,1)S(1)}, bf16[2,576,128]{2,1,0:T(8,128)(2,1)S(1)}, u32[]{:S(2)}, u32[]{:S(2)}) collective-permute-start(bf16[2,576,128]{2,1,0:T(8,128)(2,1)S(1)} %get-tuple-element.23), channel_id=1, source_target_pairs={{0,32},{32,0},{1,33},{33,1},{2,34},{34,2},{3,35},{35,3},{4,36},{36... | collective-permute-start | bytes 884744 | tf_op jit(solution)/shard_map/ppermute | solution.py:227
  23.7 12.4 %collective-permute-start.4 = (bf16[576,128]{1,0:T(8,128)(2,1)S(1)}, bf16[576,128]{1,0:T(8,128)(2,1)S(1)}, u32[]{:S(2)}, u32[]{:S(2)}) collective-permute-start(bf16[576,128]{1,0:T(8,128)(2,1)S(1)} %get-tuple-element.26), channel_id=1, source_target_pairs={{64,16},{65,17},{66,18},{67,19},{68,20},{69,21},{70,22},{71,23},{7... | collective-permute-start | bytes 442376 | tf_op jit(solution)/shard_map/ppermute | solution.py:234
  26.6 9.5 %collective-permute-start.5 = (bf16[576,128]{1,0:T(8,128)(2,1)S(1)}, bf16[576,128]{1,0:T(8,128)(2,1)S(1)}, u32[]{:S(2)}, u32[]{:S(2)}) collective-permute-start(bf16[576,128]{1,0:T(8,128)(2,1)S(1)} %get-tuple-element.27), channel_id=1, source_target_pairs={{160,32},{161,33},{162,34},{163,35},{164,36},{165,37},{166,38},{16... | collective-permute-start | bytes 442376 | tf_op jit(solution)/shard_map/ppermute | solution.py:235

commit v8 on v7

--- a/solution.py
+++ b/solution.py
@@ -41,10 +41,10 @@
 
 
 def near_kernel(
-    place, doc_ref, q_ref, g_ref, own_ref, px_ref, score_ref, grad_ref, kv_ref, bias_ref
+    place, doc_ref, q_ref, g_ref, px_ref, p2_ref, score_ref, grad_ref, kv_ref, bias_ref
 ):
     core = lax.rem(place[0], 2)
-    load_pair(place, doc_ref, (0, 3 - 2 * core), (own_ref, px_ref), kv_ref, bias_ref)
+    load_pair(place, doc_ref, (3 - 2 * core, 2), (px_ref, p2_ref), kv_ref, bias_ref)
     for head in range(HEADS):
         rows = slice(head * TOK, (head + 1) * TOK)
         score_ref[rows, :] = f32_dot(q_ref[rows, :], kv_ref[...]) * softmax_scale + bias_ref[...]
@@ -58,11 +58,11 @@
 
 
 def attention_kernel(
-    place, doc_ref, q_ref, qt_ref, g_ref, gt_ref, score_ref, grad_ref, p2_ref, sw_ref,
+    place, doc_ref, q_ref, qt_ref, g_ref, gt_ref, score_ref, grad_ref, own_ref, sw_ref,
     send_ref, p_ref, ds_ref, kv_ref, bias_ref,
 ):
     core = lax.rem(place[0], 2)
-    load_pair(place, doc_ref, (2, 1 + 2 * core), (p2_ref, sw_ref), kv_ref, bias_ref)
+    load_pair(place, doc_ref, (0, 1 + 2 * core), (own_ref, sw_ref), kv_ref, bias_ref)
     for head in range(HEADS):
         rows = slice(head * TOK, (head + 1) * TOK)
         far = f32_dot(q_ref[rows, :], kv_ref[...]) * softmax_scale + bias_ref[...]
@@ -76,7 +76,7 @@
             probs = exps * inverse
             for slot in range(2):
                 mine = slice(slot * TOK, (slot + 1) * TOK)
-                place_at = half + (0 if slot == 1 else 2)
+                place_at = ((0, 3), (2, 1))[half][slot]
                 lanes = slice(place_at * TOK, (place_at + 1) * TOK)
                 p_ref[rows, lanes] = probs[:, mine].astype(jnp.bfloat16)
                 ds_ref[rows, lanes] = (probs[:, mine] * (grads[:, mine] - delta)).astype(
@@ -208,7 +208,6 @@
     q = queries.transpose(1, 0, 2).reshape(ROWS, width)
     qt = queries.transpose(2, 1, 0).reshape(width, ROWS)
     g = grad_out.transpose(1, 0, 2).reshape(ROWS, LAT)
-    gt = jnp.pad(grad_out.transpose(2, 1, 0).reshape(LAT, ROWS), ((0, width - LAT), (0, 0)))
     doc = doc_start.astype(jnp.float32).reshape(1, tokens)
 
     pair = [pltpu.VMEM((width, 2 * TOK), jnp.bfloat16), pltpu.VMEM((TOK, 2 * TOK), jnp.float32)]
@@ -217,12 +216,13 @@
     sent = jax.ShapeDtypeStruct((2, width, tokens), jnp.bfloat16)
     kept = jax.ShapeDtypeStruct((2, width, tokens), jnp.float32)
     work = 2 * ROWS * TOK * (width + LAT)
-    px_now, p2_now = lax.optimization_barrier((px, p2))
+    px_now, p2_now, late = lax.optimization_barrier((px, p2, grad_out))
+    gt = jnp.pad(late.transpose(2, 1, 0).reshape(LAT, ROWS), ((0, width - LAT), (0, 0)))
     scores, grads = call(near_kernel, "near", (half, half), 5, pair, work, 12)(
-        place, doc, q, g, own, px_now
+        place, doc, q, g, px_now, p2_now
     )
     send, probs, ds = call(attention_kernel, "attention", (sent, table, table), 9, pair, 2 * work, 20)(
-        place, doc, q, qt, g, gt, scores, grads, p2_now, sw
+        place, doc, q, qt, g, gt, scores, grads, own, sw
     )
     came = lax.ppermute(send, "core", swap)
     keep = call(keep_kernel, "keep", kept, 4, (), work, 12)(place, qt, gt, probs, ds)

time: 73.8 us -> 72.5 us (0.982)
  blocking collectives: 36.3 us -> 34.6 us
  waiting for transfers between devices: 9.24 us -> 10.5 us
    all_to_all x1, blocking collectives: 22.4 us -> 20.6 us  [per_device(): terms = lax.all_to_all(terms.reshape(pieces.shape), HEAD, 0, 0, tiled=True)]
    ppermute x1, waiting for transfers between devices: 1.27 us -> 3.03 us  [per_device(): p2 = lax.ppermute(own, everyone, halo)]
    ppermute x1, starting transfers between devices: 3.14 us -> 1.91 us  [per_device(): sw = lax.ppermute(p2, 'core', swap)]
    ppermute x1, starting transfers between devices: 2.93 us -> 3.84 us  [per_device(): to_next = lax.ppermute(to_next, everyone, back)]
  transfers between devices with their start and end apart: 6 -> 6, of which waited for: 4 -> 3; matrix products, arithmetic and copies ran while one was open for 3% -> 3% of each run, Pallas kernels for 4% -> 4%
where the time goes in v8:
time: 72.5 us; the launch traced here: 72.1 us
  blocking collectives  34.6 us (48%)
  starting transfers between devices  18 us (25%)
  waiting for transfers between devices  10.5 us (14%)
  Pallas kernels  5.56 us (8%)
  local copies, waits for them, and re-layouts  2.64 us (4%)
  between operations  0.84 us (1%)
    all_to_all x1, blocking collectives, per_device(): terms = lax.all_to_all(terms.reshape(pieces.shape), HEAD, 0, 0, tiled=True)  20.6 us
    all_to_all x1, blocking collectives, per_device(): grad = lax.all_to_all(terms, HEAD, 0, 0, tiled=True)  13.9 us
    ppermute x1, starting transfers between devices, per_device(): p2 = lax.ppermute(own, everyone, halo)  7.26 us
    ppermute x1, waiting for transfers between devices, per_device(): to_next = lax.ppermute(to_next, everyone, back)  7.06 us
    ppermute x1, starting transfers between devices, per_device(): to_next = lax.ppermute(to_next, everyone, back)  3.84 us
    ppermute x1, waiting for transfers between devices, per_device(): p2 = lax.ppermute(own, everyone, halo)  3.03 us
    ppermute x1, starting transfers between devices, per_device(): came = lax.ppermute(send, 'core', swap)  2.39 us
    ppermute x1, starting transfers between devices, per_device(): px = lax.ppermute(own, everyone, mixed)  1.92 us
  transfers between devices with their start and end apart: 6, of which 3 were waited for; matrix products, arithmetic and copies ran while one was open for 3% of the time, Pallas kernels for 4%

profile of v8, /device:TPU:398, one launch (start us, length us, event | category | flops | bytes accessed | tf_op | source)
XLA Modules:
  0.0 72.1 jit_solution(7948669622167114104)
XLA Ops:
  0.6 0.0 copy-start.1
  0.6 7.3 %collective-permute-start.1 = (bf16[576,128]{1,0:T(8,128)(2,1)}, bf16[576,128]{1,0:T(8,128)(2,1)S(1)}, u32[]{:S(2)}, u32[]{:S(2)}) collective-permute-start(bf16[576,128]{1,0:T(8,128)(2,1)} %bitcast.25), channel_id=1, source_target_pairs={{0,80},{1,81},{2,82},{3,83},{4,84},{5,85},{6,86},{7,87},{8,88},{9,... | collective-permute-start | bytes 442376 | tf_op jit(solution)/shard_map/ppermute | solution.py:204
  7.9 1.9 %collective-permute-start = (bf16[576,128]{1,0:T(8,128)(2,1)}, bf16[576,128]{1,0:T(8,128)(2,1)S(1)}, u32[]{:S(2)}, u32[]{:S(2)}) collective-permute-start(bf16[576,128]{1,0:T(8,128)(2,1)} %bitcast.26), channel_id=1, source_target_pairs={{0,32},{1,33},{2,34},{3,35},{4,36},{5,37},{6,38},{7,39},{8,40},{9,... | collective-permute-start | bytes 442376 | tf_op jit(solution)/shard_map/ppermute | solution.py:205
  9.8 1.1 %copy.8 = bf16[4,128,512]{2,1,0:T(8,128)(2,1)S(1)} copy(bf16[4,128,512]{2,0,1:T(4,128)(2,1)} %bitcast.30) | data formatting | bytes 1048576 | tf_op jit(solution)/shard_map/transpose | solution.py:210
  11.0 0.0 copy-done.1
  11.0 0.3 copy.6
  11.3 0.0 copy-start.3
  11.3 0.0 copy-start.2
  11.3 0.1 copy_bitcast_fusion.qt_ref
  11.4 3.0 %collective-permute-done.1.p2_ref = bf16[576,128]{1,0:T(8,128)(2,1)S(1)} collective-permute-done((bf16[576,128]{1,0:T(8,128)(2,1)}, bf16[576,128]{1,0:T(8,128)(2,1)S(1)}, u32[]{:S(2)}, u32[]{:S(2)}) %collective-permute-start.1) | collective-permute-done | bytes 147488 | tf_op jit(solution)/shard_map/ppermute | solution.py:204
  14.4 1.9 %collective-permute-start.2 = (bf16[576,128]{1,0:T(8,128)(2,1)S(1)}, bf16[576,128]{1,0:T(8,128)(2,1)S(1)}, u32[]{:S(2)}, u32[]{:S(2)}) collective-permute-start(bf16[576,128]{1,0:T(8,128)(2,1)S(1)} %collective-permute-done.1.p2_ref), channel_id=1, source_target_pairs={{0,32},{32,0},{1,33},{33,1},{2,34},{34,2},{3,35},{35,3},{4,36},{36... | collective-permute-start | bytes 442376 | tf_op jit(solution)/shard_map/ppermute | solution.py:206
  16.4 0.0 copy-done.3
  16.4 0.0 collective-permute-done.px_ref
  16.4 0.0 copy-done.2
  16.4 0.6 copy.9
  17.0 0.1 copy.14
  17.1 0.0 copy-start
  17.1 0.5 near.1
  17.7 0.0 collective-permute-done.2.sw_ref
  17.7 0.3 copy-done
  18.0 1.6 %attention.1 = (bf16[2,576,128]{2,1,0:T(8,128)(2,1)S(1)}, bf16[512,512]{1,0:T(8,128)(2,1)S(1)}, bf16[512,512]{1,0:T(8,128)(2,1)S(1)}) custom-call(s32[1]{0:T(128)} %bitcast.place, f32[1,128]{1,0:T(1,128)S(1)} %convert_bitcast_fusion.doc_ref, bf16[512,576]{1,0:T(8,128)(2,1)S(1)} %bitcast.22, bf16[576,512]{1,0:T(8,128)(2,1)S(1)} %copy_bitcast_fusion.qt_ref, ...), custom_call_target="tpu_custom_call" | custom-call | flops 570425344 | bytes 1048576 | tf_op jit(solution)/shard_map/attention/pallas_call | solution.py:224
  19.7 2.4 %collective-permute-start.3 = (bf16[2,576,128]{2,1,0:T(8,128)(2,1)S(1)}, bf16[2,576,128]{2,1,0:T(8,128)(2,1)S(1)}, u32[]{:S(2)}, u32[]{:S(2)}) collective-permute-start(bf16[2,576,128]{2,1,0:T(8,128)(2,1)S(1)} %get-tuple-element.25), channel_id=1, source_target_pairs={{0,32},{32,0},{1,33},{33,1},{2,34},{34,2},{3,35},{35,3},{4,36},{36... | collective-permute-start | bytes 884744 | tf_op jit(solution)/shard_map/ppermute | solution.py:227
  22.1 0.8 %keep.1.keep_ref = f32[2,576,128]{2,1,0:T(8,128)S(1)} custom-call(s32[1]{0:T(128)} %bitcast.place, bf16[576,512]{1,0:T(8,128)(2,1)S(1)} %copy_bitcast_fusion.qt_ref, bf16[576,512]{1,0:T(8,128)(2,1)S(1)} %pad.4.gt_ref, bf16[512,512]{1,0:T(8,128)(2,1)S(1)} %get-tuple-element.24.p_ref, bf16[512,512]{1,0:T(8,128)(2,1)S(1)} %get-tuple-element.30.ds_ref), custom_call_target="tpu_custom_call" | custom-call | flops 285212672 | bytes 1048576 | tf_op jit(solution)/shard_map/keep/pallas_call | solution.py:228
  22.9 0.3 collective-permute-done.3.came_ref
  23.3 0.1 join.1
  23.3 3.8 %collective-permute-start.4 = (bf16[576,128]{1,0:T(8,128)(2,1)S(1)}, bf16[576,128]{1,0:T(8,128)(2,1)S(1)}, u32[]{:S(2)}, u32[]{:S(2)}) collective-permute-start(bf16[576,128]{1,0:T(8,128)(2,1)S(1)} %get-tuple-element.28), channel_id=1, source_target_pairs={{64,16},{65,17},{66,18},{67,19},{68,20},{69,21},{70,22},{71,23},{7... | collective-permute-start | bytes 442376 | tf_op jit(solution)/shard_map/ppermute | solution.py:234
  27.2 0.7 collective-permute-start.5
  27.8 1.6 %query_grads.1 = bf16[4,576,128]{2,1,0:T(8,128)(2,1)} custom-call(bf16[512,512]{1,0:T(8,128)(2,1)S(1)} %get-tuple-element.30.ds_ref, bf16[576,128]{1,0:T(8,128)(2,1)S(1)} %bitcast.28, bf16[576,128]{1,0:T(8,128)(2,1)S(1)} %collective-permute-done.px_ref, bf16[576,128]{1,0:T(8,128)(2,1)S(1)} %collective-permute-done.1.p2_ref, ...), custom_call_target="tpu_custom_call" | custom-call | flops 301989888 | bytes 2097152 | tf_op jit(solution)/shard_map/query_grads/pallas_call | solution.py:110
  29.4 7.1 %collective-permute-done.4.next_ref = bf16[576,128]{1,0:T(8,128)(2,1)S(1)} collective-permute-done((bf16[576,128]{1,0:T(8,128)(2,1)S(1)}, bf16[576,128]{1,0:T(8,128)(2,1)S(1)}, u32[]{:S(2)}, u32[]{:S(2)}) %collective-permute-start.4) | collective-permute-done | bytes 147488 | tf_op jit(solution)/shard_map/ppermute | solution.py:234
  36.5 0.0 collective-permute-done.5.over_ref
  36.5 0.1 total.1
  36.6 0.1 reshape.34
  36.7 20.6 %all_to_all.10.came_ref = bf16[32,2,1152]{2,1,0:T(2,128)(2,1)S(1)} all-to-all(bf16[32,2,1152]{2,1,0:T(2,128)(2,1)S(1)} %reshape.34), channel_id=1, replica_groups=mesh['z'=8,'xh'=2,'core'=2,'xl'=4,'y'=8] {'xl','y'}, dimensions={0} | all-to-all | bytes 294912 | tf_op jit(solution)/shard_map/all_to_all | solution.py:242
  57.3 0.1 reduce.1
  57.4 13.9 %all_to_all.11 = bf16[32,2,1152]{2,1,0:T(2,128)(2,1)S(1)} all-to-all(bf16[32,2,1152]{2,1,0:T(2,128)(2,1)S(1)} %reduce.1), channel_id=1, replica_groups=mesh['z'=8,'xh'=2,'core'=2,'xl'=4,'y'=8] {'xl','y'}, dimensions={0} | all-to-all | bytes 294912 | tf_op jit(solution)/shard_map/all_to_all | solution.py:244
  71.3 0.1 reshape.35.came_ref
  71.3 0.7 %finish.1 = f32[576,128]{1,0:T(8,128)} custom-call(s32[1]{0:T(128)} %bitcast.place, bf16[64,1152]{1,0:T(8,128)(2,1)S(1)} %reshape.35.came_ref), custom_call_target="tpu_custom_call" | custom-call | flops 524288 | bytes 1048576 | tf_op jit(solution)/shard_map/finish/pallas_call | solution.py:246
  (2 shorter events, 0.0 us)
Async XLA Ops:
  0.6 10.4 %copy-start.1 = (bf16[128,4,576]{0,2,1:T(8,128)(2,1)S(1)}, bf16[128,4,576]{0,2,1:T(8,128)(2,1)}, u32[]{:S(2)}) copy-start(bf16[128,4,576]{0,2,1:T(8,128)(2,1)} %param.4) | copy-start | bytes 1769476
  0.6 13.8 %collective-permute-start.1 = (bf16[576,128]{1,0:T(8,128)(2,1)}, bf16[576,128]{1,0:T(8,128)(2,1)S(1)}, u32[]{:S(2)}, u32[]{:S(2)}) collective-permute-start(bf16[576,128]{1,0:T(8,128)(2,1)} %bitcast.25), channel_id=1, source_target_pairs={{0,80},{1,81},{2,82},{3,83},{4,84},{5,85},{6,86},{7,87},{8,88},{9,... | collective-permute-start | bytes 442376 | tf_op jit(solution)/shard_map/ppermute | solution.py:204
  7.9 8.5 %collective-permute-start = (bf16[576,128]{1,0:T(8,128)(2,1)}, bf16[576,128]{1,0:T(8,128)(2,1)S(1)}, u32[]{:S(2)}, u32[]{:S(2)}) collective-permute-start(bf16[576,128]{1,0:T(8,128)(2,1)} %bitcast.26), channel_id=1, source_target_pairs={{0,32},{1,33},{2,34},{3,35},{4,36},{5,37},{6,38},{7,39},{8,40},{9,... | collective-permute-start | bytes 442376 | tf_op jit(solution)/shard_map/ppermute | solution.py:205
  11.3 5.1 %copy-start.3 = (s32[128]{0:T(128)S(1)}, s32[128]{0:T(128)}, u32[]{:S(2)}) copy-start(s32[128]{0:T(128)} %param.7) | copy-start | bytes 1540
  11.3 5.1 %copy-start.2 = (bf16[128,4,512]{2,1,0:T(4,128)(2,1)S(1)}, bf16[128,4,512]{2,1,0:T(4,128)(2,1)}, u32[]{:S(2)}) copy-start(bf16[128,4,512]{2,1,0:T(4,128)(2,1)} %param.6) | copy-start | bytes 1572868
  14.4 3.3 %collective-permute-start.2 = (bf16[576,128]{1,0:T(8,128)(2,1)S(1)}, bf16[576,128]{1,0:T(8,128)(2,1)S(1)}, u32[]{:S(2)}, u32[]{:S(2)}) collective-permute-start(bf16[576,128]{1,0:T(8,128)(2,1)S(1)} %collective-permute-done.1.p2_ref), channel_id=1, source_target_pairs={{0,32},{32,0},{1,33},{33,1},{2,34},{34,2},{3,35},{35,3},{4,36},{36... | collective-permute-start | bytes 442376 | tf_op jit(solution)/shard_map/ppermute | solution.py:206
  17.1 0.9 %copy-start = (bf16[128,576]{0,1:T(8,128)(2,1)S(1)}, bf16[128,576]{0,1:T(8,128)(2,1)}, u32[]{:S(2)}) copy-start(bf16[128,576]{0,1:T(8,128)(2,1)} %param.5) | copy-start | bytes 442372
  19.7 3.6 %collective-permute-start.3 = (bf16[2,576,128]{2,1,0:T(8,128)(2,1)S(1)}, bf16[2,576,128]{2,1,0:T(8,128)(2,1)S(1)}, u32[]{:S(2)}, u32[]{:S(2)}) collective-permute-start(bf16[2,576,128]{2,1,0:T(8,128)(2,1)S(1)} %get-tuple-element.25), channel_id=1, source_target_pairs={{0,32},{32,0},{1,33},{33,1},{2,34},{34,2},{3,35},{35,3},{4,36},{36... | collective-permute-start | bytes 884744 | tf_op jit(solution)/shard_map/ppermute | solution.py:227
  23.3 13.2 %collective-permute-start.4 = (bf16[576,128]{1,0:T(8,128)(2,1)S(1)}, bf16[576,128]{1,0:T(8,128)(2,1)S(1)}, u32[]{:S(2)}, u32[]{:S(2)}) collective-permute-start(bf16[576,128]{1,0:T(8,128)(2,1)S(1)} %get-tuple-element.28), channel_id=1, source_target_pairs={{64,16},{65,17},{66,18},{67,19},{68,20},{69,21},{70,22},{71,23},{7... | collective-permute-start | bytes 442376 | tf_op jit(solution)/shard_map/ppermute | solution.py:234
  27.2 9.3 %collective-permute-start.5 = (bf16[576,128]{1,0:T(8,128)(2,1)S(1)}, bf16[576,128]{1,0:T(8,128)(2,1)S(1)}, u32[]{:S(2)}, u32[]{:S(2)}) collective-permute-start(bf16[576,128]{1,0:T(8,128)(2,1)S(1)} %get-tuple-element.29), channel_id=1, source_target_pairs={{160,32},{161,33},{162,34},{163,35},{164,36},{165,37},{166,38},{16... | collective-permute-start | bytes 442376 | tf_op jit(solution)/shard_map/ppermute | solution.py:235

commit v9 on v8

--- a/solution.py
+++ b/solution.py
@@ -41,7 +41,7 @@
 
 
 def near_kernel(
-    place, doc_ref, q_ref, g_ref, px_ref, p2_ref, score_ref, grad_ref, kv_ref, bias_ref
+    place, doc_ref, q_ref, g_ref, px_ref, p2_ref, score_ref, grad_ref, gt_ref, kv_ref, bias_ref
 ):
     core = lax.rem(place[0], 2)
     load_pair(place, doc_ref, (3 - 2 * core, 2), (px_ref, p2_ref), kv_ref, bias_ref)
@@ -49,6 +49,8 @@
         rows = slice(head * TOK, (head + 1) * TOK)
         score_ref[rows, :] = f32_dot(q_ref[rows, :], kv_ref[...]) * softmax_scale + bias_ref[...]
         grad_ref[rows, :] = f32_dot(g_ref[rows, :], kv_ref[:LAT, :])
+        gt_ref[:LAT, rows] = g_ref[rows, :].T
+    gt_ref[LAT:, :] = jnp.zeros((KVW - LAT, ROWS), jnp.bfloat16)
 
 
 def add_terms(qt_ref, gt_ref, ds_ref, p_ref, part, lanes):
@@ -216,9 +218,9 @@
     sent = jax.ShapeDtypeStruct((2, width, tokens), jnp.bfloat16)
     kept = jax.ShapeDtypeStruct((2, width, tokens), jnp.float32)
     work = 2 * ROWS * TOK * (width + LAT)
-    px_now, p2_now, late = lax.optimization_barrier((px, p2, grad_out))
-    gt = jnp.pad(late.transpose(2, 1, 0).reshape(LAT, ROWS), ((0, width - LAT), (0, 0)))
-    scores, grads = call(near_kernel, "near", (half, half), 5, pair, work, 12)(
+    px_now, p2_now = lax.optimization_barrier((px, p2))
+    turned = jax.ShapeDtypeStruct((width, ROWS), jnp.bfloat16)
+    scores, grads, gt = call(near_kernel, "near", (half, half, turned), 5, pair, work, 12)(
         place, doc, q, g, px_now, p2_now
     )
     send, probs, ds = call(attention_kernel, "attention", (sent, table, table), 9, pair, 2 * work, 20)(

time: 72.5 us -> 71.9 us (level)
  the two profiles are of different devices: /device:TPU:398 before, /device:TPU:270 now
where the time goes in v9:
time: 71.9 us; the launch traced here: 71.5 us
  blocking collectives  36.3 us (50%)
  starting transfers between devices  17.8 us (25%)
  waiting for transfers between devices  9.28 us (13%)
  Pallas kernels  5.64 us (8%)
  local copies, waits for them, and re-layouts  1.63 us (2%)
  between operations  0.8 us (1%)
    all_to_all x1, blocking collectives, per_device(): terms = lax.all_to_all(terms.reshape(pieces.shape), HEAD, 0, 0, tiled=True)  22.4 us
    all_to_all x1, blocking collectives, per_device(): grad = lax.all_to_all(terms, HEAD, 0, 0, tiled=True)  13.9 us
    ppermute x1, starting transfers between devices, per_device(): p2 = lax.ppermute(own, everyone, halo)  6.05 us
    ppermute x1, waiting for transfers between devices, per_device(): to_next = lax.ppermute(to_next, everyone, back)  5.47 us
    ppermute x1, starting transfers between devices, per_device(): sw = lax.ppermute(p2, 'core', swap)  3.47 us
    ppermute x1, starting transfers between devices, per_device(): to_next = lax.ppermute(to_next, everyone, back)  3.45 us
    ppermute x1, waiting for transfers between devices, per_device(): p2 = lax.ppermute(own, everyone, halo)  3.04 us
    ppermute x1, starting transfers between devices, per_device(): came = lax.ppermute(send, 'core', swap)  2.25 us
  transfers between devices with their start and end apart: 6, of which 4 were waited for; matrix products, arithmetic and copies ran while one was open for 2% of the time, Pallas kernels for 4%

profile of v9, /device:TPU:270, one launch (start us, length us, event | category | flops | bytes accessed | tf_op | source)
XLA Modules:
  0.0 71.5 jit_solution(7010805397040193511)
XLA Ops:
  0.6 0.0 copy-start.1
  0.6 6.1 %collective-permute-start.1 = (bf16[576,128]{1,0:T(8,128)(2,1)}, bf16[576,128]{1,0:T(8,128)(2,1)S(1)}, u32[]{:S(2)}, u32[]{:S(2)}) collective-permute-start(bf16[576,128]{1,0:T(8,128)(2,1)} %bitcast.20), channel_id=1, source_target_pairs={{0,80},{1,81},{2,82},{3,83},{4,84},{5,85},{6,86},{7,87},{8,88},{9,... | collective-permute-start | bytes 442376 | tf_op jit(solution)/shard_map/ppermute | solution.py:206
  6.7 1.9 %collective-permute-start = (bf16[576,128]{1,0:T(8,128)(2,1)}, bf16[576,128]{1,0:T(8,128)(2,1)S(1)}, u32[]{:S(2)}, u32[]{:S(2)}) collective-permute-start(bf16[576,128]{1,0:T(8,128)(2,1)} %bitcast.21), channel_id=1, source_target_pairs={{0,32},{1,33},{2,34},{3,35},{4,36},{5,37},{6,38},{7,39},{8,40},{9,... | collective-permute-start | bytes 442376 | tf_op jit(solution)/shard_map/ppermute | solution.py:207
  8.6 1.1 %copy.8 = bf16[4,128,512]{2,1,0:T(8,128)(2,1)S(1)} copy(bf16[4,128,512]{2,0,1:T(4,128)(2,1)} %bitcast.26) | data formatting | bytes 1048576 | tf_op jit(solution)/shard_map/transpose | solution.py:212
  9.8 0.0 copy-done.1
  9.8 0.3 copy.6
  10.1 0.0 copy-start.2
  10.1 0.1 copy_bitcast_fusion.qt_ref
  10.2 3.0 %collective-permute-done.1.p2_ref = bf16[576,128]{1,0:T(8,128)(2,1)S(1)} collective-permute-done((bf16[576,128]{1,0:T(8,128)(2,1)}, bf16[576,128]{1,0:T(8,128)(2,1)S(1)}, u32[]{:S(2)}, u32[]{:S(2)}) %collective-permute-start.1) | collective-permute-done | bytes 147488 | tf_op jit(solution)/shard_map/ppermute | solution.py:206
  13.2 3.5 %collective-permute-start.2 = (bf16[576,128]{1,0:T(8,128)(2,1)S(1)}, bf16[576,128]{1,0:T(8,128)(2,1)S(1)}, u32[]{:S(2)}, u32[]{:S(2)}) collective-permute-start(bf16[576,128]{1,0:T(8,128)(2,1)S(1)} %collective-permute-done.1.p2_ref), channel_id=1, source_target_pairs={{0,32},{32,0},{1,33},{33,1},{2,34},{34,2},{3,35},{35,3},{4,36},{36... | collective-permute-start | bytes 442376 | tf_op jit(solution)/shard_map/ppermute | solution.py:208
  16.7 0.0 copy-done.2
  16.7 0.0 collective-permute-done.px_ref
  16.7 0.0 copy-start
  16.8 0.5 near.1
  17.3 0.4 collective-permute-done.2.sw_ref
  17.7 0.0 copy-done
  17.7 1.7 %attention.1 = (bf16[2,576,128]{2,1,0:T(8,128)(2,1)S(1)}, bf16[512,512]{1,0:T(8,128)(2,1)S(1)}, bf16[512,512]{1,0:T(8,128)(2,1)S(1)}) custom-call(s32[1]{0:T(128)} %bitcast.place, f32[1,128]{1,0:T(1,128)S(1)} %convert_bitcast_fusion.doc_ref, bf16[512,576]{1,0:T(8,128)(2,1)S(1)} %bitcast.17, bf16[576,512]{1,0:T(8,128)(2,1)S(1)} %copy_bitcast_fusion.qt_ref, ...), custom_call_target="tpu_custom_call" | custom-call | flops 570425344 | bytes 1048576 | tf_op jit(solution)/shard_map/attention/pallas_call | solution.py:226
  19.4 2.3 %collective-permute-start.3 = (bf16[2,576,128]{2,1,0:T(8,128)(2,1)S(1)}, bf16[2,576,128]{2,1,0:T(8,128)(2,1)S(1)}, u32[]{:S(2)}, u32[]{:S(2)}) collective-permute-start(bf16[2,576,128]{2,1,0:T(8,128)(2,1)S(1)} %get-tuple-element.25), channel_id=1, source_target_pairs={{0,32},{32,0},{1,33},{33,1},{2,34},{34,2},{3,35},{35,3},{4,36},{36... | collective-permute-start | bytes 884744 | tf_op jit(solution)/shard_map/ppermute | solution.py:229
  21.7 0.9 %keep.1.keep_ref = f32[2,576,128]{2,1,0:T(8,128)S(1)} custom-call(s32[1]{0:T(128)} %bitcast.place, bf16[576,512]{1,0:T(8,128)(2,1)S(1)} %copy_bitcast_fusion.qt_ref, bf16[576,512]{1,0:T(8,128)(2,1)S(1)} %get-tuple-element.20.gt_ref, bf16[512,512]{1,0:T(8,128)(2,1)S(1)} %get-tuple-element.24.p_ref, bf16[512,512]{1,0:T(8,128)(2,1)S(1)} %get-tuple-element.30.ds_ref), custom_call_target="tpu_custom_call" | custom-call | flops 285212672 | bytes 1048576 | tf_op jit(solution)/shard_map/keep/pallas_call | solution.py:230
  22.5 0.4 collective-permute-done.3.came_ref
  22.9 0.1 join.1
  22.9 3.5 %collective-permute-start.4 = (bf16[576,128]{1,0:T(8,128)(2,1)S(1)}, bf16[576,128]{1,0:T(8,128)(2,1)S(1)}, u32[]{:S(2)}, u32[]{:S(2)}) collective-permute-start(bf16[576,128]{1,0:T(8,128)(2,1)S(1)} %get-tuple-element.28), channel_id=1, source_target_pairs={{64,16},{65,17},{66,18},{67,19},{68,20},{69,21},{70,22},{71,23},{7... | collective-permute-start | bytes 442376 | tf_op jit(solution)/shard_map/ppermute | solution.py:236
  26.4 0.7 collective-permute-start.5
  27.1 1.6 %query_grads.1 = bf16[4,576,128]{2,1,0:T(8,128)(2,1)} custom-call(bf16[512,512]{1,0:T(8,128)(2,1)S(1)} %get-tuple-element.30.ds_ref, bf16[576,128]{1,0:T(8,128)(2,1)S(1)} %bitcast.23, bf16[576,128]{1,0:T(8,128)(2,1)S(1)} %collective-permute-done.px_ref, bf16[576,128]{1,0:T(8,128)(2,1)S(1)} %collective-permute-done.1.p2_ref, ...), custom_call_target="tpu_custom_call" | custom-call | flops 301989888 | bytes 2097152 | tf_op jit(solution)/shard_map/query_grads/pallas_call | solution.py:112
  28.7 5.5 %collective-permute-done.4.next_ref = bf16[576,128]{1,0:T(8,128)(2,1)S(1)} collective-permute-done((bf16[576,128]{1,0:T(8,128)(2,1)S(1)}, bf16[576,128]{1,0:T(8,128)(2,1)S(1)}, u32[]{:S(2)}, u32[]{:S(2)}) %collective-permute-start.4) | collective-permute-done | bytes 147488 | tf_op jit(solution)/shard_map/ppermute | solution.py:236
  34.1 0.0 collective-permute-done.5.over_ref
  34.1 0.1 total.1
  34.2 0.1 reshape.30
  34.3 22.4 %all_to_all.10.came_ref = bf16[32,2,1152]{2,1,0:T(2,128)(2,1)S(1)} all-to-all(bf16[32,2,1152]{2,1,0:T(2,128)(2,1)S(1)} %reshape.30), channel_id=1, replica_groups=mesh['z'=8,'xh'=2,'core'=2,'xl'=4,'y'=8] {'xl','y'}, dimensions={0} | all-to-all | bytes 294912 | tf_op jit(solution)/shard_map/all_to_all | solution.py:244
  56.8 0.1 reduce.1
  56.8 13.9 %all_to_all.11 = bf16[32,2,1152]{2,1,0:T(2,128)(2,1)S(1)} all-to-all(bf16[32,2,1152]{2,1,0:T(2,128)(2,1)S(1)} %reduce.1), channel_id=1, replica_groups=mesh['z'=8,'xh'=2,'core'=2,'xl'=4,'y'=8] {'xl','y'}, dimensions={0} | all-to-all | bytes 294912 | tf_op jit(solution)/shard_map/all_to_all | solution.py:246
  70.7 0.1 reshape.31.came_ref
  70.8 0.7 %finish.1 = f32[576,128]{1,0:T(8,128)} custom-call(s32[1]{0:T(128)} %bitcast.place, bf16[64,1152]{1,0:T(8,128)(2,1)S(1)} %reshape.31.came_ref), custom_call_target="tpu_custom_call" | custom-call | flops 524288 | bytes 1048576 | tf_op jit(solution)/shard_map/finish/pallas_call | solution.py:248
  (1 shorter events, 0.0 us)
Async XLA Ops:
  0.6 9.1 %copy-start.1 = (bf16[128,4,576]{0,2,1:T(8,128)(2,1)S(1)}, bf16[128,4,576]{0,2,1:T(8,128)(2,1)}, u32[]{:S(2)}) copy-start(bf16[128,4,576]{0,2,1:T(8,128)(2,1)} %param.4) | copy-start | bytes 1769476
  0.6 12.6 %collective-permute-start.1 = (bf16[576,128]{1,0:T(8,128)(2,1)}, bf16[576,128]{1,0:T(8,128)(2,1)S(1)}, u32[]{:S(2)}, u32[]{:S(2)}) collective-permute-start(bf16[576,128]{1,0:T(8,128)(2,1)} %bitcast.20), channel_id=1, source_target_pairs={{0,80},{1,81},{2,82},{3,83},{4,84},{5,85},{6,86},{7,87},{8,88},{9,... | collective-permute-start | bytes 442376 | tf_op jit(solution)/shard_map/ppermute | solution.py:206
  6.7 10.0 %collective-permute-start = (bf16[576,128]{1,0:T(8,128)(2,1)}, bf16[576,128]{1,0:T(8,128)(2,1)S(1)}, u32[]{:S(2)}, u32[]{:S(2)}) collective-permute-start(bf16[576,128]{1,0:T(8,128)(2,1)} %bitcast.21), channel_id=1, source_target_pairs={{0,32},{1,33},{2,34},{3,35},{4,36},{5,37},{6,38},{7,39},{8,40},{9,... | collective-permute-start | bytes 442376 | tf_op jit(solution)/shard_map/ppermute | solution.py:207
  10.1 6.6 %copy-start.2 = (s32[128]{0:T(128)S(1)}, s32[128]{0:T(128)}, u32[]{:S(2)}) copy-start(s32[128]{0:T(128)} %param.7) | copy-start | bytes 1540
  13.2 4.5 %collective-permute-start.2 = (bf16[576,128]{1,0:T(8,128)(2,1)S(1)}, bf16[576,128]{1,0:T(8,128)(2,1)S(1)}, u32[]{:S(2)}, u32[]{:S(2)}) collective-permute-start(bf16[576,128]{1,0:T(8,128)(2,1)S(1)} %collective-permute-done.1.p2_ref), channel_id=1, source_target_pairs={{0,32},{32,0},{1,33},{33,1},{2,34},{34,2},{3,35},{35,3},{4,36},{36... | collective-permute-start | bytes 442376 | tf_op jit(solution)/shard_map/ppermute | solution.py:208
  16.7 1.0 %copy-start = (bf16[128,576]{0,1:T(8,128)(2,1)S(1)}, bf16[128,576]{0,1:T(8,128)(2,1)}, u32[]{:S(2)}) copy-start(bf16[128,576]{0,1:T(8,128)(2,1)} %param.5) | copy-start | bytes 442372
  19.4 3.5 %collective-permute-start.3 = (bf16[2,576,128]{2,1,0:T(8,128)(2,1)S(1)}, bf16[2,576,128]{2,1,0:T(8,128)(2,1)S(1)}, u32[]{:S(2)}, u32[]{:S(2)}) collective-permute-start(bf16[2,576,128]{2,1,0:T(8,128)(2,1)S(1)} %get-tuple-element.25), channel_id=1, source_target_pairs={{0,32},{32,0},{1,33},{33,1},{2,34},{34,2},{3,35},{35,3},{4,36},{36... | collective-permute-start | bytes 884744 | tf_op jit(solution)/shard_map/ppermute | solution.py:229
  22.9 11.2 %collective-permute-start.4 = (bf16[576,128]{1,0:T(8,128)(2,1)S(1)}, bf16[576,128]{1,0:T(8,128)(2,1)S(1)}, u32[]{:S(2)}, u32[]{:S(2)}) collective-permute-start(bf16[576,128]{1,0:T(8,128)(2,1)S(1)} %get-tuple-element.28), channel_id=1, source_target_pairs={{64,16},{65,17},{66,18},{67,19},{68,20},{69,21},{70,22},{71,23},{7... | collective-permute-start | bytes 442376 | tf_op jit(solution)/shard_map/ppermute | solution.py:236
  26.4 7.7 %collective-permute-start.5 = (bf16[576,128]{1,0:T(8,128)(2,1)S(1)}, bf16[576,128]{1,0:T(8,128)(2,1)S(1)}, u32[]{:S(2)}, u32[]{:S(2)}) collective-permute-start(bf16[576,128]{1,0:T(8,128)(2,1)S(1)} %get-tuple-element.29), channel_id=1, source_target_pairs={{160,32},{161,33},{162,34},{163,35},{164,36},{165,37},{166,38},{16... | collective-permute-start | bytes 442376 | tf_op jit(solution)/shard_map/ppermute | solution.py:237
